TPU v7x, 256 devices: a whole 4x4x8 slice. The times are simulated.
256 devices in a mesh: space: 128 (over x, y, z), slab: 2 (over core).
Axes of the slice: x: 4, y: 4, z: 8, core: 2. Of those that a mesh axis runs over, the one named last changes fastest.
Arguments:
- phases: float32 [8, 1536, 24, 384], P(None, 'space', 'slab'), may hold values from 0 to 1
- mobility: float32 [8], replicated, may hold values from 0.02 to 0.08
- active: int32 [128, 2, 32, 8], P('space', 'slab'), may hold values from 0 to 1, as said below
- variants: float32 [8, 3], replicated, may hold values from -4 to 4
Outputs:
- evolved: float32 [8, 1536, 24, 384], P(None, 'space', 'slab')
- displacement: float32 [3, 384, 24, 1536], P(None, 'space', 'slab')
Inputs may be any that keep to these rules, and one draw needn't show every extreme that they name: 1 marks an order parameter that evolves in that brick; the share of active ones differs strongly between brick indices along the first dimension.
All inputs are finite; a program needn't handle non-finite values.
Results may differ from a plain program's by a relative error of at most 0.00016.
Values sent between devices are 32-bit elements; how exact they have to be, the bound alone decides.
No kernel may reach another device: no remote copies, remote signals or barrier semaphores. Data moves between devices by JAX's collectives and lax.ppermute only.
A program may use at most 128 MiB of HBM per device.

v0:
```python
import jax
import jax.numpy as jnp
from jax import lax
from jax.sharding import PartitionSpec as P

STEPS = 3
ITERS = 4


PAIR_ENERGY = 1.5
DIAGONAL_SHIFT = 3.0
SPECTRUM_CENTRE = 12.0
SPECTRUM_RADIUS = 9.0


def extended(array, sides, width):
    edges = {}
    for axis, dim in sides:
        count, length = (lax.axis_size(axis), array.shape[dim])
        up = [(i, (i + 1) % count) for i in range(count - 1)]
        last = lax.slice_in_dim(array, length - width, length, axis=dim)
        leading = lax.slice_in_dim(array, 0, width, axis=dim)
        edges[dim] = (
            lax.ppermute(last, axis, up),
            lax.ppermute(leading, axis, [(b, a) for a, b in up]),
        )
    done = []
    for _, dim in sides:
        low, high = edges[dim]
        around = [(width, width) if d in done else (0, 0) for d in range(array.ndim)]
        array = jnp.concatenate([jnp.pad(low, around), array, jnp.pad(high, around)], axis=dim)
        done.append(dim)
    return array


def relax(fields, padded, speeds):
    summed = (
        padded[:, 2:, 1:-1, 1:-1]
        + padded[:, :-2, 1:-1, 1:-1]
        + padded[:, 1:-1, 2:, 1:-1]
        + padded[:, 1:-1, :-2, 1:-1]
        + padded[:, 1:-1, 1:-1, 2:]
        + padded[:, 1:-1, 1:-1, :-2]
    )
    laplace = summed - 6.0 * fields
    squares = jnp.sum(fields * fields, axis=0)
    driving = (
        fields * fields * fields
        - fields
        + 2.0 * PAIR_ENERGY * fields * (squares - fields * fields)
        - laplace
    )
    return fields - speeds * driving


def coefficients(fields, variants):
    squared = fields * fields
    summed = jnp.sum(squared, axis=0)
    saturation = summed / (1.0 + summed)
    excess = 0.5 * saturation
    lame_first = 1.5 + saturation
    strain = jnp.einsum("pabc,pk->kabc", squared, variants, precision=lax.Precision.HIGHEST)
    dilation = strain[0] + strain[1] + strain[2]
    stress = lame_first * dilation + 2.0 * (1.0 + excess) * strain
    return jnp.concatenate([excess[None], stress], axis=0)


def shifted(padded, along, offset):
    slicer = [slice(None)] * padded.ndim
    for dimension in range(padded.ndim - 3, padded.ndim):
        lowest = 1 + (offset if dimension == padded.ndim + along else 0)
        slicer[dimension] = slice(lowest, padded.shape[dimension] - 2 + lowest)
    return padded[tuple(slicer)]


def stiffness(padded, excess_pad):
    centre = shifted(padded, -1, 0)
    excess = shifted(excess_pad, -1, 0)
    summed = DIAGONAL_SHIFT * centre
    for along in (-3, -2, -1):
        for offset in (-1, 1):
            weight = 1.0 + 0.5 * (excess + shifted(excess_pad, along, offset))
            summed = summed + weight * (centre - shifted(padded, along, offset))
    return summed


def chebyshev(forcing, operate):
    ratio_now = SPECTRUM_RADIUS / SPECTRUM_CENTRE
    residual = forcing
    direction = forcing / SPECTRUM_CENTRE
    solution = jnp.zeros_like(forcing)
    for counter in range(ITERS):
        solution = solution + direction
        residual = residual - operate(direction)
        ratio_next = 1.0 / (2.0 * SPECTRUM_CENTRE / SPECTRUM_RADIUS - ratio_now)
        direction = (
            ratio_next * ratio_now * direction + 2.0 * ratio_next / SPECTRUM_RADIUS * residual
        )
        ratio_now = ratio_next
    return solution + direction


def pad_last(padded):
    return jnp.pad(padded, ((0, 0), (0, 0), (0, 0), (1, 1)))


def derive_forcing(padded, directions):
    return jnp.stack(
        [
            0.5
            * (shifted(padded[1 + component], along, 1) - shifted(padded[1 + component], along, -1))
            for component, along in enumerate(directions)
        ]
    )


def shards(phases, mobility, active, variants):
    brick_size = phases.shape[1]
    flags = jnp.transpose(active[0].astype(jnp.float32), (2, 0, 1))
    flags = jnp.repeat(jnp.repeat(flags, brick_size, axis=1), brick_size, axis=2)
    speeds = mobility[:, None, None, None] * flags[:, None]
    fields = phases
    for counter in range(STEPS):
        padded = extended(fields, (("space", 1), ("slab", 2)), 1)
        fields = relax(fields, pad_last(padded), speeds)
    local = coefficients(fields, variants)
    padded = pad_last(extended(local, (("space", 1), ("slab", 2)), 1))
    excess_pad = padded[0]
    forcing = derive_forcing(padded, (-3, -2, -1))

    def operate_local(direction):
        widened = extended(direction, (("space", 1), ("slab", 2)), 1)
        return stiffness(pad_last(widened), excess_pad)

    solved = chebyshev(forcing, operate_local)
    arrived = lax.all_to_all(solved, "space", split_axis=3, concat_axis=1, tiled=True)
    return (fields, jnp.transpose(arrived, (0, 3, 2, 1)))


def solution(mesh):
    placed = (P(None, "space", "slab", None), P(), P("space", "slab", None, None), P())
    return jax.shard_map(
        shards,
        mesh=mesh,
        in_specs=placed,
        out_specs=(P(None, "space", "slab", None), P(None, "space", "slab", None)),
        check_vma=False,
    )
```

profile of v0, /device:TPU:1, one launch (start us, length us, event | category | flops | bytes accessed | tf_op | source)
XLA Modules:
  0.0 306.7 jit_solution(15071352822868537258)
XLA Ops:
  3.1 5.1 %collective-permute-start.2 = (f32[8,12,1,384]{3,0,2,1:T(8,128)S(1)}, f32[8,12,1,384]{3,0,2,1:T(8,128)S(1)}, u32[]{:S(2)}, u32[]{:S(2)}) collective-permute-start(f32[8,12,1,384]{3,0,2,1:T(8,128)S(1)} %get-tuple-element.19), channel_id=1, source_target_pairs={{1,0},{3,2},{5,4},{7,6},{9,8},{11,10},{13,12},{15,14},{17,16},{19,... | collective-permute-start | bytes 442376 | tf_op jit(solution)/shard_map/ppermute | solution.py:25
  10.5 4.0 %collective-permute-start.1 = (f32[8,1,12,384]{3,0,2,1:T(8,128)S(1)}, f32[8,1,12,384]{3,0,2,1:T(8,128)S(1)}, u32[]{:S(2)}, u32[]{:S(2)}) collective-permute-start(f32[8,1,12,384]{3,0,2,1:T(8,128)S(1)} %get-tuple-element.21), channel_id=1, source_target_pairs={{0,2},{2,4},{4,6},{6,8},{8,10},{10,12},{12,14},{14,16},{16,18},{18... | collective-permute-start | bytes 442376 | tf_op jit(solution)/shard_map/ppermute | solution.py:24
  19.2 14.4 %fusion.11 = f32[8,12,12,384]{3,0,2,1:T(8,128)S(1)} fusion(f32[8,12,12,384]{3,0,2,1:T(8,128)S(1)} %copy-done.2, f32[8,14,14,386]{3,0,2,1:T(8,128)S(1)} %select_maximum_fusion.8, f32[8,14,12,384]{3,0,2,1:T(8,128)S(1)} %constant_dynamic-update-slice_fusion, f32[8,14,1,384]{3,0,2,1:T(8,128)S(1)} %pad.79, f32[8,14,1,384]{3,0,2,1:T(8,128)S(1)} %pad.78, ...), kind=kOutput, calls=%fused_computation.35 | output fusion | flops 9787399 | bytes 11698176 | tf_op jit(solution)/shard_map/sub | solution.py:50
  34.9 3.0 collective-permute-start.6
  38.0 4.1 %collective-permute-start.5 = (f32[8,1,12,384]{3,0,2,1:T(8,128)S(1)}, f32[8,1,12,384]{3,0,2,1:T(8,128)S(1)}, u32[]{:S(2)}, u32[]{:S(2)}) collective-permute-start(f32[8,1,12,384]{3,0,2,1:T(8,128)S(1)} %get-tuple-element.14), channel_id=1, source_target_pairs={{0,2},{2,4},{4,6},{6,8},{8,10},{10,12},{12,14},{14,16},{16,18},{18... | collective-permute-start | bytes 442376 | tf_op jit(solution)/shard_map/ppermute | solution.py:24
  45.6 4.1 %collective-permute-done.4 = f32[8,1,12,384]{3,0,2,1:T(8,128)S(1)} collective-permute-done((f32[8,1,12,384]{3,0,2,1:T(8,128)S(1)}, f32[8,1,12,384]{3,0,2,1:T(8,128)S(1)}, u32[]{:S(2)}, u32[]{:S(2)}) %collective-permute-start.4) | collective-permute-done | bytes 147488 | tf_op jit(solution)/shard_map/ppermute | solution.py:25
  50.6 15.6 %fusion.16 = f32[8,12,12,384]{3,0,2,1:T(8,128)S(1)} fusion(f32[8,12,12,384]{3,0,2,1:T(8,128)S(1)} %fusion.11, f32[8,14,14,386]{3,0,2,1:T(8,128)S(1)} %select_maximum_fusion.4, f32[8,14,1,384]{3,0,2,1:T(8,128)S(1)} %pad.82, f32[8,1,12,384]{3,0,2,1:T(8,128)S(1)} %collective-permute-done.4, f32[8,1,12,384]{3,0,2,1:T(8,128)S(1)} %collective-permute-done.5, ...), kind=kOutput, calls=%fused_computation.40 | output fusion | flops 11556871 | bytes 9633792 | tf_op jit(solution)/shard_map/sub | solution.py:50
  67.6 3.0 collective-permute-start.10
  70.7 3.2 %collective-permute-start.9 = (f32[8,1,12,384]{3,0,2,1:T(8,128)S(1)}, f32[8,1,12,384]{3,0,2,1:T(8,128)S(1)}, u32[]{:S(2)}, u32[]{:S(2)}) collective-permute-start(f32[8,1,12,384]{3,0,2,1:T(8,128)S(1)} %get-tuple-element.10), channel_id=1, source_target_pairs={{0,2},{2,4},{4,6},{6,8},{8,10},{10,12},{12,14},{14,16},{16,18},{18... | collective-permute-start | bytes 442376 | tf_op jit(solution)/shard_map/ppermute | solution.py:24
  77.4 5.7 %collective-permute-done.8 = f32[8,1,12,384]{3,0,2,1:T(8,128)S(1)} collective-permute-done((f32[8,1,12,384]{3,0,2,1:T(8,128)S(1)}, f32[8,1,12,384]{3,0,2,1:T(8,128)S(1)}, u32[]{:S(2)}, u32[]{:S(2)}) %collective-permute-start.8) | collective-permute-done | bytes 147488 | tf_op jit(solution)/shard_map/ppermute | solution.py:25
  84.0 16.9 %multiply_reduce_fusion.3 = (f32[12,12,384]{2,1,0:T(8,128)S(1)}, f32[8,12,12,384]{3,0,2,1:T(8,128)S(1)}) fusion(f32[8,12,12,384]{3,0,2,1:T(8,128)S(1)} %fusion.16, f32[8,14,14,386]{3,0,2,1:T(8,128)S(1)} %select_maximum_fusion, f32[8,1,12,384]{3,0,2,1:T(8,128)S(1)} %collective-permute-done.8, f32[8,1,12,384]{3,0,2,1:T(8,128)S(1)} %collective-permute-done.9, ...), kind=kOutput, calls=%fused_computation.86 | output fusion | flops 12386311 | bytes 9854976 | tf_op jit(solution)/shard_map/sub | solution.py:50
  105.3 3.0 collective-permute-start.15
  108.4 4.8 %collective-permute-start.13 = (f32[4,1,12,384]{3,0,2,1:T(4,128)S(1)}, f32[4,1,12,384]{3,0,2,1:T(4,128)S(1)}, u32[]{:S(2)}, u32[]{:S(2)}) collective-permute-start(f32[4,1,12,384]{3,0,2,1:T(4,128)S(1)} %get-tuple-element.26), channel_id=1, source_target_pairs={{0,2},{2,4},{4,6},{6,8},{8,10},{10,12},{12,14},{14,16},{16,18},{18... | collective-permute-start | bytes 221192 | tf_op jit(solution)/shard_map/ppermute | solution.py:24
  115.1 4.2 %collective-permute-done.14 = f32[4,1,12,384]{3,0,2,1:T(4,128)S(1)} collective-permute-done((f32[4,1,12,384]{3,0,2,1:T(4,128)S(1)}, f32[4,1,12,384]{3,0,2,1:T(4,128)S(1)}, u32[]{:S(2)}, u32[]{:S(2)}) %collective-permute-start.14) | collective-permute-done | bytes 73760 | tf_op jit(solution)/shard_map/ppermute | solution.py:25
  119.8 3.5 %pad_slice_fusion.2 = (f32[1,14,14,386]{3,0,2,1:T(1,128)S(1)}, f32[1,14,14,386]{3,0,2,1:T(1,128)S(1)}, f32[1,14,14,386]{3,0,2,1:T(1,128)S(1)}, f32[1,14,14,386]{3,0,2,1:T(1,128)S(1)}) fusion(f32[4,14,14,384]{3,0,2,1:T(4,128)S(1)} %select_maximum_fusion.26), kind=kLoop, calls=%fused_computation.89 | loop fusion | bytes 2414720 | tf_op jit(solution)/shard_map/slice | solution.py:128
  128.7 3.4 %collective-permute-start.16 = (f32[3,1,12,384]{3,2,1,0:T(8,128)S(1)}, f32[3,1,12,384]{3,2,1,0:T(8,128)S(1)}, u32[]{:S(2)}, u32[]{:S(2)}) collective-permute-start(f32[3,1,12,384]{3,2,1,0:T(8,128)S(1)} %get-tuple-element.42), channel_id=1, source_target_pairs={{0,2},{2,4},{4,6},{6,8},{8,10},{10,12},{12,14},{14,16},{16,18},{18... | collective-permute-start | bytes 165896 | tf_op jit(solution)/shard_map/ppermute | solution.py:24
  134.3 3.9 %collective-permute-done.17 = f32[3,1,12,384]{3,2,1,0:T(8,128)S(1)} collective-permute-done((f32[3,1,12,384]{3,2,1,0:T(8,128)S(1)}, f32[3,1,12,384]{3,2,1,0:T(8,128)S(1)}, u32[]{:S(2)}, u32[]{:S(2)}) %collective-permute-start.17) | collective-permute-done | bytes 55328 | tf_op jit(solution)/shard_map/ppermute | solution.py:25
  142.6 3.0 collective-permute-start.23
  145.6 4.6 %collective-permute-start.20 = (f32[3,1,12,384]{3,2,1,0:T(8,128)S(1)}, f32[3,1,12,384]{3,2,1,0:T(8,128)S(1)}, u32[]{:S(2)}, u32[]{:S(2)}) collective-permute-start(f32[3,1,12,384]{3,2,1,0:T(8,128)S(1)} %get-tuple-element.38), channel_id=1, source_target_pairs={{0,2},{2,4},{4,6},{6,8},{8,10},{10,12},{12,14},{14,16},{16,18},{18... | collective-permute-start | bytes 165896 | tf_op jit(solution)/shard_map/ppermute | solution.py:24
  152.2 4.2 %collective-permute-done.21 = f32[3,1,12,384]{3,2,1,0:T(8,128)S(1)} collective-permute-done((f32[3,1,12,384]{3,2,1,0:T(8,128)S(1)}, f32[3,1,12,384]{3,2,1,0:T(8,128)S(1)}, u32[]{:S(2)}, u32[]{:S(2)}) %collective-permute-start.21) | collective-permute-done | bytes 55328 | tf_op jit(solution)/shard_map/ppermute | solution.py:25
  159.9 3.0 collective-permute-start.27
  162.9 4.8 %collective-permute-start.24 = (f32[3,1,12,384]{3,2,1,0:T(8,128)S(1)}, f32[3,1,12,384]{3,2,1,0:T(8,128)S(1)}, u32[]{:S(2)}, u32[]{:S(2)}) collective-permute-start(f32[3,1,12,384]{3,2,1,0:T(8,128)S(1)} %get-tuple-element.34), channel_id=1, source_target_pairs={{0,2},{2,4},{4,6},{6,8},{8,10},{10,12},{12,14},{14,16},{16,18},{18... | collective-permute-start | bytes 165896 | tf_op jit(solution)/shard_map/ppermute | solution.py:24
  169.7 4.3 %collective-permute-done.25 = f32[3,1,12,384]{3,2,1,0:T(8,128)S(1)} collective-permute-done((f32[3,1,12,384]{3,2,1,0:T(8,128)S(1)}, f32[3,1,12,384]{3,2,1,0:T(8,128)S(1)}, u32[]{:S(2)}, u32[]{:S(2)}) %collective-permute-start.25) | collective-permute-done | bytes 55328 | tf_op jit(solution)/shard_map/ppermute | solution.py:25
  180.5 3.7 %collective-permute-start.28 = (f32[3,1,12,384]{3,2,1,0:T(8,128)S(1)}, f32[3,1,12,384]{3,2,1,0:T(8,128)S(1)}, u32[]{:S(2)}, u32[]{:S(2)}) collective-permute-start(f32[3,1,12,384]{3,2,1,0:T(8,128)S(1)} %get-tuple-element.30), channel_id=1, source_target_pairs={{0,2},{2,4},{4,6},{6,8},{8,10},{10,12},{12,14},{14,16},{16,18},{18... | collective-permute-start | bytes 165896 | tf_op jit(solution)/shard_map/ppermute | solution.py:24
  186.1 4.3 %collective-permute-done.29 = f32[3,1,12,384]{3,2,1,0:T(8,128)S(1)} collective-permute-done((f32[3,1,12,384]{3,2,1,0:T(8,128)S(1)}, f32[3,1,12,384]{3,2,1,0:T(8,128)S(1)}, u32[]{:S(2)}, u32[]{:S(2)}) %collective-permute-start.29) | collective-permute-done | bytes 55328 | tf_op jit(solution)/shard_map/ppermute | solution.py:25
  193.5 5.8 %copy.30 = f32[3,12,12,384]{2,1,0,3:T(8,128)} copy(f32[3,12,12,384]{3,2,1,0:T(8,128)S(1)} %fusion.45) | data formatting | bytes 1327104 | tf_op jit(solution)/shard_map/add | solution.py:100
  199.3 7.2 %reshape.61 = f32[128,1,1296]{2,1,0:T(1,128)S(1)} reshape(f32[384,3,12,12]{3,2,1,0:T(8,128)} %bitcast.48) | data formatting | bytes 1327104
  206.5 57.6 %all_to_all.18 = f32[128,1,1296]{2,1,0:T(1,128)S(1)} all-to-all(f32[128,1,1296]{2,1,0:T(1,128)S(1)} %reshape.61), channel_id=1, replica_groups=mesh['space'=128,'slab'=2] {'space'}, dimensions={0} | all-to-all | bytes 1327104 | tf_op jit(solution)/shard_map/all_to_all | solution.py:136
  267.1 5.8 %reshape.62 = f32[384,3,12,12]{3,2,1,0:T(8,128)} reshape(f32[128,1296]{1,0:T(8,128)S(1)} %reduce) | data formatting | bytes 1327104
  272.9 10.9 %copy.56 = f32[3,12,12,128,3]{2,4,3,1,0:T(4,128)} copy(f32[3,12,12,128,3]{2,1,0,4,3:T(8,128)} %bitcast.49) | data formatting | bytes 1327104 | tf_op jit(solution)/shard_map/all_to_all | solution.py:136
  283.8 14.5 %copy.32 = f32[3,128,12,12,3]{2,1,3,4,0:T(8,128)} copy(f32[3,128,12,12,3]{3,4,1,2,0:T(4,128)} %bitcast.50) | data formatting | bytes 1327104 | tf_op jit(solution)/shard_map/all_to_all | solution.py:136
  298.3 8.4 %all_to_all.16 = f32[3,1536,12,3]{1,2,3,0:T(8,128)} reshape(f32[3,128,12,12,3]{2,1,3,4,0:T(8,128)} %copy.32) | data formatting | bytes 1327104 | tf_op jit(solution)/shard_map/all_to_all | solution.py:136
  (116 shorter events, 60.9 us)
Async XLA Ops:
  1.8 14.4 %collective-permute-start.3 = (f32[8,12,1,384]{3,0,2,1:T(8,128)S(1)}, f32[8,12,1,384]{3,0,2,1:T(8,128)S(1)}, u32[]{:S(2)}, u32[]{:S(2)}) collective-permute-start(f32[8,12,1,384]{3,0,2,1:T(8,128)S(1)} %get-tuple-element.18), channel_id=1, source_target_pairs={{0,1},{2,3},{4,5},{6,7},{8,9},{10,11},{12,13},{14,15},{16,17},{18,... | collective-permute-start | bytes 442376 | tf_op jit(solution)/shard_map/ppermute | solution.py:24
  3.1 13.1 %collective-permute-start.2 = (f32[8,12,1,384]{3,0,2,1:T(8,128)S(1)}, f32[8,12,1,384]{3,0,2,1:T(8,128)S(1)}, u32[]{:S(2)}, u32[]{:S(2)}) collective-permute-start(f32[8,12,1,384]{3,0,2,1:T(8,128)S(1)} %get-tuple-element.19), channel_id=1, source_target_pairs={{1,0},{3,2},{5,4},{7,6},{9,8},{11,10},{13,12},{15,14},{17,16},{19,... | collective-permute-start | bytes 442376 | tf_op jit(solution)/shard_map/ppermute | solution.py:25
  9.2 9.0 %collective-permute-start = (f32[8,1,12,384]{3,0,2,1:T(8,128)S(1)}, f32[8,1,12,384]{3,0,2,1:T(8,128)S(1)}, u32[]{:S(2)}, u32[]{:S(2)}) collective-permute-start(f32[8,1,12,384]{3,0,2,1:T(8,128)S(1)} %get-tuple-element.20), channel_id=1, source_target_pairs={{2,0},{4,2},{6,4},{8,6},{10,8},{12,10},{14,12},{16,14},{18,16},{20... | collective-permute-start | bytes 442376 | tf_op jit(solution)/shard_map/ppermute | solution.py:25
  10.5 7.5 %collective-permute-start.1 = (f32[8,1,12,384]{3,0,2,1:T(8,128)S(1)}, f32[8,1,12,384]{3,0,2,1:T(8,128)S(1)}, u32[]{:S(2)}, u32[]{:S(2)}) collective-permute-start(f32[8,1,12,384]{3,0,2,1:T(8,128)S(1)} %get-tuple-element.21), channel_id=1, source_target_pairs={{0,2},{2,4},{4,6},{6,8},{8,10},{10,12},{12,14},{14,16},{16,18},{18... | collective-permute-start | bytes 442376 | tf_op jit(solution)/shard_map/ppermute | solution.py:24
  33.6 9.8 %collective-permute-start.7 = (f32[8,12,1,384]{3,0,2,1:T(8,128)S(1)}, f32[8,12,1,384]{3,0,2,1:T(8,128)S(1)}, u32[]{:S(2)}, u32[]{:S(2)}) collective-permute-start(f32[8,12,1,384]{3,0,2,1:T(8,128)S(1)} %get-tuple-element.16), channel_id=1, source_target_pairs={{0,1},{2,3},{4,5},{6,7},{8,9},{10,11},{12,13},{14,15},{16,17},{18,... | collective-permute-start | bytes 442376 | tf_op jit(solution)/shard_map/ppermute | solution.py:24
  34.9 8.5 %collective-permute-start.6 = (f32[8,12,1,384]{3,0,2,1:T(8,128)S(1)}, f32[8,12,1,384]{3,0,2,1:T(8,128)S(1)}, u32[]{:S(2)}, u32[]{:S(2)}) collective-permute-start(f32[8,12,1,384]{3,0,2,1:T(8,128)S(1)} %get-tuple-element.17), channel_id=1, source_target_pairs={{1,0},{3,2},{5,4},{7,6},{9,8},{11,10},{13,12},{15,14},{17,16},{19,... | collective-permute-start | bytes 442376 | tf_op jit(solution)/shard_map/ppermute | solution.py:25
  38.0 7.6 %collective-permute-start.5 = (f32[8,1,12,384]{3,0,2,1:T(8,128)S(1)}, f32[8,1,12,384]{3,0,2,1:T(8,128)S(1)}, u32[]{:S(2)}, u32[]{:S(2)}) collective-permute-start(f32[8,1,12,384]{3,0,2,1:T(8,128)S(1)} %get-tuple-element.14), channel_id=1, source_target_pairs={{0,2},{2,4},{4,6},{6,8},{8,10},{10,12},{12,14},{14,16},{16,18},{18... | collective-permute-start | bytes 442376 | tf_op jit(solution)/shard_map/ppermute | solution.py:24
  42.1 7.6 %collective-permute-start.4 = (f32[8,1,12,384]{3,0,2,1:T(8,128)S(1)}, f32[8,1,12,384]{3,0,2,1:T(8,128)S(1)}, u32[]{:S(2)}, u32[]{:S(2)}) collective-permute-start(f32[8,1,12,384]{3,0,2,1:T(8,128)S(1)} %get-tuple-element.15), channel_id=1, source_target_pairs={{2,0},{4,2},{6,4},{8,6},{10,8},{12,10},{14,12},{16,14},{18,16},{20... | collective-permute-start | bytes 442376 | tf_op jit(solution)/shard_map/ppermute | solution.py:25
  66.3 8.9 %collective-permute-start.11 = (f32[8,12,1,384]{3,0,2,1:T(8,128)S(1)}, f32[8,12,1,384]{3,0,2,1:T(8,128)S(1)}, u32[]{:S(2)}, u32[]{:S(2)}) collective-permute-start(f32[8,12,1,384]{3,0,2,1:T(8,128)S(1)} %get-tuple-element.12), channel_id=1, source_target_pairs={{0,1},{2,3},{4,5},{6,7},{8,9},{10,11},{12,13},{14,15},{16,17},{18,... | collective-permute-start | bytes 442376 | tf_op jit(solution)/shard_map/ppermute | solution.py:24
  67.6 7.6 %collective-permute-start.10 = (f32[8,12,1,384]{3,0,2,1:T(8,128)S(1)}, f32[8,12,1,384]{3,0,2,1:T(8,128)S(1)}, u32[]{:S(2)}, u32[]{:S(2)}) collective-permute-start(f32[8,12,1,384]{3,0,2,1:T(8,128)S(1)} %get-tuple-element.13), channel_id=1, source_target_pairs={{1,0},{3,2},{5,4},{7,6},{9,8},{11,10},{13,12},{15,14},{17,16},{19,... | collective-permute-start | bytes 442376 | tf_op jit(solution)/shard_map/ppermute | solution.py:25
  70.7 6.7 %collective-permute-start.9 = (f32[8,1,12,384]{3,0,2,1:T(8,128)S(1)}, f32[8,1,12,384]{3,0,2,1:T(8,128)S(1)}, u32[]{:S(2)}, u32[]{:S(2)}) collective-permute-start(f32[8,1,12,384]{3,0,2,1:T(8,128)S(1)} %get-tuple-element.10), channel_id=1, source_target_pairs={{0,2},{2,4},{4,6},{6,8},{8,10},{10,12},{12,14},{14,16},{16,18},{18... | collective-permute-start | bytes 442376 | tf_op jit(solution)/shard_map/ppermute | solution.py:24
  73.9 9.3 %collective-permute-start.8 = (f32[8,1,12,384]{3,0,2,1:T(8,128)S(1)}, f32[8,1,12,384]{3,0,2,1:T(8,128)S(1)}, u32[]{:S(2)}, u32[]{:S(2)}) collective-permute-start(f32[8,1,12,384]{3,0,2,1:T(8,128)S(1)} %get-tuple-element.11), channel_id=1, source_target_pairs={{2,0},{4,2},{6,4},{8,6},{10,8},{12,10},{14,12},{16,14},{18,16},{20... | collective-permute-start | bytes 442376 | tf_op jit(solution)/shard_map/ppermute | solution.py:25
  104.0 10.4 %collective-permute-start.12 = (f32[4,12,1,384]{3,0,2,1:T(4,128)S(1)}, f32[4,12,1,384]{3,0,2,1:T(4,128)S(1)}, u32[]{:S(2)}, u32[]{:S(2)}) collective-permute-start(f32[4,12,1,384]{3,0,2,1:T(4,128)S(1)} %get-tuple-element.28), channel_id=1, source_target_pairs={{0,1},{2,3},{4,5},{6,7},{8,9},{10,11},{12,13},{14,15},{16,17},{18,... | collective-permute-start | bytes 221192 | tf_op jit(solution)/shard_map/ppermute | solution.py:24
  105.3 9.1 %collective-permute-start.15 = (f32[4,12,1,384]{3,0,2,1:T(4,128)S(1)}, f32[4,12,1,384]{3,0,2,1:T(4,128)S(1)}, u32[]{:S(2)}, u32[]{:S(2)}) collective-permute-start(f32[4,12,1,384]{3,0,2,1:T(4,128)S(1)} %get-tuple-element.29), channel_id=1, source_target_pairs={{1,0},{3,2},{5,4},{7,6},{9,8},{11,10},{13,12},{15,14},{17,16},{19,... | collective-permute-start | bytes 221192 | tf_op jit(solution)/shard_map/ppermute | solution.py:25
  108.4 6.8 %collective-permute-start.13 = (f32[4,1,12,384]{3,0,2,1:T(4,128)S(1)}, f32[4,1,12,384]{3,0,2,1:T(4,128)S(1)}, u32[]{:S(2)}, u32[]{:S(2)}) collective-permute-start(f32[4,1,12,384]{3,0,2,1:T(4,128)S(1)} %get-tuple-element.26), channel_id=1, source_target_pairs={{0,2},{2,4},{4,6},{6,8},{8,10},{10,12},{12,14},{14,16},{16,18},{18... | collective-permute-start | bytes 221192 | tf_op jit(solution)/shard_map/ppermute | solution.py:24
  113.1 6.2 %collective-permute-start.14 = (f32[4,1,12,384]{3,0,2,1:T(4,128)S(1)}, f32[4,1,12,384]{3,0,2,1:T(4,128)S(1)}, u32[]{:S(2)}, u32[]{:S(2)}) collective-permute-start(f32[4,1,12,384]{3,0,2,1:T(4,128)S(1)} %get-tuple-element.27), channel_id=1, source_target_pairs={{2,0},{4,2},{6,4},{8,6},{10,8},{12,10},{14,12},{16,14},{18,16},{20... | collective-permute-start | bytes 221192 | tf_op jit(solution)/shard_map/ppermute | solution.py:25
  124.4 9.8 %collective-permute-start.18 = (f32[3,12,1,384]{3,2,1,0:T(1,128)S(1)}, f32[3,12,1,384]{3,2,1,0:T(1,128)S(1)}, u32[]{:S(2)}, u32[]{:S(2)}) collective-permute-start(f32[3,12,1,384]{3,2,1,0:T(1,128)S(1)} %get-tuple-element.44), channel_id=1, source_target_pairs={{0,1},{2,3},{4,5},{6,7},{8,9},{10,11},{12,13},{14,15},{16,17},{18,... | collective-permute-start | bytes 165896 | tf_op jit(solution)/shard_map/ppermute | solution.py:24
  125.7 8.5 %collective-permute-start.19 = (f32[3,12,1,384]{3,2,1,0:T(1,128)S(1)}, f32[3,12,1,384]{3,2,1,0:T(1,128)S(1)}, u32[]{:S(2)}, u32[]{:S(2)}) collective-permute-start(f32[3,12,1,384]{3,2,1,0:T(1,128)S(1)} %get-tuple-element.45), channel_id=1, source_target_pairs={{1,0},{3,2},{5,4},{7,6},{9,8},{11,10},{13,12},{15,14},{17,16},{19,... | collective-permute-start | bytes 165896 | tf_op jit(solution)/shard_map/ppermute | solution.py:25
  128.7 5.5 %collective-permute-start.16 = (f32[3,1,12,384]{3,2,1,0:T(8,128)S(1)}, f32[3,1,12,384]{3,2,1,0:T(8,128)S(1)}, u32[]{:S(2)}, u32[]{:S(2)}) collective-permute-start(f32[3,1,12,384]{3,2,1,0:T(8,128)S(1)} %get-tuple-element.42), channel_id=1, source_target_pairs={{0,2},{2,4},{4,6},{6,8},{8,10},{10,12},{12,14},{14,16},{16,18},{18... | collective-permute-start | bytes 165896 | tf_op jit(solution)/shard_map/ppermute | solution.py:24
  132.2 6.1 %collective-permute-start.17 = (f32[3,1,12,384]{3,2,1,0:T(8,128)S(1)}, f32[3,1,12,384]{3,2,1,0:T(8,128)S(1)}, u32[]{:S(2)}, u32[]{:S(2)}) collective-permute-start(f32[3,1,12,384]{3,2,1,0:T(8,128)S(1)} %get-tuple-element.43), channel_id=1, source_target_pairs={{2,0},{4,2},{6,4},{8,6},{10,8},{12,10},{14,12},{16,14},{18,16},{20... | collective-permute-start | bytes 165896 | tf_op jit(solution)/shard_map/ppermute | solution.py:25
  141.3 10.2 %collective-permute-start.22 = (f32[3,12,1,384]{3,2,1,0:T(1,128)S(1)}, f32[3,12,1,384]{3,2,1,0:T(1,128)S(1)}, u32[]{:S(2)}, u32[]{:S(2)}) collective-permute-start(f32[3,12,1,384]{3,2,1,0:T(1,128)S(1)} %get-tuple-element.40), channel_id=1, source_target_pairs={{0,1},{2,3},{4,5},{6,7},{8,9},{10,11},{12,13},{14,15},{16,17},{18,... | collective-permute-start | bytes 165896 | tf_op jit(solution)/shard_map/ppermute | solution.py:24
  142.6 9.0 %collective-permute-start.23 = (f32[3,12,1,384]{3,2,1,0:T(1,128)S(1)}, f32[3,12,1,384]{3,2,1,0:T(1,128)S(1)}, u32[]{:S(2)}, u32[]{:S(2)}) collective-permute-start(f32[3,12,1,384]{3,2,1,0:T(1,128)S(1)} %get-tuple-element.41), channel_id=1, source_target_pairs={{1,0},{3,2},{5,4},{7,6},{9,8},{11,10},{13,12},{15,14},{17,16},{19,... | collective-permute-start | bytes 165896 | tf_op jit(solution)/shard_map/ppermute | solution.py:25
  145.6 6.5 %collective-permute-start.20 = (f32[3,1,12,384]{3,2,1,0:T(8,128)S(1)}, f32[3,1,12,384]{3,2,1,0:T(8,128)S(1)}, u32[]{:S(2)}, u32[]{:S(2)}) collective-permute-start(f32[3,1,12,384]{3,2,1,0:T(8,128)S(1)} %get-tuple-element.38), channel_id=1, source_target_pairs={{0,2},{2,4},{4,6},{6,8},{8,10},{10,12},{12,14},{14,16},{16,18},{18... | collective-permute-start | bytes 165896 | tf_op jit(solution)/shard_map/ppermute | solution.py:24
  150.2 6.2 %collective-permute-start.21 = (f32[3,1,12,384]{3,2,1,0:T(8,128)S(1)}, f32[3,1,12,384]{3,2,1,0:T(8,128)S(1)}, u32[]{:S(2)}, u32[]{:S(2)}) collective-permute-start(f32[3,1,12,384]{3,2,1,0:T(8,128)S(1)} %get-tuple-element.39), channel_id=1, source_target_pairs={{2,0},{4,2},{6,4},{8,6},{10,8},{12,10},{14,12},{16,14},{18,16},{20... | collective-permute-start | bytes 165896 | tf_op jit(solution)/shard_map/ppermute | solution.py:25
  158.6 10.4 %collective-permute-start.26 = (f32[3,12,1,384]{3,2,1,0:T(1,128)S(1)}, f32[3,12,1,384]{3,2,1,0:T(1,128)S(1)}, u32[]{:S(2)}, u32[]{:S(2)}) collective-permute-start(f32[3,12,1,384]{3,2,1,0:T(1,128)S(1)} %get-tuple-element.36), channel_id=1, source_target_pairs={{0,1},{2,3},{4,5},{6,7},{8,9},{10,11},{12,13},{14,15},{16,17},{18,... | collective-permute-start | bytes 165896 | tf_op jit(solution)/shard_map/ppermute | solution.py:24
  159.9 9.2 %collective-permute-start.27 = (f32[3,12,1,384]{3,2,1,0:T(1,128)S(1)}, f32[3,12,1,384]{3,2,1,0:T(1,128)S(1)}, u32[]{:S(2)}, u32[]{:S(2)}) collective-permute-start(f32[3,12,1,384]{3,2,1,0:T(1,128)S(1)} %get-tuple-element.37), channel_id=1, source_target_pairs={{1,0},{3,2},{5,4},{7,6},{9,8},{11,10},{13,12},{15,14},{17,16},{19,... | collective-permute-start | bytes 165896 | tf_op jit(solution)/shard_map/ppermute | solution.py:25
  162.9 6.8 %collective-permute-start.24 = (f32[3,1,12,384]{3,2,1,0:T(8,128)S(1)}, f32[3,1,12,384]{3,2,1,0:T(8,128)S(1)}, u32[]{:S(2)}, u32[]{:S(2)}) collective-permute-start(f32[3,1,12,384]{3,2,1,0:T(8,128)S(1)} %get-tuple-element.34), channel_id=1, source_target_pairs={{0,2},{2,4},{4,6},{6,8},{8,10},{10,12},{12,14},{14,16},{16,18},{18... | collective-permute-start | bytes 165896 | tf_op jit(solution)/shard_map/ppermute | solution.py:24
  167.7 6.2 %collective-permute-start.25 = (f32[3,1,12,384]{3,2,1,0:T(8,128)S(1)}, f32[3,1,12,384]{3,2,1,0:T(8,128)S(1)}, u32[]{:S(2)}, u32[]{:S(2)}) collective-permute-start(f32[3,1,12,384]{3,2,1,0:T(8,128)S(1)} %get-tuple-element.35), channel_id=1, source_target_pairs={{2,0},{4,2},{6,4},{8,6},{10,8},{12,10},{14,12},{16,14},{18,16},{20... | collective-permute-start | bytes 165896 | tf_op jit(solution)/shard_map/ppermute | solution.py:25
  176.1 9.3 %collective-permute-start.30 = (f32[3,12,1,384]{3,2,1,0:T(1,128)S(1)}, f32[3,12,1,384]{3,2,1,0:T(1,128)S(1)}, u32[]{:S(2)}, u32[]{:S(2)}) collective-permute-start(f32[3,12,1,384]{3,2,1,0:T(1,128)S(1)} %get-tuple-element.32), channel_id=1, source_target_pairs={{0,1},{2,3},{4,5},{6,7},{8,9},{10,11},{12,13},{14,15},{16,17},{18,... | collective-permute-start | bytes 165896 | tf_op jit(solution)/shard_map/ppermute | solution.py:24
  177.4 8.1 %collective-permute-start.31 = (f32[3,12,1,384]{3,2,1,0:T(1,128)S(1)}, f32[3,12,1,384]{3,2,1,0:T(1,128)S(1)}, u32[]{:S(2)}, u32[]{:S(2)}) collective-permute-start(f32[3,12,1,384]{3,2,1,0:T(1,128)S(1)} %get-tuple-element.33), channel_id=1, source_target_pairs={{1,0},{3,2},{5,4},{7,6},{9,8},{11,10},{13,12},{15,14},{17,16},{19,... | collective-permute-start | bytes 165896 | tf_op jit(solution)/shard_map/ppermute | solution.py:25
  180.5 5.7 %collective-permute-start.28 = (f32[3,1,12,384]{3,2,1,0:T(8,128)S(1)}, f32[3,1,12,384]{3,2,1,0:T(8,128)S(1)}, u32[]{:S(2)}, u32[]{:S(2)}) collective-permute-start(f32[3,1,12,384]{3,2,1,0:T(8,128)S(1)} %get-tuple-element.30), channel_id=1, source_target_pairs={{0,2},{2,4},{4,6},{6,8},{8,10},{10,12},{12,14},{14,16},{16,18},{18... | collective-permute-start | bytes 165896 | tf_op jit(solution)/shard_map/ppermute | solution.py:24
  184.1 6.2 %collective-permute-start.29 = (f32[3,1,12,384]{3,2,1,0:T(8,128)S(1)}, f32[3,1,12,384]{3,2,1,0:T(8,128)S(1)}, u32[]{:S(2)}, u32[]{:S(2)}) collective-permute-start(f32[3,1,12,384]{3,2,1,0:T(8,128)S(1)} %get-tuple-element.31), channel_id=1, source_target_pairs={{2,0},{4,2},{6,4},{8,6},{10,8},{12,10},{14,12},{16,14},{18,16},{20... | collective-permute-start | bytes 165896 | tf_op jit(solution)/shard_map/ppermute | solution.py:25
  (4 other events, 128.5 us)
where the time goes:
time: 308 us; the launch traced here: 307 us
  starting transfers between devices  79.7 us (26%)
  other arithmetic  66 us (21%)
  local copies, waits for them, and re-layouts  60.9 us (20%)
  blocking collectives  57.6 us (19%)
  waiting for transfers between devices  39.3 us (13%)
    all_to_all x1, blocking collectives, shards(): lax.all_to_all(solved, 'space', split_axis=3, concat_axis=1, tiled=True)  57.6 us
    sub x3, other arithmetic, relax(): squares - fields * fields  46.9 us
    ppermute x16, starting transfers between devices, extended(): lax.ppermute(last, axis, up)  42.8 us
    ppermute x16, starting transfers between devices, extended(): lax.ppermute(leading, axis, [(b, a) for a, b in up])  36.9 us
    all_to_all x4, local copies, waits for them, and re-layouts, shards(): lax.all_to_all(solved, 'space', split_axis=3, concat_axis=1, tiled=True)  34.3 us
    ppermute x16, waiting for transfers between devices, extended(): lax.ppermute(leading, axis, [(b, a) for a, b in up])  30.8 us
    unnamed x14, local copies, waits for them, and re-layouts  13.2 us
    ppermute x16, waiting for transfers between devices, extended(): lax.ppermute(last, axis, up)  8.47 us
  transfers between devices with their start and end apart: 32, of which 14 were waited for; matrix products, arithmetic and copies ran while one was open for 1% of the time, Pallas kernels for 0%

commit v1 on v0

v1 whole, which is shorter than its diff:
```python
import functools

import jax
import jax.numpy as jnp
from jax import lax
from jax.experimental import pallas as pl
from jax.experimental.pallas import tpu as pltpu
from jax.sharding import PartitionSpec as P

STEPS = 3
ITERS = 4
DIAGONAL_SHIFT = 3.0
SPECTRUM_CENTRE = 12.0
SPECTRUM_RADIUS = 9.0

B = 12
F = 8
K = 384
H = 3
W = B + H
GO = ITERS + 1
HIGHEST = lax.Precision.HIGHEST
VMEM = pl.BlockSpec(memory_space=pltpu.VMEM)


def roll(x, shift, axis):
    return pltpu.roll(x, shift % x.shape[axis], axis)


def relax_kernel(
    ph, low, high, across, corner, own_speed, mix, ev, coef, down, up, first, second, speed
):
    slab = lax.axis_index("slab")
    own = 1 + H * slab
    other = 1 + B * (1 - slab)
    zero = jnp.zeros((F, K), jnp.float32)
    lane = lax.broadcasted_iota(jnp.int32, (F, K), 1)

    speed[0, 0] = low[H * B]
    speed[0, 1] = corner[H * H]
    speed[1, 0] = own_speed[...]
    speed[1, 1] = across[H * B]
    speed[2, 0] = high[H * B]
    speed[2, 1] = corner[2 * H * H + 1]

    def clear(a, _):
        for buf in (first, second):
            buf[a, 0] = zero
            buf[a, W + 1] = zero
        return 0

    lax.fori_loop(0, B + 2 * H, clear, 0)

    def fill(i, _):
        for j in range(B):
            first[H + i, own + j] = ph[i, j]
        for t in range(H):
            first[H + i, other + t] = across[H * i + t]
        return 0

    lax.fori_loop(0, B, fill, 0)
    for a in range(H):
        for j in range(B):
            first[a, own + j] = low[B * a + j]
            first[H + B + a, own + j] = high[B * a + j]
        for t in range(H):
            first[a, other + t] = corner[H * a + t]
            first[H + B + a, other + t] = corner[H * H + 1 + H * a + t]

    def update(x, around, s):
        square = x * x
        total = square + roll(square, 4, 0)
        total = total + roll(total, 2, 0)
        total = total + roll(total, 1, 0)
        left = jnp.where(lane == 0, 0.0, roll(x, 1, 1))
        right = jnp.where(lane == K - 1, 0.0, roll(x, -1, 1))
        summed = around + (left + right)
        return x - s * (x * (5.0 + 3.0 * total - 2.0 * square) - summed)

    def window_step(src, dst, depth):
        def plane(a, _):
            group = (a >= H).astype(jnp.int32) + (a >= H + B).astype(jnp.int32)
            before = src[a, 0]
            x = src[a, 1]
            for w in range(W):
                after = src[a, w + 2]
                whose = slab if w < H else (1 - slab if w >= B else 0)
                around = (before + after) + (src[a - 1, w + 1] + src[a + 1, w + 1])
                dst[a, w + 1] = update(x, around, speed[group, whose])
                before, x = x, after
            return 0

        lax.fori_loop(depth, B + 2 * H - depth, plane, 0)

    window_step(first, second, 1)
    window_step(second, first, 2)

    row = lax.broadcasted_iota(jnp.int32, (4 * B, K), 0)
    is_excess = (row >= B) & (row < 2 * B)

    def last_plane(i, _):
        a = i + H
        before = first[a, own - 1]
        x = first[a, own]
        for j in range(B):
            after = first[a, own + j + 1]
            around = (before + after) + (first[a - 1, own + j] + first[a + 1, own + j])
            ev[i, j] = update(x, around, own_speed[...])
            before, x = x, after
        values = ev[i].reshape(B * F, K)
        mixed = jnp.dot(
            mix[...], values * values, precision=HIGHEST, preferred_element_type=jnp.float32
        )
        total = mixed[: 4 * B]
        strain = mixed[4 * B : 8 * B]
        dilation = mixed[8 * B :]
        saturation = total / (1.0 + total)
        excess = 0.5 * saturation
        stress = (1.5 + saturation) * dilation + 2.0 * (1.0 + excess) * strain
        coef[i] = jnp.where(is_excess, excess, stress)
        return 0

    lax.fori_loop(0, B, last_plane, 0)
    for t in range(ITERS):
        down[4 * B * t : 4 * B * (t + 1)] = coef[t]
        up[4 * B * t : 4 * B * (t + 1)] = coef[B - ITERS + t]
    down[4 * B * ITERS :] = coef[ITERS, :16]
    up[4 * B * ITERS :] = coef[B - ITERS - 1, :16]


def solve_kernel(
    coef, low, high, o_coef, o_low, o_high, out,
    s0, s1, s2, ex, dia, wi, wjp, wjm, wkp, wkm, dir_a, dir_b, res, sol, rows,
):
    slab = lax.axis_index("slab")
    place = lax.axis_index("space")
    count = lax.axis_size("space")
    bottom = slab == 0
    J = 2 * B
    N = B + 2 * GO
    row = lax.broadcasted_iota(jnp.int32, (J, K), 0)
    lane = lax.broadcasted_iota(jnp.int32, (J, K), 1)

    def joined(mine, others):
        lo = jnp.where(bottom, mine, others)
        hi = jnp.where(bottom, others, mine)
        n = mine.shape[0] // B
        return [
            jnp.concatenate([lo[B * c : B * c + B], hi[B * c : B * c + B]], 0) for c in range(n)
        ]

    def put(a, mine, others):
        s0[a], ex[a], s1[a], s2[a] = joined(mine, others)

    def put_own(i, _):
        put(i + GO, coef[i], o_coef[i])
        return 0

    lax.fori_loop(0, B, put_own, 0)
    for t in range(ITERS):
        part = slice(4 * B * t, 4 * B * (t + 1))
        put(1 + t, low[part], o_low[part])
        put(GO + B + t, high[part], o_high[part])
    tail = slice(4 * B * ITERS, 4 * B * ITERS + 16)
    (s0[0],) = joined(low[tail], o_low[tail])
    (s0[N - 1],) = joined(high[tail], o_high[tail])

    def next_j(x):
        return jnp.where(row == J - 1, 0.0, roll(x, -1, 0))

    def last_j(x):
        return jnp.where(row == 0, 0.0, roll(x, 1, 0))

    def next_k(x):
        return jnp.where(lane == K - 1, 0.0, roll(x, -1, 1))

    def last_k(x):
        return jnp.where(lane == 0, 0.0, roll(x, 1, 1))

    def force(a, _):
        forcing = (
            0.5 * (s0[a + 1] - s0[a - 1]),
            0.5 * (next_j(s1[a]) - last_j(s1[a])),
            0.5 * (next_k(s2[a]) - last_k(s2[a])),
        )
        for c in range(3):
            dir_a[c, a] = forcing[c] / SPECTRUM_CENTRE
            res[c, a] = forcing[c]
        return 0

    lax.fori_loop(1, N - 1, force, 0)

    wi[1] = 1.0 + 0.5 * (ex[1] + ex[2])

    def weigh(a, _):
        e = ex[a]
        i_next = 1.0 + 0.5 * (e + ex[a + 1])
        i_last = 1.0 + 0.5 * (e + ex[a - 1])
        j_next = 1.0 + 0.5 * (e + next_j(e))
        j_last = 1.0 + 0.5 * (e + last_j(e))
        k_next = 1.0 + 0.5 * (e + next_k(e))
        k_last = 1.0 + 0.5 * (e + last_k(e))
        dia[a] = DIAGONAL_SHIFT + ((i_next + i_last) + (j_next + j_last) + (k_next + k_last))
        wi[a] = i_next
        wjp[a] = jnp.where(row == J - 1, 0.0, j_next)
        wjm[a] = jnp.where(row == 0, 0.0, j_last)
        wkp[a] = jnp.where(lane == K - 1, 0.0, k_next)
        wkm[a] = jnp.where(lane == 0, 0.0, k_last)
        return 0

    lax.fori_loop(2, N - 2, weigh, 0)

    @pl.when(place == 0)
    def _():
        wi[GO - 1] = jnp.zeros((J, K), jnp.float32)

    @pl.when(place == count - 1)
    def _():
        wi[GO + B - 1] = jnp.zeros((J, K), jnp.float32)

    def apply(src, c, a):
        v = src[c, a]
        r = res[c, a] - dia[a] * v
        r = r + wi[a] * src[c, a + 1]
        r = r + wi[a - 1] * src[c, a - 1]
        r = r + wjp[a] * roll(v, -1, 0)
        r = r + wjm[a] * roll(v, 1, 0)
        r = r + wkp[a] * roll(v, -1, 1)
        r = r + wkm[a] * roll(v, 1, 1)
        return v, r

    ratio = SPECTRUM_RADIUS / SPECTRUM_CENTRE
    src, dst = dir_a, dir_b
    for t in range(ITERS):
        ratio_next = 1.0 / (2.0 * SPECTRUM_CENTRE / SPECTRUM_RADIUS - ratio)
        keep, gain = ratio_next * ratio, 2.0 * ratio_next / SPECTRUM_RADIUS
        ratio = ratio_next
        if t == ITERS - 1:
            break

        def plane(a, _, src=src, dst=dst, keep=keep, gain=gain, t=t, inner=False):
            for c in range(3):
                v, r = apply(src, c, a)
                res[c, a] = r
                dst[c, a] = keep * v + gain * r
                if inner:
                    sol[c, a - GO] = v if t == 0 else sol[c, a - GO] + v
            return 0

        lax.fori_loop(2 + t, GO, plane, 0)
        lax.fori_loop(GO, GO + B, functools.partial(plane, inner=True), 0)
        lax.fori_loop(GO + B, N - 2 - t, plane, 0)
        src, dst = dst, src

    third = lax.broadcasted_iota(jnp.int32, (B, K), 1) % 3
    target = lax.broadcasted_iota(jnp.int32, (K // 3, K), 0)
    source = lax.broadcasted_iota(jnp.int32, (K // 3, K), 1) // 3
    pick = jnp.where(target == source, 1.0, 0.0)
    rows[9 * B :] = jnp.zeros((128 - 9 * B, K), jnp.float32)

    def finish(i, _):
        a = i + GO
        for c in range(3):
            v, r = apply(src, c, a)
            total = sol[c, i] + v + (keep * v + gain * r)
            mine = jnp.where(bottom, total[:B], total[B:])
            for q in range(3):
                g = 3 * c + q
                rows[B * g : B * g + B] = jnp.where(third == q, mine, 0.0)
        moved = lax.dot_general(
            pick,
            rows[...],
            (((1,), (1,)), ((), ())),
            precision=HIGHEST,
            preferred_element_type=jnp.float32,
        )
        out[pl.ds(i, K // 3, stride=B), :] = moved
        return 0

    lax.fori_loop(0, B, finish, 0)


def unpack_kernel(got, out):
    tiles = got.shape[0] // 128
    for t in range(tiles):
        turned = got[128 * t : 128 * (t + 1), :].T
        for c in range(3):
            for q in range(3):
                g = 3 * c + q
                out[c, q, :, 128 * t : 128 * (t + 1)] = turned[B * g : B * g + B]


def call(kernel, shapes, inputs, scratch=(), name=None):
    return pl.pallas_call(
        kernel,
        out_shape=[jax.ShapeDtypeStruct(s, jnp.float32) for s in shapes],
        in_specs=[VMEM] * len(inputs),
        out_specs=[VMEM] * len(shapes),
        scratch_shapes=[pltpu.VMEM(s, jnp.float32) for s in scratch],
        compiler_params=pltpu.CompilerParams(vmem_limit_bytes=58 * 1024 * 1024),
        name=name,
    )(*inputs)


def shards(phases, mobility, active, variants):
    count = lax.axis_size("space")
    slab = lax.axis_index("slab")
    upward = [(i, i + 1) for i in range(count - 1)]
    downward = [(b, a) for a, b in upward]
    swap = [(0, 1), (1, 0)]

    ph = jnp.transpose(phases, (1, 2, 0, 3))
    flags = jnp.repeat(active[0, 0].astype(jnp.float32).T, B, axis=1)
    speed = mobility[:, None] * flags

    def edge(array, start):
        return lax.dynamic_slice_in_dim(array, start, H, axis=1).reshape(-1, F, K)

    start = (B - H) * (1 - slab)
    low = lax.ppermute(
        jnp.concatenate([ph[B - H :].reshape(H * B, F, K), speed[None]]), "space", upward
    )
    high = lax.ppermute(
        jnp.concatenate([ph[:H].reshape(H * B, F, K), speed[None]]), "space", downward
    )
    across = lax.ppermute(jnp.concatenate([edge(ph, start), speed[None]]), "slab", swap)
    corner = lax.ppermute(
        jnp.concatenate(
            [
                edge(low[: H * B].reshape(H, B, F, K), start),
                low[H * B :],
                edge(high[: H * B].reshape(H, B, F, K), start),
                high[H * B :],
            ]
        ),
        "slab",
        swap,
    )

    by_field = jnp.concatenate([variants.T[:1], jnp.zeros((1, F)), variants.T[1:]])
    table = jnp.stack(
        [
            jnp.ones((4, F), jnp.float32),
            by_field,
            jnp.broadcast_to(jnp.sum(variants, axis=1), (4, F)),
        ]
    )
    mix = (table[:, :, None, None, :] * jnp.eye(B)[None, None, :, :, None]).reshape(12 * B, B * F)

    block = (B + 2 * H, W + 2, F, K)
    message = (4 * B * ITERS + 16, K)
    evolved, coef, down, up = call(
        relax_kernel,
        [(B, B, F, K), (B, 4 * B, K), message, message],
        [ph, low, high, across, corner, speed, mix],
        [block, block, (3, 2, F, K)],
        name="relax",
    )
    low = lax.ppermute(up, "space", upward)
    high = lax.ppermute(down, "space", downward)
    o_coef = lax.ppermute(coef, "slab", swap)
    both = lax.ppermute(jnp.stack([low, high]), "slab", swap)
    J, N = 2 * B, B + 2 * GO
    (packed,) = call(
        solve_kernel,
        [(K // 3 * B, 128)],
        [coef, low, high, o_coef, both[0], both[1]],
        [(N, J, K)] * 10 + [(3, N, J, K)] * 3 + [(3, B, J, K), (128, K)],
        name="solve",
    )
    arrived = lax.all_to_all(packed.reshape(count, 1, B * 128), "space", 0, 0, tiled=True)
    (displacement,) = call(
        unpack_kernel, [(3, K // count, B, count * B)], [arrived.reshape(count * B, 128)], name="unpack"
    )
    return jnp.transpose(evolved, (2, 0, 1, 3)), displacement


def solution(mesh):
    placed = (P(None, "space", "slab", None), P(), P("space", "slab", None, None), P())
    return jax.shard_map(
        shards,
        mesh=mesh,
        in_specs=placed,
        out_specs=(P(None, "space", "slab", None), P(None, "space", "slab", None)),
        check_vma=False,
    )
```

time: 308 us -> 135 us (0.44)
  other arithmetic: 66 us -> 1.92 us
  starting transfers between devices: 79.7 us -> 16.6 us
  local copies, waits for them, and re-layouts: 60.9 us -> 7.17 us
  Pallas kernels: 0 us -> 37 us
  waiting for transfers between devices: 39.3 us -> 20.6 us
  blocking collectives: 57.6 us -> 50 us
    ppermute x32 -> x8, starting transfers between devices: 79.7 us -> 16.6 us  [the longest x1 4.13 us: shards(): low = lax.ppermute(up, 'space', upward)]
    sub x3 -> x0, other arithmetic: 46.9 us -> none  [relax(): squares - fields * fields]
    pallas_call x0 -> x3, Pallas kernels: none -> 37 us  [call(): pl.pallas_call(kernel, out_shape=[jax.ShapeDtypeStruct(s, jnp.float32) fo...]
    all_to_all x4 -> x0, local copies, waits for them, and re-layouts: 34.3 us -> none  [shards(): lax.all_to_all(solved, 'space', split_axis=3, concat_axis=1, tiled=True)]
    ppermute x32 -> x8, waiting for transfers between devices: 39.3 us -> 20.6 us  [the longest x1 8.13 us: shards(): lax.ppermute(jnp.concatenate([ph[:H].reshape(H * B, F, K), speed[None]]),...]
    unnamed x14 -> x18, local copies, waits for them, and re-layouts: 13.2 us -> 2.4 us
    all_to_all x1, blocking collectives: 57.6 us -> 50 us  [shards(): lax.all_to_all(packed.reshape(count, 1, B * 128), 'space', 0, 0, tiled=True)]
    add x6 -> x0, other arithmetic: 7.3 us -> none  [the longest x3 4.27 us: chebyshev(): ratio_next * ratio_now * direction]
  transfers between devices with their start and end apart: 32 -> 8, of which waited for: 14 -> 6; matrix products, arithmetic and copies ran while one was open for 1% -> 2% of each run, Pallas kernels for 0% -> 0%
where the time goes in v1:
time: 135 us; the launch traced here: 134 us
  blocking collectives  50 us (37%)
  Pallas kernels  37 us (27%)
  waiting for transfers between devices  20.6 us (15%)
  starting transfers between devices  16.6 us (12%)
  local copies, waits for them, and re-layouts  7.17 us (5%)
  other arithmetic  1.92 us (1%)
    all_to_all x1, blocking collectives, shards(): lax.all_to_all(packed.reshape(count, 1, B * 128), 'space', 0, 0, tiled=True)  50 us
    pallas_call x3, Pallas kernels, call(): pl.pallas_call(kernel, out_shape=[jax.ShapeDtypeStruct(s, jnp.float32) fo...  37 us
    ppermute x1, waiting for transfers between devices, shards(): lax.ppermute(jnp.concatenate([ph[:H].reshape(H * B, F, K), speed[None]]),...  8.13 us
    ppermute x1, waiting for transfers between devices, shards(): low = lax.ppermute(up, 'space', upward)  5.87 us
    ppermute x1, starting transfers between devices, shards(): low = lax.ppermute(up, 'space', upward)  4.13 us
    ppermute x1, starting transfers between devices, shards(): lax.ppermute(jnp.concatenate([ph[B - H:].reshape(H * B, F, K), speed[None...  4.01 us
    ppermute x1, waiting for transfers between devices, shards(): high = lax.ppermute(down, 'space', downward)  3.74 us
    ppermute x1, starting transfers between devices, shards(): lax.ppermute(jnp.concatenate([edge(ph, start), speed[None]]), 'slab', swap)  3.29 us
  transfers between devices with their start and end apart: 8, of which 6 were waited for; matrix products, arithmetic and copies ran while one was open for 2% of the time, Pallas kernels for 0%

profile of v1, /device:TPU:1, one launch (start us, length us, event | category | flops | bytes accessed | tf_op | source)
XLA Modules:
  0.0 134.1 jit_solution(2753531960818859798)
XLA Ops:
  0.6 0.7 convert_bitcast_fusion
  1.4 0.1 reshape.79
  1.6 1.1 constant_dynamic-slice_fusion.2
  2.6 1.2 fusion.1
  4.0 3.3 %collective-permute-start.2 = (f32[37,8,384]{2,1,0:T(8,128)S(1)}, f32[37,8,384]{2,1,0:T(8,128)S(1)}, u32[]{:S(2)}, u32[]{:S(2)}) collective-permute-start(f32[37,8,384]{2,1,0:T(8,128)S(1)} %get-tuple-element.14), channel_id=1, source_target_pairs={{0,1},{1,0},{2,3},{3,2},{4,5},{5,4},{6,7},{7,6},{8,9},{9,8},{10,11... | collective-permute-start | bytes 1363976 | tf_op jit(solution)/shard_map/ppermute | solution.py:326
  7.3 1.3 collective-permute-start.1
  8.6 4.0 %collective-permute-start = (f32[37,8,384]{2,1,0:T(8,128)S(1)}, f32[37,8,384]{2,1,0:T(8,128)S(1)}, u32[]{:S(2)}, u32[]{:S(2)}) collective-permute-start(f32[37,8,384]{2,1,0:T(8,128)S(1)} %get-tuple-element.16), channel_id=1, source_target_pairs={{0,2},{2,4},{4,6},{6,8},{8,10},{10,12},{12,14},{14,16},{16,18},{18... | collective-permute-start | bytes 1363976 | tf_op jit(solution)/shard_map/ppermute | solution.py:320
  12.9 0.1 copy.8
  13.0 8.1 %collective-permute-done.1.high = f32[37,8,384]{2,1,0:T(8,128)S(1)} collective-permute-done((f32[37,8,384]{2,1,0:T(8,128)S(1)}, f32[37,8,384]{2,1,0:T(8,128)S(1)}, u32[]{:S(2)}, u32[]{:S(2)}) %collective-permute-start.1) | collective-permute-done | bytes 454688 | tf_op jit(solution)/shard_map/ppermute | solution.py:323
  21.2 0.8 collective-permute-done.low
  22.2 1.2 collective-permute-start.3
  23.4 0.2 broadcast_multiply_fusion
  23.6 0.1 reshape.86
  23.7 0.3 mul.36
  24.0 0.7 copy.9.mix
  24.7 0.7 broadcast_multiply_fusion.1.own_speed
  25.4 0.8 copy-done.5
  26.2 0.7 copy-done.6
  26.9 14.7 %relax.1 = (f32[12,12,8,384]{3,2,1,0:T(8,128)}, f32[12,48,384]{2,1,0:T(8,128)}, f32[208,384]{1,0:T(8,128)}, f32[208,384]{1,0:T(8,128)}) custom-call(f32[12,12,8,384]{3,2,1,0:T(8,128)} %bitcast.31, f32[37,8,384]{2,1,0:T(8,128)} %copy-done.1, f32[37,8,384]{2,1,0:T(8,128)} %copy-done, f32[37,8,384]{2,1,0:T(8,128)} %copy-done.5, f32[20,8,384]{2,1,0:T(8,128)} %copy-done.6, ...), custom_call_target="tpu_custom_call" | custom-call | tf_op jit(solution)/shard_map/relax/pallas_call | solution.py:294
  41.6 4.1 %collective-permute-start.4 = (f32[208,384]{1,0:T(8,128)}, f32[208,384]{1,0:T(8,128)S(1)}, u32[]{:S(2)}, u32[]{:S(2)}) collective-permute-start(f32[208,384]{1,0:T(8,128)} %get-tuple-element.8), channel_id=1, source_target_pairs={{0,2},{2,4},{4,6},{6,8},{8,10},{10,12},{12,14},{14,16},{16,18},{18... | collective-permute-start | bytes 958472 | tf_op jit(solution)/shard_map/ppermute | solution.py:359
  45.7 1.3 collective-permute-start.5
  47.0 5.9 %collective-permute-done.4.low = f32[208,384]{1,0:T(8,128)S(1)} collective-permute-done((f32[208,384]{1,0:T(8,128)}, f32[208,384]{1,0:T(8,128)S(1)}, u32[]{:S(2)}, u32[]{:S(2)}) %collective-permute-start.4) | collective-permute-done | bytes 319520 | tf_op jit(solution)/shard_map/ppermute | solution.py:359
  52.9 3.7 %collective-permute-done.5.high = f32[208,384]{1,0:T(8,128)S(1)} collective-permute-done((f32[208,384]{1,0:T(8,128)}, f32[208,384]{1,0:T(8,128)S(1)}, u32[]{:S(2)}, u32[]{:S(2)}) %collective-permute-start.5) | collective-permute-done | bytes 319520 | tf_op jit(solution)/shard_map/ppermute | solution.py:360
  56.7 1.2 collective-permute-start.7
  57.9 0.1 collective-permute-start.6
  58.0 1.6 %collective-permute-done.7 = f32[2,208,384]{2,1,0:T(8,128)S(1)} collective-permute-done((f32[2,208,384]{2,1,0:T(8,128)S(1)}, f32[2,208,384]{2,1,0:T(8,128)S(1)}, u32[]{:S(2)}, u32[]{:S(2)}) %collective-permute-start.7) | collective-permute-done | bytes 639008 | tf_op jit(solution)/shard_map/ppermute | solution.py:362
  59.6 0.9 slice_bitcast_fusion
  60.5 0.4 collective-permute-done.6.o_coef
  60.9 0.9 copy-done.4
  61.8 19.9 %solve.1 = f32[1536,128]{1,0:T(8,128)} custom-call(f32[12,48,384]{2,1,0:T(8,128)} %get-tuple-element.7.coef, f32[208,384]{1,0:T(8,128)} %copy-done.2, f32[208,384]{1,0:T(8,128)} %copy-done.3, f32[12,48,384]{2,1,0:T(8,128)} %copy-done.4, f32[208,384]{1,0:T(8,128)} %get-tuple-element.13.o_low, f32[208,384]{1,0:T(8,128)} %get-tuple-element.12.o_high), custom_call_target="tpu_custom_call" | custom-call | tf_op jit(solution)/shard_map/solve/pallas_call | solution.py:294
  81.7 50.0 %all_to_all.5 = f32[128,1,1536]{2,1,0:T(1,128)} all-to-all(f32[128,1,1536]{2,1,0:T(1,128)} %bitcast.33), channel_id=1, replica_groups=mesh['space'=128,'slab'=2] {'space'}, dimensions={0} | all-to-all | bytes 1572864 | tf_op jit(solution)/shard_map/all_to_all | solution.py:371
  131.8 2.3 %unpack.1 = f32[3,3,12,1536]{3,2,1,0:T(8,128)} custom-call(f32[1536,128]{1,0:T(8,128)} %bitcast.32), custom_call_target="tpu_custom_call" | custom-call | tf_op jit(solution)/shard_map/unpack/pallas_call | solution.py:294
  (37 shorter events, 0.7 us)
Async XLA Ops:
  0.6 3.2 %copy-start.8 = (f32[8]{0:T(128)S(1)}, f32[8]{0:T(128)}, u32[]{:S(2)}) copy-start(f32[8]{0:T(128)} %param.5) | copy-start | bytes 100
  3.8 8.8 %copy-start.7 = (f32[8,3]{0,1:T(4,128)S(1)}, f32[8,3]{0,1:T(4,128)}, u32[]{:S(2)}) copy-start(f32[8,3]{0,1:T(4,128)} %param.7) | copy-start | bytes 292
  4.0 21.4 %collective-permute-start.2 = (f32[37,8,384]{2,1,0:T(8,128)S(1)}, f32[37,8,384]{2,1,0:T(8,128)S(1)}, u32[]{:S(2)}, u32[]{:S(2)}) collective-permute-start(f32[37,8,384]{2,1,0:T(8,128)S(1)} %get-tuple-element.14), channel_id=1, source_target_pairs={{0,1},{1,0},{2,3},{3,2},{4,5},{5,4},{6,7},{7,6},{8,9},{9,8},{10,11... | collective-permute-start | bytes 1363976 | tf_op jit(solution)/shard_map/ppermute | solution.py:326
  7.3 13.8 %collective-permute-start.1 = (f32[37,8,384]{2,1,0:T(8,128)S(1)}, f32[37,8,384]{2,1,0:T(8,128)S(1)}, u32[]{:S(2)}, u32[]{:S(2)}) collective-permute-start(f32[37,8,384]{2,1,0:T(8,128)S(1)} %get-tuple-element.15), channel_id=1, source_target_pairs={{2,0},{4,2},{6,4},{8,6},{10,8},{12,10},{14,12},{16,14},{18,16},{20... | collective-permute-start | bytes 1363976 | tf_op jit(solution)/shard_map/ppermute | solution.py:323
  8.6 13.5 %collective-permute-start = (f32[37,8,384]{2,1,0:T(8,128)S(1)}, f32[37,8,384]{2,1,0:T(8,128)S(1)}, u32[]{:S(2)}, u32[]{:S(2)}) collective-permute-start(f32[37,8,384]{2,1,0:T(8,128)S(1)} %get-tuple-element.16), channel_id=1, source_target_pairs={{0,2},{2,4},{4,6},{6,8},{8,10},{10,12},{12,14},{14,16},{16,18},{18... | collective-permute-start | bytes 1363976 | tf_op jit(solution)/shard_map/ppermute | solution.py:320
  21.1 2.9 %copy-start = (f32[37,8,384]{2,1,0:T(8,128)}, f32[37,8,384]{2,1,0:T(8,128)S(1)}, u32[]{:S(2)}) copy-start(f32[37,8,384]{2,1,0:T(8,128)S(1)} %collective-permute-done.1.high) | copy-start | bytes 1363972
  22.1 3.4 %copy-start.1 = (f32[37,8,384]{2,1,0:T(8,128)}, f32[37,8,384]{2,1,0:T(8,128)S(1)}, u32[]{:S(2)}) copy-start(f32[37,8,384]{2,1,0:T(8,128)S(1)} %collective-permute-done.low) | copy-start | bytes 1363972
  22.2 3.2 %collective-permute-start.3 = (f32[20,8,384]{2,1,0:T(8,128)S(1)}, f32[20,8,384]{2,1,0:T(8,128)S(1)}, u32[]{:S(2)}, u32[]{:S(2)}) collective-permute-start(f32[20,8,384]{2,1,0:T(8,128)S(1)} %pad_maximum_fusion.4), channel_id=1, source_target_pairs={{0,1},{1,0},{2,3},{3,2},{4,5},{5,4},{6,7},{7,6},{8,9},{9,8},{10,11... | collective-permute-start | bytes 737288 | tf_op jit(solution)/shard_map/ppermute | solution.py:327
  25.4 0.8 copy-start.5
  26.2 0.7 copy-start.6
  41.6 11.3 %collective-permute-start.4 = (f32[208,384]{1,0:T(8,128)}, f32[208,384]{1,0:T(8,128)S(1)}, u32[]{:S(2)}, u32[]{:S(2)}) collective-permute-start(f32[208,384]{1,0:T(8,128)} %get-tuple-element.8), channel_id=1, source_target_pairs={{0,2},{2,4},{4,6},{6,8},{8,10},{10,12},{12,14},{14,16},{16,18},{18... | collective-permute-start | bytes 958472 | tf_op jit(solution)/shard_map/ppermute | solution.py:359
  45.7 10.9 %collective-permute-start.5 = (f32[208,384]{1,0:T(8,128)}, f32[208,384]{1,0:T(8,128)S(1)}, u32[]{:S(2)}, u32[]{:S(2)}) collective-permute-start(f32[208,384]{1,0:T(8,128)} %get-tuple-element.9), channel_id=1, source_target_pairs={{2,0},{4,2},{6,4},{8,6},{10,8},{12,10},{14,12},{16,14},{18,16},{20... | collective-permute-start | bytes 958472 | tf_op jit(solution)/shard_map/ppermute | solution.py:360
  52.9 8.0 %copy-start.2 = (f32[208,384]{1,0:T(8,128)}, f32[208,384]{1,0:T(8,128)S(1)}, u32[]{:S(2)}) copy-start(f32[208,384]{1,0:T(8,128)S(1)} %collective-permute-done.4.low) | copy-start | bytes 958468
  56.7 4.3 %copy-start.3 = (f32[208,384]{1,0:T(8,128)}, f32[208,384]{1,0:T(8,128)S(1)}, u32[]{:S(2)}) copy-start(f32[208,384]{1,0:T(8,128)S(1)} %collective-permute-done.5.high) | copy-start | bytes 958468
  56.7 2.9 %collective-permute-start.7 = (f32[2,208,384]{2,1,0:T(8,128)S(1)}, f32[2,208,384]{2,1,0:T(8,128)S(1)}, u32[]{:S(2)}, u32[]{:S(2)}) collective-permute-start(f32[2,208,384]{2,1,0:T(8,128)S(1)} %pad_maximum_fusion.3), channel_id=1, source_target_pairs={{0,1},{1,0},{2,3},{3,2},{4,5},{5,4},{6,7},{7,6},{8,9},{9,8},{10,11... | collective-permute-start | bytes 1916936 | tf_op jit(solution)/shard_map/ppermute | solution.py:362
  57.9 3.0 %collective-permute-start.6 = (f32[12,48,384]{2,1,0:T(8,128)}, f32[12,48,384]{2,1,0:T(8,128)S(1)}, u32[]{:S(2)}, u32[]{:S(2)}) collective-permute-start(f32[12,48,384]{2,1,0:T(8,128)} %get-tuple-element.7.coef), channel_id=1, source_target_pairs={{0,1},{1,0},{2,3},{3,2},{4,5},{5,4},{6,7},{7,6},{8,9},{9,8},{10,11... | collective-permute-start | bytes 2654216 | tf_op jit(solution)/shard_map/ppermute | solution.py:361
  60.9 0.9 copy-start.4

commit v2 on v1

--- a/solution.py
+++ b/solution.py
@@ -27,21 +27,58 @@
     return pltpu.roll(x, shift % x.shape[axis], axis)
 
 
+def parity():
+    even = 1 - lax.axis_index("space") % 2
+    return even, 1 - even
+
+
+def pack_kernel(ph, mobility, active, to_near, to_far, to_other, sems):
+    even, odd = parity()
+    start = (B - H) * (1 - lax.axis_index("slab"))
+    copies = []
+    for t in range(H):
+        for message, top in ((to_near, even), (to_far, odd)):
+            source = ph.at[(B - H) * top + t]
+            copies.append((source, message.at[pl.ds(B * t, B)]))
+    for i in range(B):
+        copies.append((ph.at[i, pl.ds(start, H)], to_other.at[pl.ds(H * i, H)]))
+    copies = [pltpu.make_async_copy(a, b, sems.at[n]) for n, (a, b) in enumerate(copies)]
+    for copy in copies:
+        copy.start()
+    scaled = active[...].astype(jnp.float32) * mobility[...]
+    bricks = K // B
+    brick = lax.broadcasted_iota(jnp.int32, (bricks, K), 0)
+    spread = jnp.where(brick == lax.broadcasted_iota(jnp.int32, (bricks, K), 1) // B, 1.0, 0.0)
+    speed = lax.dot_general(
+        scaled,
+        spread,
+        (((0,), (0,)), ((), ())),
+        precision=HIGHEST,
+        preferred_element_type=jnp.float32,
+    )
+    for message in (to_near, to_far, to_other):
+        message[H * B] = speed
+    for copy in copies:
+        copy.wait()
+
+
 def relax_kernel(
-    ph, low, high, across, corner, own_speed, mix, ev, coef, down, up, first, second, speed
+    ph, mine, near, far, across, c_near, c_far, mix, ev, coef, m_near, m_far, first, second, speed
 ):
+    even, odd = parity()
+    halos = ((near, c_near, even), (far, c_far, odd))
+    own_speed = mine.at[H * B]
     slab = lax.axis_index("slab")
     own = 1 + H * slab
     other = 1 + B * (1 - slab)
     zero = jnp.zeros((F, K), jnp.float32)
     lane = lax.broadcasted_iota(jnp.int32, (F, K), 1)
 
-    speed[0, 0] = low[H * B]
-    speed[0, 1] = corner[H * H]
+    for halo, corner, top in halos:
+        speed[2 * top, 0] = halo[H * B]
+        speed[2 * top, 1] = corner[H * H]
     speed[1, 0] = own_speed[...]
     speed[1, 1] = across[H * B]
-    speed[2, 0] = high[H * B]
-    speed[2, 1] = corner[2 * H * H + 1]
 
     def clear(a, _):
         for buf in (first, second):
@@ -59,13 +96,12 @@
         return 0
 
     lax.fori_loop(0, B, fill, 0)
-    for a in range(H):
-        for j in range(B):
-            first[a, own + j] = low[B * a + j]
-            first[H + B + a, own + j] = high[B * a + j]
-        for t in range(H):
-            first[a, other + t] = corner[H * a + t]
-            first[H + B + a, other + t] = corner[H * H + 1 + H * a + t]
+    for halo, corner, top in halos:
+        for a in range(H):
+            for j in range(B):
+                first[(H + B) * top + a, own + j] = halo[B * a + j]
+            for t in range(H):
+                first[(H + B) * top + a, other + t] = corner[H * a + t]
 
     def update(x, around, s):
         square = x * x
@@ -121,17 +157,17 @@
         return 0
 
     lax.fori_loop(0, B, last_plane, 0)
-    for t in range(ITERS):
-        down[4 * B * t : 4 * B * (t + 1)] = coef[t]
-        up[4 * B * t : 4 * B * (t + 1)] = coef[B - ITERS + t]
-    down[4 * B * ITERS :] = coef[ITERS, :16]
-    up[4 * B * ITERS :] = coef[B - ITERS - 1, :16]
+    for message, top in ((m_near, even), (m_far, odd)):
+        for t in range(ITERS):
+            message[4 * B * t : 4 * B * (t + 1)] = coef[(B - ITERS) * top + t]
+        message[4 * B * ITERS :] = coef[ITERS + (B - 2 * ITERS - 1) * top, :16]
 
 
 def solve_kernel(
-    coef, low, high, o_coef, o_low, o_high, out,
-    s0, s1, s2, ex, dia, wi, wjp, wjm, wkp, wkm, dir_a, dir_b, res, sol, rows,
+    coef, near, far, o_coef, o_near, o_far, out,
+    s0, s1, s2, ex, dia, wi, wjp, wjm, wkp, wkm, dir_a, dir_b, res, sol, rows, flat,
 ):
+    even, odd = parity()
     slab = lax.axis_index("slab")
     place = lax.axis_index("space")
     count = lax.axis_size("space")
@@ -157,13 +193,12 @@
         return 0
 
     lax.fori_loop(0, B, put_own, 0)
-    for t in range(ITERS):
-        part = slice(4 * B * t, 4 * B * (t + 1))
-        put(1 + t, low[part], o_low[part])
-        put(GO + B + t, high[part], o_high[part])
     tail = slice(4 * B * ITERS, 4 * B * ITERS + 16)
-    (s0[0],) = joined(low[tail], o_low[tail])
-    (s0[N - 1],) = joined(high[tail], o_high[tail])
+    for halo, others, top in ((near, o_near, even), (far, o_far, odd)):
+        for t in range(ITERS):
+            part = slice(4 * B * t, 4 * B * (t + 1))
+            put(1 + t + (GO + B - 1) * top, halo[part], others[part])
+        (s0[(N - 1) * top],) = joined(halo[tail], others[tail])
 
     def next_j(x):
         return jnp.where(row == J - 1, 0.0, roll(x, -1, 0))
@@ -274,30 +309,33 @@
             precision=HIGHEST,
             preferred_element_type=jnp.float32,
         )
-        out[pl.ds(i, K // 3, stride=B), :] = moved
+        flat[pl.ds(i, K // 3, stride=B), :] = moved
         return 0
 
     lax.fori_loop(0, B, finish, 0)
-
-
-def unpack_kernel(got, out):
-    tiles = got.shape[0] // 128
-    for t in range(tiles):
-        turned = got[128 * t : 128 * (t + 1), :].T
+    for n in range(out.shape[0]):
+        out[n] = flat[B * n : B * (n + 1), :]
+
+
+def unpack_kernel(got, out, flat):
+    for n in range(got.shape[0]):
+        flat[B * n : B * (n + 1), :] = got[n]
+    for t in range(flat.shape[0] // 128):
+        turned = flat[128 * t : 128 * (t + 1), :].T
         for c in range(3):
             for q in range(3):
                 g = 3 * c + q
                 out[c, q, :, 128 * t : 128 * (t + 1)] = turned[B * g : B * g + B]
 
 
-def call(kernel, shapes, inputs, scratch=(), name=None):
+def call(kernel, shapes, inputs, scratch=(), name=None, grant=8, in_specs=None, extra=()):
     return pl.pallas_call(
         kernel,
         out_shape=[jax.ShapeDtypeStruct(s, jnp.float32) for s in shapes],
-        in_specs=[VMEM] * len(inputs),
+        in_specs=in_specs or [VMEM] * len(inputs),
         out_specs=[VMEM] * len(shapes),
-        scratch_shapes=[pltpu.VMEM(s, jnp.float32) for s in scratch],
-        compiler_params=pltpu.CompilerParams(vmem_limit_bytes=58 * 1024 * 1024),
+        scratch_shapes=[pltpu.VMEM(s, jnp.float32) for s in scratch] + list(extra),
+        compiler_params=pltpu.CompilerParams(vmem_limit_bytes=grant * 1024 * 1024),
         name=name,
     )(*inputs)
 
@@ -305,37 +343,36 @@
 def shards(phases, mobility, active, variants):
     count = lax.axis_size("space")
     slab = lax.axis_index("slab")
-    upward = [(i, i + 1) for i in range(count - 1)]
-    downward = [(b, a) for a, b in upward]
-    swap = [(0, 1), (1, 0)]
+
+    def pairs(first):
+        forward = [(i, i + 1) for i in range(first, count - 1, 2)]
+        return forward + [(b, a) for a, b in forward]
+
+    def exchange(to_near, to_far):
+        return lax.ppermute(to_near, "space", pairs(0)), lax.ppermute(to_far, "space", pairs(1))
+
+    def swap(array):
+        return lax.ppermute(array, "slab", [(0, 1), (1, 0)])
 
     ph = jnp.transpose(phases, (1, 2, 0, 3))
-    flags = jnp.repeat(active[0, 0].astype(jnp.float32).T, B, axis=1)
-    speed = mobility[:, None] * flags
-
-    def edge(array, start):
-        return lax.dynamic_slice_in_dim(array, start, H, axis=1).reshape(-1, F, K)
-
+    to_near, to_far, to_other = call(
+        pack_kernel,
+        [(H * B + 1, F, K)] * 3,
+        [ph, mobility[None], active[0, 0]],
+        name="pack",
+        in_specs=[pl.BlockSpec(memory_space=pl.ANY), VMEM, VMEM],
+        extra=[pltpu.SemaphoreType.DMA((2 * H + B,))],
+    )
     start = (B - H) * (1 - slab)
-    low = lax.ppermute(
-        jnp.concatenate([ph[B - H :].reshape(H * B, F, K), speed[None]]), "space", upward
-    )
-    high = lax.ppermute(
-        jnp.concatenate([ph[:H].reshape(H * B, F, K), speed[None]]), "space", downward
-    )
-    across = lax.ppermute(jnp.concatenate([edge(ph, start), speed[None]]), "slab", swap)
-    corner = lax.ppermute(
-        jnp.concatenate(
-            [
-                edge(low[: H * B].reshape(H, B, F, K), start),
-                low[H * B :],
-                edge(high[: H * B].reshape(H, B, F, K), start),
-                high[H * B :],
-            ]
-        ),
-        "slab",
-        swap,
-    )
+
+    def corner(halo):
+        part = halo[: H * B].reshape(H, B, F, K)
+        part = lax.dynamic_slice_in_dim(part, start, H, axis=1).reshape(H * H, F, K)
+        return jnp.concatenate([part, halo[H * B :]])
+
+    across = swap(to_other)
+    near, far = exchange(to_near, to_far)
+    c_near, c_far = swap(corner(near)), swap(corner(far))
 
     by_field = jnp.concatenate([variants.T[:1], jnp.zeros((1, F)), variants.T[1:]])
     table = jnp.stack(
@@ -349,28 +386,33 @@
 
     block = (B + 2 * H, W + 2, F, K)
     message = (4 * B * ITERS + 16, K)
-    evolved, coef, down, up = call(
+    evolved, coef, to_near, to_far = call(
         relax_kernel,
         [(B, B, F, K), (B, 4 * B, K), message, message],
-        [ph, low, high, across, corner, speed, mix],
+        [ph, to_other, near, far, across, c_near, c_far, mix],
         [block, block, (3, 2, F, K)],
         name="relax",
-    )
-    low = lax.ppermute(up, "space", upward)
-    high = lax.ppermute(down, "space", downward)
-    o_coef = lax.ppermute(coef, "slab", swap)
-    both = lax.ppermute(jnp.stack([low, high]), "slab", swap)
+        grant=20,
+    )
+    o_coef = swap(coef)
+    near, far = exchange(to_near, to_far)
+    o_near, o_far = swap(near), swap(far)
     J, N = 2 * B, B + 2 * GO
     (packed,) = call(
         solve_kernel,
-        [(K // 3 * B, 128)],
-        [coef, low, high, o_coef, both[0], both[1]],
-        [(N, J, K)] * 10 + [(3, N, J, K)] * 3 + [(3, B, J, K), (128, K)],
+        [(K // 3, B, 128)],
+        [coef, near, far, o_coef, o_near, o_far],
+        [(N, J, K)] * 10 + [(3, N, J, K)] * 3 + [(3, B, J, K), (128, K), (K // 3 * B, 128)],
         name="solve",
-    )
-    arrived = lax.all_to_all(packed.reshape(count, 1, B * 128), "space", 0, 0, tiled=True)
+        grant=28,
+    )
+    arrived = lax.all_to_all(packed, "space", 0, 0, tiled=True)
     (displacement,) = call(
-        unpack_kernel, [(3, K // count, B, count * B)], [arrived.reshape(count * B, 128)], name="unpack"
+        unpack_kernel,
+        [(3, K // count, B, count * B)],
+        [arrived],
+        [(count * B, 128)],
+        name="unpack",
     )
     return jnp.transpose(evolved, (2, 0, 1, 3)), displacement
 

time: 135 us -> 125 us (0.926)
  waiting for transfers between devices: 20.6 us -> 15.9 us
  blocking collectives: 50 us -> 53.1 us
  starting transfers between devices: 16.6 us -> 13.6 us
  local copies, waits for them, and re-layouts: 7.17 us -> 4.63 us
  Pallas kernels: 37 us -> 34.6 us
    ppermute x8 -> x10, waiting for transfers between devices: 20.6 us -> 15.9 us  [the longest x2 14.2 us: exchange(): lax.ppermute(to_near, 'space', pairs(0))]
    all_to_all x1, blocking collectives: 50 us -> 53.1 us  [shards(): arrived = lax.all_to_all(packed, 'space', 0, 0, tiled=True)]
    ppermute x8 -> x10, starting transfers between devices: 16.6 us -> 13.6 us  [the longest x2 7.86 us: exchange(): lax.ppermute(to_near, 'space', pairs(0))]
    pallas_call x3 -> x4, Pallas kernels: 37 us -> 34.6 us  [call(): pl.pallas_call(kernel, out_shape=[jax.ShapeDtypeStruct(s, jnp.float32) fo...]
    unnamed x18 -> x9, local copies, waits for them, and re-layouts: 2.4 us -> 2.91 us
  transfers between devices with their start and end apart: 8 -> 10, of which waited for: 6 -> 4; matrix products, arithmetic and copies ran while one was open for 2% -> 3% of each run, Pallas kernels for 0% -> 0%
where the time goes in v2:
time: 125 us
  blocking collectives  53.1 us (42%)
  Pallas kernels  34.6 us (28%)
  waiting for transfers between devices  15.9 us (13%)
  starting transfers between devices  13.6 us (11%)
  local copies, waits for them, and re-layouts  4.63 us (4%)
  other arithmetic  2.47 us (2%)
    all_to_all x1, blocking collectives, shards(): arrived = lax.all_to_all(packed, 'space', 0, 0, tiled=True)  53.1 us
    pallas_call x4, Pallas kernels, call(): pl.pallas_call(kernel, out_shape=[jax.ShapeDtypeStruct(s, jnp.float32) fo...  34.6 us
    ppermute x2, waiting for transfers between devices, exchange(): lax.ppermute(to_near, 'space', pairs(0))  14.2 us
    ppermute x2, starting transfers between devices, exchange(): lax.ppermute(to_near, 'space', pairs(0))  7.86 us
    ppermute x6, starting transfers between devices, swap(): return lax.ppermute(array, 'slab', [(0, 1), (1, 0)])  4.41 us
    unnamed x9, local copies, waits for them, and re-layouts  2.91 us
  transfers between devices with their start and end apart: 10, of which 4 were waited for; matrix products, arithmetic and copies ran while one was open for 3% of the time, Pallas kernels for 0%

profile of v2, /device:TPU:1, one launch (start us, length us, event | category | flops | bytes accessed | tf_op | source)
XLA Modules:
  0.0 125.1 jit_solution(12003730388413495046)
XLA Ops:
  0.6 0.8 copy.7
  1.4 1.5 %copy-done = f32[8,12,12,384]{3,0,2,1:T(8,128)S(1)} copy-done((f32[8,12,12,384]{3,0,2,1:T(8,128)S(1)}, f32[8,12,12,384]{3,0,2,1:T(8,128)}, u32[]{:S(2)}) %copy-start) | copy-done | bytes 1769496
  2.9 0.7 copy-done.2
  3.5 2.9 %pack.1 = (f32[37,8,384]{2,1,0:T(8,128)S(1)}, f32[37,8,384]{2,1,0:T(8,128)}, f32[37,8,384]{2,1,0:T(8,128)S(1)}) custom-call(f32[12,12,8,384]{3,2,1,0:T(8,128)S(1)} %bitcast.15, f32[1,8]{1,0:T(1,128)S(1)} %bitcast.18, s32[32,8]{1,0:T(8,128)S(1)} %bitcast.17), custom_call_target="tpu_custom_call" | custom-call | tf_op jit(solution)/shard_map/pack/pallas_call | solution.py:332
  6.4 2.5 %collective-permute-start = (f32[37,8,384]{2,1,0:T(8,128)S(1)}, f32[37,8,384]{2,1,0:T(8,128)S(1)}, u32[]{:S(2)}, u32[]{:S(2)}) collective-permute-start(f32[37,8,384]{2,1,0:T(8,128)S(1)} %get-tuple-element.10), channel_id=1, source_target_pairs={{0,2},{4,6},{8,10},{12,14},{16,18},{20,22},{24,26},{28,30},{32,34}... | collective-permute-start | bytes 1363976 | tf_op jit(solution)/shard_map/ppermute | solution.py:352
  8.9 0.7 collective-permute-start.1
  9.6 1.0 collective-permute-start.2
  10.7 0.1 pad.4.clone
  10.8 0.1 maximum_bitcast_fusion
  10.9 0.1 pad_maximum_fusion.2
  10.9 0.1 copy.8
  11.1 7.0 %collective-permute-done.near = f32[37,8,384]{2,1,0:T(8,128)S(1)} collective-permute-done((f32[37,8,384]{2,1,0:T(8,128)S(1)}, f32[37,8,384]{2,1,0:T(8,128)S(1)}, u32[]{:S(2)}, u32[]{:S(2)}) %collective-permute-start) | collective-permute-done | bytes 454688 | tf_op jit(solution)/shard_map/ppermute | solution.py:352
  18.1 0.0 copy-start.1
  18.2 0.7 pad_maximum_fusion
  18.9 2.3 %collective-permute-start.3 = (f32[10,8,384]{2,1,0:T(8,128)}, f32[10,8,384]{2,1,0:T(8,128)S(1)}, u32[]{:S(2)}, u32[]{:S(2)}) collective-permute-start(f32[10,8,384]{2,1,0:T(8,128)} %pad_maximum_fusion), channel_id=1, source_target_pairs={{0,1},{1,0},{2,3},{3,2},{4,5},{5,4},{6,7},{7,6},{8,9},{9,8},{10,11... | collective-permute-start | bytes 368648 | tf_op jit(solution)/shard_map/ppermute | solution.py:355
  21.1 0.7 pad_maximum_fusion.1
  21.8 0.0 collective-permute-start.4
  21.8 1.0 broadcast_multiply_fusion
  22.8 1.4 %mul.20 = f32[144,96]{0,1:T(8,128)S(1)} reshape(f32[3,4,12,12,8]{2,1,0,4,3:T(4,128)} %broadcast_multiply_fusion) | data formatting | bytes 110592 | tf_op jit(solution)/shard_map/mul | solution.py:385
  24.1 0.1 copy.9.mix
  24.3 13.3 %relax.1 = (f32[12,12,8,384]{3,2,1,0:T(8,128)}, f32[12,48,384]{2,1,0:T(8,128)S(1)}, f32[208,384]{1,0:T(8,128)S(1)}, f32[208,384]{1,0:T(8,128)S(1)}) custom-call(f32[12,12,8,384]{3,2,1,0:T(8,128)S(1)} %bitcast.16, f32[37,8,384]{2,1,0:T(8,128)S(1)} %get-tuple-element.9.mine, f32[37,8,384]{2,1,0:T(8,128)S(1)} %collective-permute-done.near, ...), custom_call_target="tpu_custom_call" | custom-call | tf_op jit(solution)/shard_map/relax/pallas_call | solution.py:332
  37.5 0.5 collective-permute-start.7
  38.0 5.3 %collective-permute-start.5 = (f32[208,384]{1,0:T(8,128)S(1)}, f32[208,384]{1,0:T(8,128)S(1)}, u32[]{:S(2)}, u32[]{:S(2)}) collective-permute-start(f32[208,384]{1,0:T(8,128)S(1)} %get-tuple-element.14), channel_id=1, source_target_pairs={{0,2},{4,6},{8,10},{12,14},{16,18},{20,22},{24,26},{28,30},{32,34}... | collective-permute-start | bytes 958472 | tf_op jit(solution)/shard_map/ppermute | solution.py:352
  43.4 0.7 collective-permute-start.6
  44.0 7.2 %collective-permute-done.5.near = f32[208,384]{1,0:T(8,128)S(1)} collective-permute-done((f32[208,384]{1,0:T(8,128)S(1)}, f32[208,384]{1,0:T(8,128)S(1)}, u32[]{:S(2)}, u32[]{:S(2)}) %collective-permute-start.5) | collective-permute-done | bytes 319520 | tf_op jit(solution)/shard_map/ppermute | solution.py:352
  51.3 0.6 collective-permute-start.8
  51.9 0.0 collective-permute-start.9
  51.9 1.2 collective-permute-done.8.o_near
  53.1 0.5 collective-permute-done.9.o_far
  53.6 17.3 %solve.1 = f32[128,12,128]{2,1,0:T(8,128)S(1)} custom-call(f32[12,48,384]{2,1,0:T(8,128)S(1)} %get-tuple-element.13.coef, f32[208,384]{1,0:T(8,128)S(1)} %collective-permute-done.5.near, f32[208,384]{1,0:T(8,128)S(1)} %collective-permute-done.6.far, f32[12,48,384]{2,1,0:T(8,128)S(1)} %collective-permute-done.7.o_coef, ...), custom_call_target="tpu_custom_call" | custom-call | tf_op jit(solution)/shard_map/solve/pallas_call | solution.py:332
  70.9 53.1 %all_to_all.5.got = f32[128,12,128]{2,1,0:T(8,128)S(1)} all-to-all(f32[128,12,128]{2,1,0:T(8,128)S(1)} %solve.1), channel_id=1, replica_groups=mesh['space'=128,'slab'=2] {'space'}, dimensions={0} | all-to-all | bytes 1572864 | tf_op jit(solution)/shard_map/all_to_all | solution.py:409
  124.0 1.2 unpack.1
  (22 shorter events, 0.2 us)
Async XLA Ops:
  0.6 10.0 %copy-start.3 = (f32[8,3]{0,1:T(4,128)S(1)}, f32[8,3]{0,1:T(4,128)}, u32[]{:S(2)}) copy-start(f32[8,3]{0,1:T(4,128)} %param.7) | copy-start | bytes 292
  1.4 1.5 %copy-start = (f32[8,12,12,384]{3,0,2,1:T(8,128)S(1)}, f32[8,12,12,384]{3,0,2,1:T(8,128)}, u32[]{:S(2)}) copy-start(f32[8,12,12,384]{3,0,2,1:T(8,128)} %param.4) | copy-start | bytes 5308420
  2.9 0.7 copy-start.2
  6.4 11.7 %collective-permute-start = (f32[37,8,384]{2,1,0:T(8,128)S(1)}, f32[37,8,384]{2,1,0:T(8,128)S(1)}, u32[]{:S(2)}, u32[]{:S(2)}) collective-permute-start(f32[37,8,384]{2,1,0:T(8,128)S(1)} %get-tuple-element.10), channel_id=1, source_target_pairs={{0,2},{4,6},{8,10},{12,14},{16,18},{20,22},{24,26},{28,30},{32,34}... | collective-permute-start | bytes 1363976 | tf_op jit(solution)/shard_map/ppermute | solution.py:352
  8.9 9.2 %collective-permute-start.1 = (f32[37,8,384]{2,1,0:T(8,128)}, f32[37,8,384]{2,1,0:T(8,128)S(1)}, u32[]{:S(2)}, u32[]{:S(2)}) collective-permute-start(f32[37,8,384]{2,1,0:T(8,128)} %get-tuple-element.11), channel_id=1, source_target_pairs={{2,4},{6,8},{10,12},{14,16},{18,20},{22,24},{26,28},{30,32},{34,36... | collective-permute-start | bytes 1363976 | tf_op jit(solution)/shard_map/ppermute | solution.py:352
  9.6 14.6 %collective-permute-start.2 = (f32[37,8,384]{2,1,0:T(8,128)S(1)}, f32[37,8,384]{2,1,0:T(8,128)}, u32[]{:S(2)}, u32[]{:S(2)}) collective-permute-start(f32[37,8,384]{2,1,0:T(8,128)S(1)} %get-tuple-element.9.mine), channel_id=1, source_target_pairs={{0,1},{1,0},{2,3},{3,2},{4,5},{5,4},{6,7},{7,6},{8,9},{9,8},{10,11... | collective-permute-start | bytes 1363976 | tf_op jit(solution)/shard_map/ppermute | solution.py:355
  18.1 6.2 %copy-start.1 = (f32[8,12,12,384]{3,0,2,1:T(8,128)S(1)}, f32[8,12,12,384]{3,0,2,1:T(8,128)}, u32[]{:S(2)}) copy-start(f32[8,12,12,384]{3,0,2,1:T(8,128)} %param.4) | copy-start | bytes 5308420
  18.9 5.4 %collective-permute-start.3 = (f32[10,8,384]{2,1,0:T(8,128)}, f32[10,8,384]{2,1,0:T(8,128)S(1)}, u32[]{:S(2)}, u32[]{:S(2)}) collective-permute-start(f32[10,8,384]{2,1,0:T(8,128)} %pad_maximum_fusion), channel_id=1, source_target_pairs={{0,1},{1,0},{2,3},{3,2},{4,5},{5,4},{6,7},{7,6},{8,9},{9,8},{10,11... | collective-permute-start | bytes 368648 | tf_op jit(solution)/shard_map/ppermute | solution.py:355
  21.8 2.5 %collective-permute-start.4 = (f32[10,8,384]{2,1,0:T(8,128)}, f32[10,8,384]{2,1,0:T(8,128)S(1)}, u32[]{:S(2)}, u32[]{:S(2)}) collective-permute-start(f32[10,8,384]{2,1,0:T(8,128)} %pad_maximum_fusion.1), channel_id=1, source_target_pairs={{0,1},{1,0},{2,3},{3,2},{4,5},{5,4},{6,7},{7,6},{8,9},{9,8},{10,11... | collective-permute-start | bytes 368648 | tf_op jit(solution)/shard_map/ppermute | solution.py:355
  37.5 16.0 %collective-permute-start.7 = (f32[12,48,384]{2,1,0:T(8,128)S(1)}, f32[12,48,384]{2,1,0:T(8,128)S(1)}, u32[]{:S(2)}, u32[]{:S(2)}) collective-permute-start(f32[12,48,384]{2,1,0:T(8,128)S(1)} %get-tuple-element.13.coef), channel_id=1, source_target_pairs={{0,1},{1,0},{2,3},{3,2},{4,5},{5,4},{6,7},{7,6},{8,9},{9,8},{10,11... | collective-permute-start | bytes 2654216 | tf_op jit(solution)/shard_map/ppermute | solution.py:355
  38.0 13.2 %collective-permute-start.5 = (f32[208,384]{1,0:T(8,128)S(1)}, f32[208,384]{1,0:T(8,128)S(1)}, u32[]{:S(2)}, u32[]{:S(2)}) collective-permute-start(f32[208,384]{1,0:T(8,128)S(1)} %get-tuple-element.14), channel_id=1, source_target_pairs={{0,2},{4,6},{8,10},{12,14},{16,18},{20,22},{24,26},{28,30},{32,34}... | collective-permute-start | bytes 958472 | tf_op jit(solution)/shard_map/ppermute | solution.py:352
  43.4 8.5 %collective-permute-start.6 = (f32[208,384]{1,0:T(8,128)S(1)}, f32[208,384]{1,0:T(8,128)S(1)}, u32[]{:S(2)}, u32[]{:S(2)}) collective-permute-start(f32[208,384]{1,0:T(8,128)S(1)} %get-tuple-element.15), channel_id=1, source_target_pairs={{2,4},{6,8},{10,12},{14,16},{18,20},{22,24},{26,28},{30,32},{34,36... | collective-permute-start | bytes 958472 | tf_op jit(solution)/shard_map/ppermute | solution.py:352
  51.3 1.8 %collective-permute-start.8 = (f32[208,384]{1,0:T(8,128)S(1)}, f32[208,384]{1,0:T(8,128)S(1)}, u32[]{:S(2)}, u32[]{:S(2)}) collective-permute-start(f32[208,384]{1,0:T(8,128)S(1)} %collective-permute-done.5.near), channel_id=1, source_target_pairs={{0,1},{1,0},{2,3},{3,2},{4,5},{5,4},{6,7},{7,6},{8,9},{9,8},{10,11... | collective-permute-start | bytes 958472 | tf_op jit(solution)/shard_map/ppermute | solution.py:355
  51.9 1.7 %collective-permute-start.9 = (f32[208,384]{1,0:T(8,128)S(1)}, f32[208,384]{1,0:T(8,128)S(1)}, u32[]{:S(2)}, u32[]{:S(2)}) collective-permute-start(f32[208,384]{1,0:T(8,128)S(1)} %collective-permute-done.6.far), channel_id=1, source_target_pairs={{0,1},{1,0},{2,3},{3,2},{4,5},{5,4},{6,7},{7,6},{8,9},{9,8},{10,11... | collective-permute-start | bytes 958472 | tf_op jit(solution)/shard_map/ppermute | solution.py:355

commit v3 on v2

v3 whole, which is shorter than its diff:
```python
import jax
import jax.numpy as jnp
from jax import lax
from jax.experimental import pallas as pl
from jax.experimental.pallas import tpu as pltpu
from jax.sharding import PartitionSpec as P


ITERS = 4
DIAGONAL_SHIFT = 3.0
SPECTRUM_CENTRE = 12.0
SPECTRUM_RADIUS = 9.0

B = 12
F = 8
K = 384
H = 3
W = B + H
GO = ITERS + 1
HIGHEST = lax.Precision.HIGHEST
VMEM = pl.BlockSpec(memory_space=pltpu.VMEM)
HBM = pl.BlockSpec(memory_space=pltpu.HBM)


def roll(x, shift, axis):
    return pltpu.roll(x, shift % x.shape[axis], axis)


def parity():
    even = 1 - lax.axis_index("space") % 2
    return even, 1 - even


def pack_kernel(ph, mobility, active, to_near, to_far, to_other, sems):
    even, odd = parity()
    start = (B - H) * (1 - lax.axis_index("slab"))
    copies = []
    for t in range(H):
        for message, top in ((to_far, odd), (to_near, even)):
            source = ph.at[(B - H) * top + t]
            copies.append((source, message.at[pl.ds(B * t, B)]))
    for i in range(B):
        copies.append((ph.at[i, pl.ds(start, H)], to_other.at[pl.ds(H * i, H)]))
    copies = [pltpu.make_async_copy(a, b, sems.at[n]) for n, (a, b) in enumerate(copies)]
    for copy in copies:
        copy.start()
    bricks = K // B
    brick = lax.broadcasted_iota(jnp.int32, (bricks, K), 0)
    spread = jnp.where(brick == lax.broadcasted_iota(jnp.int32, (bricks, K), 1) // B, 1.0, 0.0)
    flags = jnp.dot(
        active[...].astype(jnp.float32), spread, preferred_element_type=jnp.float32
    )
    field = lax.broadcasted_iota(jnp.int32, (F, F), 0)
    rates = jnp.where(field == lax.broadcasted_iota(jnp.int32, (F, F), 1), mobility[...], 0.0)
    speed = flags * jnp.sum(rates, axis=1, keepdims=True)
    for message in (to_near, to_far, to_other):
        message[H * B] = speed
    for copy in copies:
        copy.wait()


def update(x, around, s):
    lane = lax.broadcasted_iota(jnp.int32, (F, K), 1)
    square = x * x
    total = square + roll(square, 4, 0)
    total = total + roll(total, 2, 0)
    total = total + roll(total, 1, 0)
    left = jnp.where(lane == 0, 0.0, roll(x, 1, 1))
    right = jnp.where(lane == K - 1, 0.0, roll(x, -1, 1))
    summed = around + (left + right)
    return x - s * (x * (5.0 + 3.0 * total - 2.0 * square) - summed)


def window_step(src, dst, speed, count, place):
    slab = lax.axis_index("slab")

    def plane(n, _):
        a = place(n)
        group = (a >= H).astype(jnp.int32) + (a >= H + B).astype(jnp.int32)
        before = src[a, 0]
        x = src[a, 1]
        for w in range(W):
            after = src[a, w + 2]
            whose = slab if w < H else (1 - slab if w >= B else 0)
            around = (before + after) + (src[a - 1, w + 1] + src[a + 1, w + 1])
            dst[a, w + 1] = update(x, around, speed[group, whose])
            before, x = x, after
        return 0

    lax.fori_loop(0, count, plane, 0)


def halves(x):
    high = x.astype(jnp.bfloat16)
    return high, (x - high.astype(jnp.float32)).astype(jnp.bfloat16)


def last_step(src, own_speed, mix, ev, coef, count, place, staged, sems):
    own = 1 + H * lax.axis_index("slab")
    row = lax.broadcasted_iota(jnp.int32, (4 * B, K), 0)
    is_excess = (row >= B) & (row < 2 * B)

    def plane(n, _):
        a = place(n)
        i = a - H
        before = src[a, own - 1]
        x = src[a, own]
        squares = []
        for j in range(B):
            after = src[a, own + j + 1]
            around = (before + after) + (src[a - 1, own + j] + src[a + 1, own + j])
            value = update(x, around, own_speed[...])
            staged[n, j] = value
            squares.append(value * value)
            before, x = x, after
        pltpu.make_async_copy(staged.at[n], ev.at[i], sems.at[n]).start()
        high, low = halves(jnp.concatenate(squares, 0))
        mixed = jnp.dot(
            mix[...],
            jnp.concatenate([high, low, high], 0),
            preferred_element_type=jnp.float32,
        )
        total = mixed[: 4 * B]
        strain = mixed[4 * B : 8 * B]
        dilation = mixed[8 * B :]
        saturation = total / (1.0 + total)
        excess = 0.5 * saturation
        stress = (1.5 + saturation) * dilation + 2.0 * (1.0 + excess) * strain
        coef[i] = jnp.where(is_excess, excess, stress)
        return 0

    lax.fori_loop(0, count, plane, 0)

    def settle(n, _):
        pltpu.make_async_copy(staged.at[n], ev.at[place(n) - H], sems.at[n]).wait()
        return 0

    lax.fori_loop(0, count, settle, 0)


def relax_inner_kernel(
    ph, mine, across, variants, first, second, ev, coef, mix, speed, staged, sems
):
    slab = lax.axis_index("slab")
    own = 1 + H * slab
    other = 1 + B * (1 - slab)
    zero = jnp.zeros((F, K), jnp.float32)
    speed[1, 0] = mine[H * B]
    speed[1, 1] = across[H * B]

    v = variants[...]
    each = jnp.concatenate([v[:1], jnp.zeros((1, F)), v[1:]], 0)
    whole = jnp.broadcast_to(v[:1] + v[1:2] + v[2:], (4, F))
    table = jnp.concatenate([jnp.ones((4, F)), each, whole], 0)
    shape = (12 * B, B * F)
    group = lax.broadcasted_iota(jnp.int32, (12 * B, 12), 0) // B
    down = jnp.where(group == lax.broadcasted_iota(jnp.int32, (12 * B, 12), 1), 1.0, 0.0)
    field = lax.broadcasted_iota(jnp.int32, (F, B * F), 1) % F
    along = jnp.where(field == lax.broadcasted_iota(jnp.int32, (F, B * F), 0), 1.0, 0.0)
    table = jnp.dot(down, table, precision=HIGHEST, preferred_element_type=jnp.float32)
    table = jnp.dot(table, along, precision=HIGHEST, preferred_element_type=jnp.float32)
    same = lax.broadcasted_iota(jnp.int32, shape, 0) % B
    same = same == lax.broadcasted_iota(jnp.int32, shape, 1) // F
    high, low = halves(jnp.where(same, table, 0.0))
    mix[...] = jnp.concatenate([high, high, low], 1)

    def clear(a, _):
        for buf in (first, second):
            buf[a, 0] = zero
            buf[a, W + 1] = zero
        return 0

    lax.fori_loop(0, B + 2 * H, clear, 0)

    def fill(i, _):
        for j in range(B):
            first[H + i, own + j] = ph[i, j]
        for t in range(H):
            first[H + i, other + t] = across[H * i + t]
        return 0

    lax.fori_loop(0, B, fill, 0)
    window_step(first, second, speed, B - 2, lambda n: H + 1 + n)
    window_step(second, first, speed, B - 4, lambda n: H + 2 + n)
    last_step(first, speed.at[1, 0], mix, ev, coef, B - 6, lambda n: H + 3 + n, staged, sems)


def relax_outer_kernel(
    near, far, c_near, c_far, mine, across, mix, first_in, second_in, ev_in, coef_in,
    first, second, ev, coef, m_near, m_far, speed, staged, sems,
):
    even, odd = parity()
    slab = lax.axis_index("slab")
    own = 1 + H * slab
    other = 1 + B * (1 - slab)
    speed[1, 0] = mine[H * B]
    speed[1, 1] = across[H * B]
    for halo, corner, top in ((near, c_near, even), (far, c_far, odd)):
        speed[2 * top, 0] = halo[H * B]
        speed[2 * top, 1] = corner[H * B]
        for a in range(H):
            for j in range(B):
                first[(H + B) * top + a, own + j] = halo[B * a + j]
            for t in range(H):
                first[(H + B) * top + a, other + t] = corner[B * a + (B - H) * slab + t]

    def ends(depth):
        jump = B + H - 2 * depth - 1
        return lambda n: depth + n + jnp.where(n >= H, jump + 1 - H, 0)

    window_step(first, second, speed, 2 * H, ends(1))
    window_step(second, first, speed, 2 * H, ends(2))
    last_step(first, speed.at[1, 0], mix, ev, coef, 2 * H, ends(3), staged, sems)
    for message, top in ((m_near, even), (m_far, odd)):
        for t in range(ITERS):
            message[4 * B * t : 4 * B * (t + 1)] = coef[(B - ITERS) * top + t]
        message[4 * B * ITERS :] = coef[ITERS + (B - 2 * ITERS - 1) * top, :16]


J = 2 * B
N = B + 2 * GO


def ratios():
    ratio = SPECTRUM_RADIUS / SPECTRUM_CENTRE
    out = []
    for _ in range(ITERS):
        ratio_next = 1.0 / (2.0 * SPECTRUM_CENTRE / SPECTRUM_RADIUS - ratio)
        out.append((ratio_next * ratio, 2.0 * ratio_next / SPECTRUM_RADIUS))
        ratio = ratio_next
    return out


def joined(mine, others):
    bottom = lax.axis_index("slab") == 0
    lo = jnp.where(bottom, mine, others)
    hi = jnp.where(bottom, others, mine)
    n = mine.shape[0] // B
    return [jnp.concatenate([lo[B * c : B * c + B], hi[B * c : B * c + B]], 0) for c in range(n)]


class Solver:
    def __init__(self, state):
        self.s0, self.s1, self.s2, self.ex = state[:4]
        self.dia, self.wi, self.wjp, self.wjm, self.wkp, self.wkm = state[4:10]
        self.even, self.odd, self.res, self.sol = state[10:]
        self.row = lax.broadcasted_iota(jnp.int32, (J, K), 0)
        self.lane = lax.broadcasted_iota(jnp.int32, (J, K), 1)

    def put(self, a, mine, others):
        self.s0[a], self.ex[a], self.s1[a], self.s2[a] = joined(mine, others)

    def next_j(self, x):
        return jnp.where(self.row == J - 1, 0.0, roll(x, -1, 0))

    def last_j(self, x):
        return jnp.where(self.row == 0, 0.0, roll(x, 1, 0))

    def next_k(self, x):
        return jnp.where(self.lane == K - 1, 0.0, roll(x, -1, 1))

    def last_k(self, x):
        return jnp.where(self.lane == 0, 0.0, roll(x, 1, 1))

    def force(self, a):
        forcing = (
            0.5 * (self.s0[a + 1] - self.s0[a - 1]),
            0.5 * (self.next_j(self.s1[a]) - self.last_j(self.s1[a])),
            0.5 * (self.next_k(self.s2[a]) - self.last_k(self.s2[a])),
        )
        for c in range(3):
            self.even[c, a] = forcing[c] / SPECTRUM_CENTRE
            self.res[c, a] = forcing[c]

    def weigh(self, a):
        e = self.ex[a]
        i_next = 1.0 + 0.5 * (e + self.ex[a + 1])
        i_last = 1.0 + 0.5 * (e + self.ex[a - 1])
        j_next = 1.0 + 0.5 * (e + self.next_j(e))
        j_last = 1.0 + 0.5 * (e + self.last_j(e))
        k_next = 1.0 + 0.5 * (e + self.next_k(e))
        k_last = 1.0 + 0.5 * (e + self.last_k(e))
        ends = (i_next + i_last) + (j_next + j_last) + (k_next + k_last)
        self.dia[a] = DIAGONAL_SHIFT + ends
        self.wi[a] = i_next
        self.wjp[a] = jnp.where(self.row == J - 1, 0.0, j_next)
        self.wjm[a] = jnp.where(self.row == 0, 0.0, j_last)
        self.wkp[a] = jnp.where(self.lane == K - 1, 0.0, k_next)
        self.wkm[a] = jnp.where(self.lane == 0, 0.0, k_last)

    def apply(self, src, c, a):
        v = src[c, a]
        r = self.res[c, a] - self.dia[a] * v
        r = r + self.wi[a] * src[c, a + 1]
        r = r + self.wi[a - 1] * src[c, a - 1]
        r = r + self.wjp[a] * roll(v, -1, 0)
        r = r + self.wjm[a] * roll(v, 1, 0)
        r = r + self.wkp[a] * roll(v, -1, 1)
        r = r + self.wkm[a] * roll(v, 1, 1)
        return v, r

    def buffers(self, t):
        return (self.even, self.odd) if t % 2 == 0 else (self.odd, self.even)

    def iterate(self, t, start, stop):
        keep, gain = ratios()[t]
        src, dst = self.buffers(t)

        def plane(a, inner):
            for c in range(3):
                v, r = self.apply(src, c, a)
                self.res[c, a] = r
                dst[c, a] = keep * v + gain * r
                if inner:
                    self.sol[c, a - GO] = v if t == 0 else self.sol[c, a - GO] + v

        low, high = min(max(start, GO), stop), max(min(stop, GO + B), start)
        loop(start, low, lambda a: plane(a, False))
        loop(low, high, lambda a: plane(a, True))
        loop(high, stop, lambda a: plane(a, False))


def loop(start, stop, body):
    if start < stop:
        lax.fori_loop(start, stop, lambda a, _: (body(a), 0)[1], 0)


def solve_inner_kernel(coef, o_coef, *state):
    solver = Solver(state)
    loop(0, B, lambda i: solver.put(i + GO, coef[i], o_coef[i]))
    loop(GO + 1, GO + B - 1, solver.force)
    loop(GO + 1, GO + B - 1, solver.weigh)
    for t in range(ITERS - 1):
        solver.iterate(t, GO + 2 + t, GO + B - 2 - t)


def solve_outer_kernel(near, far, o_near, o_far, *refs):
    state = refs[14:28]
    out, rows, flat = refs[28:]
    solver = Solver(state)
    even, odd = parity()
    place = lax.axis_index("space")
    bottom = lax.axis_index("slab") == 0
    tail = slice(4 * B * ITERS, 4 * B * ITERS + 16)
    for halo, others, top in ((near, o_near, even), (far, o_far, odd)):
        for t in range(ITERS):
            part = slice(4 * B * t, 4 * B * (t + 1))
            solver.put(1 + t + (GO + B - 1) * top, halo[part], others[part])
        (solver.s0[(N - 1) * top],) = joined(halo[tail], others[tail])

    loop(1, GO + 1, solver.force)
    loop(GO + B - 1, N - 1, solver.force)
    solver.wi[1] = 1.0 + 0.5 * (solver.ex[1] + solver.ex[2])
    loop(2, GO + 1, solver.weigh)
    loop(GO + B - 1, N - 2, solver.weigh)

    @pl.when(place == 0)
    def _():
        solver.wi[GO - 1] = jnp.zeros((J, K), jnp.float32)

    @pl.when(place == lax.axis_size("space") - 1)
    def _():
        solver.wi[GO + B - 1] = jnp.zeros((J, K), jnp.float32)

    for t in range(ITERS - 1):
        solver.iterate(t, 2 + t, GO + 2 + t)
        solver.iterate(t, GO + B - 2 - t, N - 2 - t)

    keep, gain = ratios()[ITERS - 1]
    src, _ = solver.buffers(ITERS - 1)
    third = lax.broadcasted_iota(jnp.int32, (B, K), 1) % 3
    target = lax.broadcasted_iota(jnp.int32, (K // 3, K), 0)
    source = lax.broadcasted_iota(jnp.int32, (K // 3, K), 1) // 3
    pick = jnp.where(target == source, 1.0, 0.0).astype(jnp.bfloat16)
    pick = jnp.concatenate([pick, pick, pick], 1)
    rows[9 * B :] = jnp.zeros((128 - 9 * B, K), jnp.float32)

    def finish(i):
        a = i + GO
        for c in range(3):
            v, r = solver.apply(src, c, a)
            total = solver.sol[c, i] + v + (keep * v + gain * r)
            mine = jnp.where(bottom, total[:B], total[B:])
            for q in range(3):
                g = 3 * c + q
                rows[B * g : B * g + B] = jnp.where(third == q, mine, 0.0)
        value = rows[...]
        high, low = halves(value)
        rest = value - high.astype(jnp.float32) - low.astype(jnp.float32)
        flat[pl.ds(i, K // 3, stride=B), :] = lax.dot_general(
            pick,
            jnp.concatenate([high, low, rest.astype(jnp.bfloat16)], 1),
            (((1,), (1,)), ((), ())),
            preferred_element_type=jnp.float32,
        )

    loop(0, B, finish)
    for n in range(out.shape[0]):
        out[n] = flat[B * n : B * (n + 1), :]


def unpack_kernel(got, out, flat):
    for n in range(got.shape[0]):
        flat[B * n : B * (n + 1), :] = got[n]
    for t in range(flat.shape[0] // 128):
        turned = flat[128 * t : 128 * (t + 1), :].T
        for c in range(3):
            for q in range(3):
                g = 3 * c + q
                out[c, q, :, 128 * t : 128 * (t + 1)] = turned[B * g : B * g + B]


def call(kernel, shapes, inputs, scratch=(), grant=8, extra=(), aliases={}, hbm_in=(), hbm_out=()):
    return pl.pallas_call(
        kernel,
        out_shape=[
            s if hasattr(s, "dtype") else jax.ShapeDtypeStruct(s, jnp.float32) for s in shapes
        ],
        in_specs=[HBM if n in hbm_in else VMEM for n in range(len(inputs))],
        out_specs=[HBM if n in hbm_out else VMEM for n in range(len(shapes))],
        scratch_shapes=[pltpu.VMEM(s, jnp.float32) for s in scratch] + list(extra),
        input_output_aliases=aliases,
        compiler_params=pltpu.CompilerParams(vmem_limit_bytes=int(grant * 1024 * 1024)),
    )(*inputs)


def program(phases, mobility, active, variants):
    count = lax.axis_size("space")

    def pairs(first):
        forward = [(i, i + 1) for i in range(first, count - 1, 2)]
        return forward + [(b, a) for a, b in forward]

    def exchange(to_near, to_far):
        far = lax.ppermute(to_far, "space", pairs(1))
        near = lax.ppermute(to_near, "space", pairs(0))
        return near, far

    def swap(array):
        return lax.ppermute(array, "slab", [(0, 1), (1, 0)])

    ph = jnp.transpose(phases, (1, 2, 0, 3))
    to_near, to_far, to_other = call(
        pack_kernel,
        [(H * B + 1, F, K)] * 3,
        [ph, mobility[None], active[0, 0].T],
        hbm_in=(0,),
        extra=[pltpu.SemaphoreType.DMA((2 * H + B,))],
        grant=61,
    )
    across = swap(to_other)
    near, far = exchange(to_near, to_far)
    block = (B + 2 * H, W + 2, F, K)
    coefs = (B, 4 * B, K)
    first, second, evolved, coef, mix = call(
        relax_inner_kernel,
        [block, block, (B, B, F, K), coefs, jax.ShapeDtypeStruct((12 * B, 3 * B * F), jnp.bfloat16)],
        [ph, to_other, across, variants.T],
        [(3, 2, F, K), (B - 6, B, F, K)],
        grant=4,
        extra=[pltpu.SemaphoreType.DMA((B - 6,))],
        hbm_out=(2,),
    )
    message = (4 * B * ITERS + 16, K)
    first, second, evolved, coef, to_near, to_far = call(
        relax_outer_kernel,
        [block, block, (B, B, F, K), coefs, message, message],
        [near, far, swap(near), swap(far), to_other, across, mix, first, second, evolved, coef],
        [(3, 2, F, K), (2 * H, B, F, K)],
        grant=4,
        aliases={7: 0, 8: 1, 9: 2, 10: 3},
        extra=[pltpu.SemaphoreType.DMA((2 * H,))],
        hbm_in=(9,),
        hbm_out=(2,),
    )
    o_coef = swap(coef)
    near, far = exchange(to_near, to_far)
    shapes = [(N, J, K)] * 10 + [(3, N, J, K)] * 3 + [(3, B, J, K)]
    state = call(solve_inner_kernel, shapes, [coef, o_coef], grant=4)
    packed = call(
        solve_outer_kernel,
        shapes + [(K // 3, B, 128)],
        [near, far, swap(near), swap(far), *state],
        [(128, K), (K // 3 * B, 128)],
        grant=8,
        aliases={4 + n: n for n in range(14)},
    )[-1]
    arrived = lax.all_to_all(packed, "space", 0, 0, tiled=True)
    (displacement,) = call(
        unpack_kernel, [(3, K // count, B, count * B)], [arrived], [(count * B, 128)]
    )
    return jnp.transpose(evolved, (2, 0, 1, 3)), displacement


def solution(mesh):
    placed = (P(None, "space", "slab", None), P(), P("space", "slab", None, None), P())
    return jax.shard_map(
        program,
        mesh=mesh,
        in_specs=placed,
        out_specs=(P(None, "space", "slab", None), P(None, "space", "slab", None)),
        check_vma=False,
    )
```

time: 125 us -> 117 us (0.936)
  local copies, waits for them, and re-layouts: 4.63 us -> 1.7 us
  other arithmetic: 2.47 us -> 0 us
  Pallas kernels: 34.6 us -> 32.2 us
  waiting for transfers between devices: 15.9 us -> 14.6 us
    pallas_call x4 -> x6, Pallas kernels: 34.6 us -> 32.2 us  [call(): pl.pallas_call(kernel, out_shape=[s if hasattr(s, 'dtype') else jax.Shape...]
    ppermute x6, waiting for transfers between devices: 1.7 us -> 0.02 us  [swap(): return lax.ppermute(array, 'slab', [(0, 1), (1, 0)])]
    mul x2 -> x0, local copies, waits for them, and re-layouts: 1.44 us -> none  [shards(): table[:, :, None, None, :] * jnp.eye(B)[None, None, :, :, None]]
    concatenate x2 -> x0, other arithmetic: 1.31 us -> none  [corner(): return jnp.concatenate([part, halo[H * B:]])]
    unnamed x9 -> x8, local copies, waits for them, and re-layouts: 2.91 us -> 1.7 us
  transfers between devices with their start and end apart: 10 -> 10, of which waited for: 4 -> 2; matrix products, arithmetic and copies ran while one was open for 3% -> 0% of each run, Pallas kernels for 0% -> 10%
where the time goes in v3:
time: 117 us; the launch traced here: 116 us
  blocking collectives  53.8 us (46%)
  Pallas kernels  32.2 us (28%)
  waiting for transfers between devices  14.6 us (12%)
  starting transfers between devices  13.4 us (11%)
  local copies, waits for them, and re-layouts  1.7 us (1%)
    all_to_all x1, blocking collectives, program(): arrived = lax.all_to_all(packed, 'space', 0, 0, tiled=True)  53.8 us
    pallas_call x6, Pallas kernels, call(): pl.pallas_call(kernel, out_shape=[s if hasattr(s, 'dtype') else jax.Shape...  32.2 us
    ppermute x2, waiting for transfers between devices, exchange(): near = lax.ppermute(to_near, 'space', pairs(0))  14.5 us
    ppermute x2, starting transfers between devices, exchange(): near = lax.ppermute(to_near, 'space', pairs(0))  7.3 us
    ppermute x6, starting transfers between devices, swap(): return lax.ppermute(array, 'slab', [(0, 1), (1, 0)])  4.78 us
  transfers between devices with their start and end apart: 10, of which 2 were waited for; matrix products, arithmetic and copies ran while one was open for 0% of the time, Pallas kernels for 10%

profile of v3, /device:TPU:1, one launch (start us, length us, event | category | flops | bytes accessed | tf_op | source)
XLA Modules:
  0.0 116.5 jit_solution(13362831928168025558)
XLA Ops:
  0.6 0.0 copy-start
  0.6 3.3 %shard_map.59 = (f32[37,8,384]{2,1,0:T(8,128)}, f32[37,8,384]{2,1,0:T(8,128)}, f32[37,8,384]{2,1,0:T(8,128)}) custom-call(f32[12,12,8,384]{3,2,1,0:T(8,128)} %bitcast.7, f32[1,8]{1,0:T(1,128)} %bitcast.12, s32[8,32]{1,0:T(8,128)} %bitcast.11), custom_call_target="tpu_custom_call" | custom-call | tf_op jit(solution)/shard_map/pallas_call | solution.py:414
  4.0 2.5 %collective-permute-start = (f32[37,8,384]{2,1,0:T(8,128)}, f32[37,8,384]{2,1,0:T(8,128)S(1)}, u32[]{:S(2)}, u32[]{:S(2)}) collective-permute-start(f32[37,8,384]{2,1,0:T(8,128)} %get-tuple-element.29), channel_id=1, source_target_pairs={{0,2},{4,6},{8,10},{12,14},{16,18},{20,22},{24,26},{28,30},{32,34}... | collective-permute-start | bytes 1363976 | tf_op jit(solution)/shard_map/ppermute | solution.py:436
  6.5 0.7 collective-permute-start.1
  7.2 1.0 collective-permute-start.4
  8.3 7.7 %collective-permute-done.near = f32[37,8,384]{2,1,0:T(8,128)S(1)} collective-permute-done((f32[37,8,384]{2,1,0:T(8,128)}, f32[37,8,384]{2,1,0:T(8,128)S(1)}, u32[]{:S(2)}, u32[]{:S(2)}) %collective-permute-start) | collective-permute-done | bytes 454688 | tf_op jit(solution)/shard_map/ppermute | solution.py:436
  16.0 2.2 %collective-permute-start.2 = (f32[37,8,384]{2,1,0:T(8,128)S(1)}, f32[37,8,384]{2,1,0:T(8,128)S(1)}, u32[]{:S(2)}, u32[]{:S(2)}) collective-permute-start(f32[37,8,384]{2,1,0:T(8,128)S(1)} %collective-permute-done.near), channel_id=1, source_target_pairs={{0,1},{1,0},{2,3},{3,2},{4,5},{5,4},{6,7},{7,6},{8,9},{9,8},{10,11... | collective-permute-start | bytes 1363976 | tf_op jit(solution)/shard_map/ppermute | solution.py:440
  18.1 0.0 collective-permute-done.1.far
  18.1 0.0 collective-permute-start.3
  18.1 0.0 collective-permute-done.4.across
  18.1 0.0 copy-done
  18.2 0.0 copy-start.1
  18.2 1.0 copy-done.1
  19.2 0.7 copy-done.3
  19.9 6.8 %shard_map.60 = (f32[18,17,8,384]{3,2,1,0:T(8,128)S(1)}, f32[18,17,8,384]{3,2,1,0:T(8,128)S(1)}, f32[12,12,8,384]{3,2,1,0:T(8,128)}, f32[12,48,384]{2,1,0:T(8,128)S(1)}, bf16[144,288]{1,0:T(8,128)(2,1)S(1)}) custom-call(f32[12,12,8,384]{3,2,1,0:T(8,128)S(1)} %bitcast.8, f32[37,8,384]{2,1,0:T(8,128)S(1)} %copy-done.1, ...), custom_call_target="tpu_custom_call" | custom-call | tf_op jit(solution)/shard_map/pallas_call | solution.py:414
  26.6 0.0 collective-permute-done.2.c_near
  26.6 0.0 collective-permute-done.3.c_far
  26.7 5.1 %shard_map.61 = (f32[18,17,8,384]{3,2,1,0:T(8,128)S(1)}, f32[18,17,8,384]{3,2,1,0:T(8,128)S(1)}, f32[12,12,8,384]{3,2,1,0:T(8,128)}, f32[12,48,384]{2,1,0:T(8,12...) custom-call(f32[37,8,384]{2,1,0:T(8,128)S(1)} %collective-permute-do, ...), custom_call_target="tpu_custom_call", output_to_operand_aliasing={{0}: (7, {}), {1}: (8, {}), {2}: (9, {}), {3}: (10, {})} | custom-call | tf_op jit(solution)/shard_map/pallas_call | solution.py:414
  31.7 0.6 collective-permute-start.9
  32.3 4.8 %collective-permute-start.5 = (f32[208,384]{1,0:T(8,128)S(1)}, f32[208,384]{1,0:T(8,128)S(1)}, u32[]{:S(2)}, u32[]{:S(2)}) collective-permute-start(f32[208,384]{1,0:T(8,128)S(1)} %get-tuple-element.38), channel_id=1, source_target_pairs={{0,2},{4,6},{8,10},{12,14},{16,18},{20,22},{24,26},{28,30},{32,34}... | collective-permute-start | bytes 958472 | tf_op jit(solution)/shard_map/ppermute | solution.py:436
  37.1 0.7 collective-permute-start.6
  37.7 6.8 %collective-permute-done.5.near = f32[208,384]{1,0:T(8,128)S(1)} collective-permute-done((f32[208,384]{1,0:T(8,128)S(1)}, f32[208,384]{1,0:T(8,128)S(1)}, u32[]{:S(2)}, u32[]{:S(2)}) %collective-permute-start.5) | collective-permute-done | bytes 319520 | tf_op jit(solution)/shard_map/ppermute | solution.py:436
  44.6 1.0 collective-permute-start.7
  45.6 0.0 collective-permute-done.6.far
  45.6 0.0 collective-permute-start.8
  45.6 0.0 collective-permute-done.9.o_coef
  45.6 4.8 %shard_map.62 = (f32[22,24,384]{2,1,0:T(8,128)S(1)}, f32[22,24,384]{2,1,0:T(8,128)S(1)}, f32[22,24,384]{2,1,0:T(8,128)S(1)}, f32[22,24,384]{2,1,0:T(8,128)S(1)},...) custom-call(f32[12,48,384]{2,1,0:T(8,128)S(1)} %get-tuple-element.40, ...), custom_call_target="tpu_custom_call" | custom-call | tf_op jit(solution)/shard_map/pallas_call | solution.py:414
  50.4 0.0 collective-permute-done.7.o_near
  50.4 0.0 collective-permute-done.8.o_far
  50.4 11.0 %shard_map.63 = (f32[22,24,384]{2,1,0:T(8,128)S(1)}, f32[22,24,384]{2,1,0:T(8,128)S(1)}, f32[22,24,384]{2,1,0:T(8,128)S(1)}, f32[22,24,384]{2,1,0:T(8,128)S(1)},...) custom-call(f32[208,384]{1,0:T(8,128)S(1)} %collective-permute-done., ...), custom_call_target="tpu_custom_call", output_to_operand_aliasing={{0}: (4, {}), {1}: (5, {}), {2}: (6, {}), {3}: (7, {}), {4}... | custom-call | tf_op jit(solution)/shard_map/pallas_call | solution.py:414
  61.5 53.8 %all_to_all.5.got = f32[128,12,128]{2,1,0:T(8,128)S(1)} all-to-all(f32[128,12,128]{2,1,0:T(8,128)S(1)} %get-tuple-element.55), channel_id=1, replica_groups=mesh['space'=128,'slab'=2] {'space'}, dimensions={0} | all-to-all | bytes 1572864 | tf_op jit(solution)/shard_map/all_to_all | solution.py:488
  115.3 1.2 %shard_map.64 = f32[3,3,12,1536]{3,2,1,0:T(8,128)} custom-call(f32[128,12,128]{2,1,0:T(8,128)S(1)} %all_to_all.5.got), custom_call_target="tpu_custom_call" | custom-call | tf_op jit(solution)/shard_map/pallas_call | solution.py:414
  (3 shorter events, 0.0 us)
Async XLA Ops:
  0.6 17.5 %copy-start = (f32[8,12,12,384]{3,0,2,1:T(8,128)S(1)}, f32[8,12,12,384]{3,0,2,1:T(8,128)}, u32[]{:S(2)}) copy-start(f32[8,12,12,384]{3,0,2,1:T(8,128)} %param.4) | copy-start | bytes 5308420
  4.0 12.0 %collective-permute-start = (f32[37,8,384]{2,1,0:T(8,128)}, f32[37,8,384]{2,1,0:T(8,128)S(1)}, u32[]{:S(2)}, u32[]{:S(2)}) collective-permute-start(f32[37,8,384]{2,1,0:T(8,128)} %get-tuple-element.29), channel_id=1, source_target_pairs={{0,2},{4,6},{8,10},{12,14},{16,18},{20,22},{24,26},{28,30},{32,34}... | collective-permute-start | bytes 1363976 | tf_op jit(solution)/shard_map/ppermute | solution.py:436
  6.5 11.6 %collective-permute-start.1 = (f32[37,8,384]{2,1,0:T(8,128)}, f32[37,8,384]{2,1,0:T(8,128)S(1)}, u32[]{:S(2)}, u32[]{:S(2)}) collective-permute-start(f32[37,8,384]{2,1,0:T(8,128)} %get-tuple-element.30), channel_id=1, source_target_pairs={{2,4},{6,8},{10,12},{14,16},{18,20},{22,24},{26,28},{30,32},{34,36... | collective-permute-start | bytes 1363976 | tf_op jit(solution)/shard_map/ppermute | solution.py:435
  7.2 10.9 %collective-permute-start.4 = (f32[37,8,384]{2,1,0:T(8,128)}, f32[37,8,384]{2,1,0:T(8,128)S(1)}, u32[]{:S(2)}, u32[]{:S(2)}) collective-permute-start(f32[37,8,384]{2,1,0:T(8,128)} %get-tuple-element.31.mine), channel_id=1, source_target_pairs={{0,1},{1,0},{2,3},{3,2},{4,5},{5,4},{6,7},{7,6},{8,9},{9,8},{10,11... | collective-permute-start | bytes 1363976 | tf_op jit(solution)/shard_map/ppermute | solution.py:440
  16.0 10.7 %collective-permute-start.2 = (f32[37,8,384]{2,1,0:T(8,128)S(1)}, f32[37,8,384]{2,1,0:T(8,128)S(1)}, u32[]{:S(2)}, u32[]{:S(2)}) collective-permute-start(f32[37,8,384]{2,1,0:T(8,128)S(1)} %collective-permute-done.near), channel_id=1, source_target_pairs={{0,1},{1,0},{2,3},{3,2},{4,5},{5,4},{6,7},{7,6},{8,9},{9,8},{10,11... | collective-permute-start | bytes 1363976 | tf_op jit(solution)/shard_map/ppermute | solution.py:440
  18.1 8.5 %collective-permute-start.3 = (f32[37,8,384]{2,1,0:T(8,128)S(1)}, f32[37,8,384]{2,1,0:T(8,128)S(1)}, u32[]{:S(2)}, u32[]{:S(2)}) collective-permute-start(f32[37,8,384]{2,1,0:T(8,128)S(1)} %collective-permute-done.1.far), channel_id=1, source_target_pairs={{0,1},{1,0},{2,3},{3,2},{4,5},{5,4},{6,7},{7,6},{8,9},{9,8},{10,11... | collective-permute-start | bytes 1363976 | tf_op jit(solution)/shard_map/ppermute | solution.py:440
  18.2 1.0 copy-start.1
  19.2 0.7 copy-start.3
  19.9 6.8 %copy-start.2 = (f32[37,8,384]{2,1,0:T(8,128)S(1)}, f32[37,8,384]{2,1,0:T(8,128)}, u32[]{:S(2)}) copy-start(f32[37,8,384]{2,1,0:T(8,128)} %get-tuple-element.31.mine) | copy-start | bytes 1363972
  31.7 13.8 %collective-permute-start.9 = (f32[12,48,384]{2,1,0:T(8,128)S(1)}, f32[12,48,384]{2,1,0:T(8,128)S(1)}, u32[]{:S(2)}, u32[]{:S(2)}) collective-permute-start(f32[12,48,384]{2,1,0:T(8,128)S(1)} %get-tuple-element.40.coef), channel_id=1, source_target_pairs={{0,1},{1,0},{2,3},{3,2},{4,5},{5,4},{6,7},{7,6},{8,9},{9,8},{10,11... | collective-permute-start | bytes 2654216 | tf_op jit(solution)/shard_map/ppermute | solution.py:440
  32.3 12.3 %collective-permute-start.5 = (f32[208,384]{1,0:T(8,128)S(1)}, f32[208,384]{1,0:T(8,128)S(1)}, u32[]{:S(2)}, u32[]{:S(2)}) collective-permute-start(f32[208,384]{1,0:T(8,128)S(1)} %get-tuple-element.38), channel_id=1, source_target_pairs={{0,2},{4,6},{8,10},{12,14},{16,18},{20,22},{24,26},{28,30},{32,34}... | collective-permute-start | bytes 958472 | tf_op jit(solution)/shard_map/ppermute | solution.py:436
  37.1 8.5 %collective-permute-start.6 = (f32[208,384]{1,0:T(8,128)S(1)}, f32[208,384]{1,0:T(8,128)S(1)}, u32[]{:S(2)}, u32[]{:S(2)}) collective-permute-start(f32[208,384]{1,0:T(8,128)S(1)} %get-tuple-element.39), channel_id=1, source_target_pairs={{2,4},{6,8},{10,12},{14,16},{18,20},{22,24},{26,28},{30,32},{34,36... | collective-permute-start | bytes 958472 | tf_op jit(solution)/shard_map/ppermute | solution.py:435
  44.6 5.8 %collective-permute-start.7 = (f32[208,384]{1,0:T(8,128)S(1)}, f32[208,384]{1,0:T(8,128)S(1)}, u32[]{:S(2)}, u32[]{:S(2)}) collective-permute-start(f32[208,384]{1,0:T(8,128)S(1)} %collective-permute-done.5.near), channel_id=1, source_target_pairs={{0,1},{1,0},{2,3},{3,2},{4,5},{5,4},{6,7},{7,6},{8,9},{9,8},{10,11... | collective-permute-start | bytes 958472 | tf_op jit(solution)/shard_map/ppermute | solution.py:440
  45.6 4.9 %collective-permute-start.8 = (f32[208,384]{1,0:T(8,128)S(1)}, f32[208,384]{1,0:T(8,128)S(1)}, u32[]{:S(2)}, u32[]{:S(2)}) collective-permute-start(f32[208,384]{1,0:T(8,128)S(1)} %collective-permute-done.6.far), channel_id=1, source_target_pairs={{0,1},{1,0},{2,3},{3,2},{4,5},{5,4},{6,7},{7,6},{8,9},{9,8},{10,11... | collective-permute-start | bytes 958472 | tf_op jit(solution)/shard_map/ppermute | solution.py:440

commit v4 on v3

--- a/solution.py
+++ b/solution.py
@@ -16,6 +16,7 @@
 K = 384
 H = 3
 W = B + H
+REST = H * H + 1
 GO = ITERS + 1
 HIGHEST = lax.Precision.HIGHEST
 VMEM = pl.BlockSpec(memory_space=pltpu.VMEM)
@@ -31,32 +32,28 @@
     return even, 1 - even
 
 
-def pack_kernel(ph, mobility, active, to_near, to_far, to_other, sems):
+def pack_kernel(ph, rates, to_near, to_far, to_other, speed_out):
     even, odd = parity()
-    start = (B - H) * (1 - lax.axis_index("slab"))
-    copies = []
-    for t in range(H):
-        for message, top in ((to_far, odd), (to_near, even)):
+    slab = lax.axis_index("slab")
+    start = (B - H) * (1 - slab)
+    for message, top in ((to_far, odd), (to_near, even)):
+        for t in range(H):
             source = ph.at[(B - H) * top + t]
-            copies.append((source, message.at[pl.ds(B * t, B)]))
+            message[H * t : H * (t + 1)] = source[pl.ds(start, H)]
+            rest = REST + (B - H) * t
+            message[rest : rest + B - H] = source[pl.ds(H * slab, B - H)]
     for i in range(B):
-        copies.append((ph.at[i, pl.ds(start, H)], to_other.at[pl.ds(H * i, H)]))
-    copies = [pltpu.make_async_copy(a, b, sems.at[n]) for n, (a, b) in enumerate(copies)]
-    for copy in copies:
-        copy.start()
+        to_other[H * i : H * (i + 1)] = ph[i, pl.ds(start, H)]
     bricks = K // B
     brick = lax.broadcasted_iota(jnp.int32, (bricks, K), 0)
     spread = jnp.where(brick == lax.broadcasted_iota(jnp.int32, (bricks, K), 1) // B, 1.0, 0.0)
-    flags = jnp.dot(
-        active[...].astype(jnp.float32), spread, preferred_element_type=jnp.float32
+    speed = jnp.dot(
+        rates[...], spread, precision=HIGHEST, preferred_element_type=jnp.float32
     )
-    field = lax.broadcasted_iota(jnp.int32, (F, F), 0)
-    rates = jnp.where(field == lax.broadcasted_iota(jnp.int32, (F, F), 1), mobility[...], 0.0)
-    speed = flags * jnp.sum(rates, axis=1, keepdims=True)
-    for message in (to_near, to_far, to_other):
-        message[H * B] = speed
-    for copy in copies:
-        copy.wait()
+    to_near[REST - 1] = speed
+    to_far[REST - 1] = speed
+    to_other[H * B] = speed
+    speed_out[...] = speed
 
 
 def update(x, around, s):
@@ -71,19 +68,20 @@
     return x - s * (x * (5.0 + 3.0 * total - 2.0 * square) - summed)
 
 
-def window_step(src, dst, speed, count, place):
+def window_step(src, dst, speed, depth, count, place):
     slab = lax.axis_index("slab")
 
     def plane(n, _):
         a = place(n)
         group = (a >= H).astype(jnp.int32) + (a >= H + B).astype(jnp.int32)
-        before = src[a, 0]
-        x = src[a, 1]
-        for w in range(W):
-            after = src[a, w + 2]
-            whose = slab if w < H else (1 - slab if w >= B else 0)
-            around = (before + after) + (src[a - 1, w + 1] + src[a + 1, w + 1])
-            dst[a, w + 1] = update(x, around, speed[group, whose])
+        edge = depth * slab
+        before = src[a, edge]
+        x = src[a, edge + 1]
+        for w in range(W - depth):
+            after = src[a, edge + w + 2]
+            whose = slab if w < H - depth else (1 - slab if w >= B else 0)
+            around = (before + after) + (src[a - 1, edge + w + 1] + src[a + 1, edge + w + 1])
+            dst[a, edge + w + 1] = update(x, around, speed[group, whose])
             before, x = x, after
         return 0
 
@@ -145,7 +143,7 @@
     own = 1 + H * slab
     other = 1 + B * (1 - slab)
     zero = jnp.zeros((F, K), jnp.float32)
-    speed[1, 0] = mine[H * B]
+    speed[1, 0] = mine[...]
     speed[1, 1] = across[H * B]
 
     v = variants[...]
@@ -180,8 +178,8 @@
         return 0
 
     lax.fori_loop(0, B, fill, 0)
-    window_step(first, second, speed, B - 2, lambda n: H + 1 + n)
-    window_step(second, first, speed, B - 4, lambda n: H + 2 + n)
+    window_step(first, second, speed, 1, B - 2, lambda n: H + 1 + n)
+    window_step(second, first, speed, 2, B - 4, lambda n: H + 2 + n)
     last_step(first, speed.at[1, 0], mix, ev, coef, B - 6, lambda n: H + 3 + n, staged, sems)
 
 
@@ -193,23 +191,24 @@
     slab = lax.axis_index("slab")
     own = 1 + H * slab
     other = 1 + B * (1 - slab)
-    speed[1, 0] = mine[H * B]
+    speed[1, 0] = mine[...]
     speed[1, 1] = across[H * B]
     for halo, corner, top in ((near, c_near, even), (far, c_far, odd)):
-        speed[2 * top, 0] = halo[H * B]
-        speed[2 * top, 1] = corner[H * B]
+        speed[2 * top, 0] = halo[REST - 1]
+        speed[2 * top, 1] = corner[REST - 1]
         for a in range(H):
-            for j in range(B):
-                first[(H + B) * top + a, own + j] = halo[B * a + j]
             for t in range(H):
-                first[(H + B) * top + a, other + t] = corner[B * a + (B - H) * slab + t]
+                first[(H + B) * top + a, own + (B - H) * (1 - slab) + t] = halo[H * a + t]
+                first[(H + B) * top + a, other + t] = corner[H * a + t]
+            for m in range(B - H):
+                first[(H + B) * top + a, own + H * slab + m] = halo[REST + (B - H) * a + m]
 
     def ends(depth):
         jump = B + H - 2 * depth - 1
         return lambda n: depth + n + jnp.where(n >= H, jump + 1 - H, 0)
 
-    window_step(first, second, speed, 2 * H, ends(1))
-    window_step(second, first, speed, 2 * H, ends(2))
+    window_step(first, second, speed, 1, 2 * H, ends(1))
+    window_step(second, first, speed, 2, 2 * H, ends(2))
     last_step(first, speed.at[1, 0], mix, ev, coef, 2 * H, ends(3), staged, sems)
     for message, top in ((m_near, even), (m_far, odd)):
         for t in range(ITERS):
@@ -217,7 +216,7 @@
         message[4 * B * ITERS :] = coef[ITERS + (B - 2 * ITERS - 1) * top, :16]
 
 
-J = 2 * B
+J = B + ITERS
 N = B + 2 * GO
 
 
@@ -243,12 +242,17 @@
     def __init__(self, state):
         self.s0, self.s1, self.s2, self.ex = state[:4]
         self.dia, self.wi, self.wjp, self.wjm, self.wkp, self.wkm = state[4:10]
-        self.even, self.odd, self.res, self.sol = state[10:]
+        self.even, self.odd, self.sol = state[10:]
         self.row = lax.broadcasted_iota(jnp.int32, (J, K), 0)
         self.lane = lax.broadcasted_iota(jnp.int32, (J, K), 1)
 
+    def window(self, x):
+        return jnp.where(lax.axis_index("slab") == 0, x[:J], x[2 * B - J :])
+
     def put(self, a, mine, others):
-        self.s0[a], self.ex[a], self.s1[a], self.s2[a] = joined(mine, others)
+        s0, ex, s1, s2 = joined(mine, others)
+        self.s1[a] = s1
+        self.s0[a], self.ex[a], self.s2[a] = self.window(s0), self.window(ex), self.window(s2)
 
     def next_j(self, x):
         return jnp.where(self.row == J - 1, 0.0, roll(x, -1, 0))
@@ -263,14 +267,17 @@
         return jnp.where(self.lane == 0, 0.0, roll(x, 1, 1))
 
     def force(self, a):
+        s1 = self.s1[a]
+        row = lax.broadcasted_iota(jnp.int32, (2 * B, K), 0)
+        ahead = jnp.where(row == 2 * B - 1, 0.0, roll(s1, -1, 0))
+        behind = jnp.where(row == 0, 0.0, roll(s1, 1, 0))
         forcing = (
             0.5 * (self.s0[a + 1] - self.s0[a - 1]),
-            0.5 * (self.next_j(self.s1[a]) - self.last_j(self.s1[a])),
+            0.5 * self.window(ahead - behind),
             0.5 * (self.next_k(self.s2[a]) - self.last_k(self.s2[a])),
         )
         for c in range(3):
             self.even[c, a] = forcing[c] / SPECTRUM_CENTRE
-            self.res[c, a] = forcing[c]
 
     def weigh(self, a):
         e = self.ex[a]
@@ -288,29 +295,34 @@
         self.wkp[a] = jnp.where(self.lane == K - 1, 0.0, k_next)
         self.wkm[a] = jnp.where(self.lane == 0, 0.0, k_last)
 
-    def apply(self, src, c, a):
-        v = src[c, a]
-        r = self.res[c, a] - self.dia[a] * v
-        r = r + self.wi[a] * src[c, a + 1]
-        r = r + self.wi[a - 1] * src[c, a - 1]
-        r = r + self.wjp[a] * roll(v, -1, 0)
-        r = r + self.wjm[a] * roll(v, 1, 0)
-        r = r + self.wkp[a] * roll(v, -1, 1)
-        r = r + self.wkm[a] * roll(v, 1, 1)
-        return v, r
-
     def buffers(self, t):
         return (self.even, self.odd) if t % 2 == 0 else (self.odd, self.even)
 
+    def advance(self, t, a):
+        keep, gain = ratios()[t]
+        if t == 0:
+            now, past = keep + SPECTRUM_CENTRE * gain, 0.0
+        else:
+            keep_past, gain_past = ratios()[t - 1]
+            now, past = keep + gain / gain_past, gain * keep_past / gain_past
+        src, dst = self.buffers(t)
+        centre = now - gain * self.dia[a]
+        out = []
+        for c in range(3):
+            v = src[c, a]
+            side = self.wi[a] * src[c, a + 1] + self.wi[a - 1] * src[c, a - 1]
+            side = side + (self.wjp[a] * roll(v, -1, 0) + self.wjm[a] * roll(v, 1, 0))
+            side = side + (self.wkp[a] * roll(v, -1, 1) + self.wkm[a] * roll(v, 1, 1))
+            new = centre * v + gain * side
+            out.append((v, new - past * dst[c, a] if t else new))
+        return out
+
     def iterate(self, t, start, stop):
-        keep, gain = ratios()[t]
-        src, dst = self.buffers(t)
+        dst = self.buffers(t)[1]
 
         def plane(a, inner):
-            for c in range(3):
-                v, r = self.apply(src, c, a)
-                self.res[c, a] = r
-                dst[c, a] = keep * v + gain * r
+            for c, (v, new) in enumerate(self.advance(t, a)):
+                dst[c, a] = new
                 if inner:
                     self.sol[c, a - GO] = v if t == 0 else self.sol[c, a - GO] + v
 
@@ -335,8 +347,8 @@
 
 
 def solve_outer_kernel(near, far, o_near, o_far, *refs):
-    state = refs[14:28]
-    out, rows, flat = refs[28:]
+    state = refs[13:26]
+    out, rows, flat = refs[26:]
     solver = Solver(state)
     even, odd = parity()
     place = lax.axis_index("space")
@@ -346,7 +358,7 @@
         for t in range(ITERS):
             part = slice(4 * B * t, 4 * B * (t + 1))
             solver.put(1 + t + (GO + B - 1) * top, halo[part], others[part])
-        (solver.s0[(N - 1) * top],) = joined(halo[tail], others[tail])
+        solver.s0[(N - 1) * top] = solver.window(joined(halo[tail], others[tail])[0])
 
     loop(1, GO + 1, solver.force)
     loop(GO + B - 1, N - 1, solver.force)
@@ -366,30 +378,25 @@
         solver.iterate(t, 2 + t, GO + 2 + t)
         solver.iterate(t, GO + B - 2 - t, N - 2 - t)
 
-    keep, gain = ratios()[ITERS - 1]
-    src, _ = solver.buffers(ITERS - 1)
     third = lax.broadcasted_iota(jnp.int32, (B, K), 1) % 3
     target = lax.broadcasted_iota(jnp.int32, (K // 3, K), 0)
     source = lax.broadcasted_iota(jnp.int32, (K // 3, K), 1) // 3
     pick = jnp.where(target == source, 1.0, 0.0).astype(jnp.bfloat16)
-    pick = jnp.concatenate([pick, pick, pick], 1)
+    pick = jnp.concatenate([pick, pick], 1)
     rows[9 * B :] = jnp.zeros((128 - 9 * B, K), jnp.float32)
 
     def finish(i):
         a = i + GO
-        for c in range(3):
-            v, r = solver.apply(src, c, a)
-            total = solver.sol[c, i] + v + (keep * v + gain * r)
-            mine = jnp.where(bottom, total[:B], total[B:])
+        for c, (v, new) in enumerate(solver.advance(ITERS - 1, a)):
+            total = solver.sol[c, i] + v + new
+            mine = jnp.where(bottom, total[:B], total[J - B :])
             for q in range(3):
                 g = 3 * c + q
                 rows[B * g : B * g + B] = jnp.where(third == q, mine, 0.0)
-        value = rows[...]
-        high, low = halves(value)
-        rest = value - high.astype(jnp.float32) - low.astype(jnp.float32)
+        high, low = halves(rows[...])
         flat[pl.ds(i, K // 3, stride=B), :] = lax.dot_general(
             pick,
-            jnp.concatenate([high, low, rest.astype(jnp.bfloat16)], 1),
+            jnp.concatenate([high, low], 1),
             (((1,), (1,)), ((), ())),
             preferred_element_type=jnp.float32,
         )
@@ -440,13 +447,9 @@
         return lax.ppermute(array, "slab", [(0, 1), (1, 0)])
 
     ph = jnp.transpose(phases, (1, 2, 0, 3))
-    to_near, to_far, to_other = call(
-        pack_kernel,
-        [(H * B + 1, F, K)] * 3,
-        [ph, mobility[None], active[0, 0].T],
-        hbm_in=(0,),
-        extra=[pltpu.SemaphoreType.DMA((2 * H + B,))],
-        grant=61,
+    rates = mobility[:, None] * active[0, 0].T.astype(jnp.float32)
+    to_near, to_far, to_other, speed = call(
+        pack_kernel, [(H * B + 1, F, K)] * 3 + [(F, K)], [ph, rates], grant=4
     )
     across = swap(to_other)
     near, far = exchange(to_near, to_far)
@@ -455,7 +458,7 @@
     first, second, evolved, coef, mix = call(
         relax_inner_kernel,
         [block, block, (B, B, F, K), coefs, jax.ShapeDtypeStruct((12 * B, 3 * B * F), jnp.bfloat16)],
-        [ph, to_other, across, variants.T],
+        [ph, speed, across, variants.T],
         [(3, 2, F, K), (B - 6, B, F, K)],
         grant=4,
         extra=[pltpu.SemaphoreType.DMA((B - 6,))],
@@ -465,7 +468,7 @@
     first, second, evolved, coef, to_near, to_far = call(
         relax_outer_kernel,
         [block, block, (B, B, F, K), coefs, message, message],
-        [near, far, swap(near), swap(far), to_other, across, mix, first, second, evolved, coef],
+        [near, far, swap(near[:REST]), swap(far[:REST]), speed, across, mix, first, second, evolved, coef],
         [(3, 2, F, K), (2 * H, B, F, K)],
         grant=4,
         aliases={7: 0, 8: 1, 9: 2, 10: 3},
@@ -475,7 +478,7 @@
     )
     o_coef = swap(coef)
     near, far = exchange(to_near, to_far)
-    shapes = [(N, J, K)] * 10 + [(3, N, J, K)] * 3 + [(3, B, J, K)]
+    shapes = [(N, J, K), (N, 2 * B, K)] + [(N, J, K)] * 8 + [(3, N, J, K)] * 2 + [(3, B, J, K)]
     state = call(solve_inner_kernel, shapes, [coef, o_coef], grant=4)
     packed = call(
         solve_outer_kernel,
@@ -483,7 +486,7 @@
         [near, far, swap(near), swap(far), *state],
         [(128, K), (K // 3 * B, 128)],
         grant=8,
-        aliases={4 + n: n for n in range(14)},
+        aliases={4 + n: n for n in range(13)},
     )[-1]
     arrived = lax.all_to_all(packed, "space", 0, 0, tiled=True)
     (displacement,) = call(

time: 117 us -> 111 us (0.949)
  Pallas kernels: 32.2 us -> 26.6 us
    pallas_call x6, Pallas kernels: 32.2 us -> 26.6 us  [call(): pl.pallas_call(kernel, out_shape=[s if hasattr(s, 'dtype') else jax.Shape...]
where the time goes in v4:
time: 111 us
  blocking collectives  53.8 us (48%)
  Pallas kernels  26.6 us (24%)
  waiting for transfers between devices  14.1 us (13%)
  starting transfers between devices  13.7 us (12%)
  local copies, waits for them, and re-layouts  1.5 us (1%)
    all_to_all x1, blocking collectives, program(): arrived = lax.all_to_all(packed, 'space', 0, 0, tiled=True)  53.8 us
    pallas_call x6, Pallas kernels, call(): pl.pallas_call(kernel, out_shape=[s if hasattr(s, 'dtype') else jax.Shape...  26.6 us
    ppermute x2, waiting for transfers between devices, exchange(): near = lax.ppermute(to_near, 'space', pairs(0))  14.1 us
    ppermute x2, starting transfers between devices, exchange(): near = lax.ppermute(to_near, 'space', pairs(0))  7.18 us
    ppermute x6, starting transfers between devices, swap(): return lax.ppermute(array, 'slab', [(0, 1), (1, 0)])  5.16 us
  transfers between devices with their start and end apart: 10, of which 2 were waited for; matrix products, arithmetic and copies ran while one was open for 0% of the time, Pallas kernels for 10%

profile of v4, /device:TPU:1, one launch (start us, length us, event | category | flops | bytes accessed | tf_op | source)
XLA Modules:
  0.0 111.3 jit_solution(14501117589954671189)
XLA Ops:
  0.6 0.0 copy-start.2
  0.6 0.8 fusion.rates
  1.4 1.5 %copy-done = f32[8,12,12,384]{3,0,2,1:T(8,128)S(1)} copy-done((f32[8,12,12,384]{3,0,2,1:T(8,128)S(1)}, f32[8,12,12,384]{3,0,2,1:T(8,128)}, u32[]{:S(2)}) %copy-start) | copy-done | bytes 1769496
  2.9 0.2 shard_map.59
  3.0 2.5 %collective-permute-start = (f32[37,8,384]{2,1,0:T(8,128)S(1)}, f32[37,8,384]{2,1,0:T(8,128)S(1)}, u32[]{:S(2)}, u32[]{:S(2)}) collective-permute-start(f32[37,8,384]{2,1,0:T(8,128)S(1)} %get-tuple-element.29), channel_id=1, source_target_pairs={{0,2},{4,6},{8,10},{12,14},{16,18},{20,22},{24,26},{28,30},{32,34}... | collective-permute-start | bytes 1363976 | tf_op jit(solution)/shard_map/ppermute | solution.py:443
  5.5 0.7 collective-permute-start.1
  6.2 1.2 %collective-permute-start.4 = (f32[37,8,384]{2,1,0:T(8,128)S(1)}, f32[37,8,384]{2,1,0:T(8,128)S(1)}, u32[]{:S(2)}, u32[]{:S(2)}) collective-permute-start(f32[37,8,384]{2,1,0:T(8,128)S(1)} %get-tuple-element.32), channel_id=1, source_target_pairs={{0,1},{1,0},{2,3},{3,2},{4,5},{5,4},{6,7},{7,6},{8,9},{9,8},{10,11... | collective-permute-start | bytes 1363976 | tf_op jit(solution)/shard_map/ppermute | solution.py:447
  7.4 7.3 %collective-permute-done.near = f32[37,8,384]{2,1,0:T(8,128)S(1)} collective-permute-done((f32[37,8,384]{2,1,0:T(8,128)S(1)}, f32[37,8,384]{2,1,0:T(8,128)S(1)}, u32[]{:S(2)}, u32[]{:S(2)}) %collective-permute-start) | collective-permute-done | bytes 454688 | tf_op jit(solution)/shard_map/ppermute | solution.py:443
  14.7 2.4 %collective-permute-start.2 = (f32[10,8,384]{2,1,0:T(8,128)S(1)}, f32[10,8,384]{2,1,0:T(8,128)S(1)}, u32[]{:S(2)}, u32[]{:S(2)}) collective-permute-start(f32[10,8,384]{2,1,0:T(8,128)S(1)} %slice.8), channel_id=1, source_target_pairs={{0,1},{1,0},{2,3},{3,2},{4,5},{5,4},{6,7},{7,6},{8,9},{9,8},{10,11... | collective-permute-start | bytes 368648 | tf_op jit(solution)/shard_map/ppermute | solution.py:447
  17.0 0.0 collective-permute-done.1.far
  17.0 0.1 collective-permute-start.3
  17.2 0.0 collective-permute-done.4.across
  17.2 0.0 copy-done.2
  17.2 0.0 copy-done.1
  17.2 6.6 %shard_map.60 = (f32[18,17,8,384]{3,2,1,0:T(8,128)S(1)}, f32[18,17,8,384]{3,2,1,0:T(8,128)S(1)}, f32[12,12,8,384]{3,2,1,0:T(8,128)}, f32[12,48,384]{2,1,0:T(8,128)S(1)}, bf16[144,288]{1,0:T(8,128)(2,1)S(1)}) custom-call(f32[12,12,8,384]{3,2,1,0:T(8,128)S(1)} %bitcast.10, f32[8,384]{1,0:T(8,128)S(1)} %get-tuple-element.31.mine, ...), custom_call_target="tpu_custom_call" | custom-call | tf_op jit(solution)/shard_map/pallas_call | solution.py:421
  23.8 0.0 collective-permute-done.2.c_near
  23.8 0.0 collective-permute-done.3.c_far
  23.8 5.0 %shard_map.61 = (f32[18,17,8,384]{3,2,1,0:T(8,128)S(1)}, f32[18,17,8,384]{3,2,1,0:T(8,128)S(1)}, f32[12,12,8,384]{3,2,1,0:T(8,128)}, f32[12,48,384]{2,1,0:T(8,12...) custom-call(f32[37,8,384]{2,1,0:T(8,128)S(1)} %collective-permute-do, ...), custom_call_target="tpu_custom_call", output_to_operand_aliasing={{0}: (7, {}), {1}: (8, {}), {2}: (9, {}), {3}: (10, {})} | custom-call | tf_op jit(solution)/shard_map/pallas_call | solution.py:421
  28.8 0.5 collective-permute-start.9
  29.3 4.7 %collective-permute-start.5 = (f32[208,384]{1,0:T(8,128)S(1)}, f32[208,384]{1,0:T(8,128)S(1)}, u32[]{:S(2)}, u32[]{:S(2)}) collective-permute-start(f32[208,384]{1,0:T(8,128)S(1)} %get-tuple-element.39), channel_id=1, source_target_pairs={{0,2},{4,6},{8,10},{12,14},{16,18},{20,22},{24,26},{28,30},{32,34}... | collective-permute-start | bytes 958472 | tf_op jit(solution)/shard_map/ppermute | solution.py:443
  34.0 0.7 collective-permute-start.6
  34.7 6.8 %collective-permute-done.5.near = f32[208,384]{1,0:T(8,128)S(1)} collective-permute-done((f32[208,384]{1,0:T(8,128)S(1)}, f32[208,384]{1,0:T(8,128)S(1)}, u32[]{:S(2)}, u32[]{:S(2)}) %collective-permute-start.5) | collective-permute-done | bytes 319520 | tf_op jit(solution)/shard_map/ppermute | solution.py:443
  41.5 1.0 collective-permute-start.7
  42.5 0.0 collective-permute-done.6.far
  42.5 0.0 collective-permute-start.8
  42.5 0.0 collective-permute-done.9.o_coef
  42.5 4.2 %shard_map.62 = (f32[22,16,384]{2,1,0:T(8,128)S(1)}, f32[22,24,384]{2,1,0:T(8,128)S(1)}, f32[22,16,384]{2,1,0:T(8,128)S(1)}, f32[22,16,384]{2,1,0:T(8,128)S(1)},...) custom-call(f32[12,48,384]{2,1,0:T(8,128)S(1)} %get-tuple-element.41, ...), custom_call_target="tpu_custom_call" | custom-call | tf_op jit(solution)/shard_map/pallas_call | solution.py:421
  46.7 0.0 collective-permute-done.7.o_near
  46.7 0.0 collective-permute-done.8.o_far
  46.7 9.5 %shard_map.63 = (f32[22,16,384]{2,1,0:T(8,128)S(1)}, f32[22,24,384]{2,1,0:T(8,128)S(1)}, f32[22,16,384]{2,1,0:T(8,128)S(1)}, f32[22,16,384]{2,1,0:T(8,128)S(1)},...) custom-call(f32[208,384]{1,0:T(8,128)S(1)} %collective-permute-done., ...), custom_call_target="tpu_custom_call", output_to_operand_aliasing={{0}: (4, {}), {1}: (5, {}), {2}: (6, {}), {3}: (7, {}), {4}... | custom-call | tf_op jit(solution)/shard_map/pallas_call | solution.py:421
  56.3 53.8 %all_to_all.5.got = f32[128,12,128]{2,1,0:T(8,128)S(1)} all-to-all(f32[128,12,128]{2,1,0:T(8,128)S(1)} %get-tuple-element.55), channel_id=1, replica_groups=mesh['space'=128,'slab'=2] {'space'}, dimensions={0} | all-to-all | bytes 1572864 | tf_op jit(solution)/shard_map/all_to_all | solution.py:491
  110.1 1.2 %shard_map.64 = f32[3,3,12,1536]{3,2,1,0:T(8,128)} custom-call(f32[128,12,128]{2,1,0:T(8,128)S(1)} %all_to_all.5.got), custom_call_target="tpu_custom_call" | custom-call | tf_op jit(solution)/shard_map/pallas_call | solution.py:421
  (4 shorter events, 0.0 us)
Async XLA Ops:
  0.6 16.5 %copy-start.2 = (f32[8,3]{0,1:T(4,128)S(1)}, f32[8,3]{0,1:T(4,128)}, u32[]{:S(2)}) copy-start(f32[8,3]{0,1:T(4,128)} %param.7) | copy-start | bytes 292
  1.4 1.5 %copy-start = (f32[8,12,12,384]{3,0,2,1:T(8,128)S(1)}, f32[8,12,12,384]{3,0,2,1:T(8,128)}, u32[]{:S(2)}) copy-start(f32[8,12,12,384]{3,0,2,1:T(8,128)} %param.4) | copy-start | bytes 5308420
  2.9 14.3 %copy-start.1 = (f32[8,12,12,384]{3,0,2,1:T(8,128)S(1)}, f32[8,12,12,384]{3,0,2,1:T(8,128)}, u32[]{:S(2)}) copy-start(f32[8,12,12,384]{3,0,2,1:T(8,128)} %param.4) | copy-start | bytes 5308420
  3.0 11.6 %collective-permute-start = (f32[37,8,384]{2,1,0:T(8,128)S(1)}, f32[37,8,384]{2,1,0:T(8,128)S(1)}, u32[]{:S(2)}, u32[]{:S(2)}) collective-permute-start(f32[37,8,384]{2,1,0:T(8,128)S(1)} %get-tuple-element.29), channel_id=1, source_target_pairs={{0,2},{4,6},{8,10},{12,14},{16,18},{20,22},{24,26},{28,30},{32,34}... | collective-permute-start | bytes 1363976 | tf_op jit(solution)/shard_map/ppermute | solution.py:443
  5.5 11.5 %collective-permute-start.1 = (f32[37,8,384]{2,1,0:T(8,128)S(1)}, f32[37,8,384]{2,1,0:T(8,128)S(1)}, u32[]{:S(2)}, u32[]{:S(2)}) collective-permute-start(f32[37,8,384]{2,1,0:T(8,128)S(1)} %get-tuple-element.30), channel_id=1, source_target_pairs={{2,4},{6,8},{10,12},{14,16},{18,20},{22,24},{26,28},{30,32},{34,36... | collective-permute-start | bytes 1363976 | tf_op jit(solution)/shard_map/ppermute | solution.py:442
  6.2 10.9 %collective-permute-start.4 = (f32[37,8,384]{2,1,0:T(8,128)S(1)}, f32[37,8,384]{2,1,0:T(8,128)S(1)}, u32[]{:S(2)}, u32[]{:S(2)}) collective-permute-start(f32[37,8,384]{2,1,0:T(8,128)S(1)} %get-tuple-element.32), channel_id=1, source_target_pairs={{0,1},{1,0},{2,3},{3,2},{4,5},{5,4},{6,7},{7,6},{8,9},{9,8},{10,11... | collective-permute-start | bytes 1363976 | tf_op jit(solution)/shard_map/ppermute | solution.py:447
  14.7 9.1 %collective-permute-start.2 = (f32[10,8,384]{2,1,0:T(8,128)S(1)}, f32[10,8,384]{2,1,0:T(8,128)S(1)}, u32[]{:S(2)}, u32[]{:S(2)}) collective-permute-start(f32[10,8,384]{2,1,0:T(8,128)S(1)} %slice.8), channel_id=1, source_target_pairs={{0,1},{1,0},{2,3},{3,2},{4,5},{5,4},{6,7},{7,6},{8,9},{9,8},{10,11... | collective-permute-start | bytes 368648 | tf_op jit(solution)/shard_map/ppermute | solution.py:447
  17.0 6.8 %collective-permute-start.3 = (f32[10,8,384]{2,1,0:T(8,128)S(1)}, f32[10,8,384]{2,1,0:T(8,128)S(1)}, u32[]{:S(2)}, u32[]{:S(2)}) collective-permute-start(f32[10,8,384]{2,1,0:T(8,128)S(1)} %slice.9), channel_id=1, source_target_pairs={{0,1},{1,0},{2,3},{3,2},{4,5},{5,4},{6,7},{7,6},{8,9},{9,8},{10,11... | collective-permute-start | bytes 368648 | tf_op jit(solution)/shard_map/ppermute | solution.py:447
  28.8 13.7 %collective-permute-start.9 = (f32[12,48,384]{2,1,0:T(8,128)S(1)}, f32[12,48,384]{2,1,0:T(8,128)S(1)}, u32[]{:S(2)}, u32[]{:S(2)}) collective-permute-start(f32[12,48,384]{2,1,0:T(8,128)S(1)} %get-tuple-element.41.coef), channel_id=1, source_target_pairs={{0,1},{1,0},{2,3},{3,2},{4,5},{5,4},{6,7},{7,6},{8,9},{9,8},{10,11... | collective-permute-start | bytes 2654216 | tf_op jit(solution)/shard_map/ppermute | solution.py:447
  29.3 12.2 %collective-permute-start.5 = (f32[208,384]{1,0:T(8,128)S(1)}, f32[208,384]{1,0:T(8,128)S(1)}, u32[]{:S(2)}, u32[]{:S(2)}) collective-permute-start(f32[208,384]{1,0:T(8,128)S(1)} %get-tuple-element.39), channel_id=1, source_target_pairs={{0,2},{4,6},{8,10},{12,14},{16,18},{20,22},{24,26},{28,30},{32,34}... | collective-permute-start | bytes 958472 | tf_op jit(solution)/shard_map/ppermute | solution.py:443
  34.0 8.5 %collective-permute-start.6 = (f32[208,384]{1,0:T(8,128)S(1)}, f32[208,384]{1,0:T(8,128)S(1)}, u32[]{:S(2)}, u32[]{:S(2)}) collective-permute-start(f32[208,384]{1,0:T(8,128)S(1)} %get-tuple-element.40), channel_id=1, source_target_pairs={{2,4},{6,8},{10,12},{14,16},{18,20},{22,24},{26,28},{30,32},{34,36... | collective-permute-start | bytes 958472 | tf_op jit(solution)/shard_map/ppermute | solution.py:442
  41.5 5.2 %collective-permute-start.7 = (f32[208,384]{1,0:T(8,128)S(1)}, f32[208,384]{1,0:T(8,128)S(1)}, u32[]{:S(2)}, u32[]{:S(2)}) collective-permute-start(f32[208,384]{1,0:T(8,128)S(1)} %collective-permute-done.5.near), channel_id=1, source_target_pairs={{0,1},{1,0},{2,3},{3,2},{4,5},{5,4},{6,7},{7,6},{8,9},{9,8},{10,11... | collective-permute-start | bytes 958472 | tf_op jit(solution)/shard_map/ppermute | solution.py:447
  42.5 4.2 %collective-permute-start.8 = (f32[208,384]{1,0:T(8,128)S(1)}, f32[208,384]{1,0:T(8,128)S(1)}, u32[]{:S(2)}, u32[]{:S(2)}) collective-permute-start(f32[208,384]{1,0:T(8,128)S(1)} %collective-permute-done.6.far), channel_id=1, source_target_pairs={{0,1},{1,0},{2,3},{3,2},{4,5},{5,4},{6,7},{7,6},{8,9},{9,8},{10,11... | collective-permute-start | bytes 958472 | tf_op jit(solution)/shard_map/ppermute | solution.py:447

commit v5 on v4

--- a/solution.py
+++ b/solution.py
@@ -100,19 +100,20 @@
 
     def plane(n, _):
         a = place(n)
-        i = a - H
         before = src[a, own - 1]
         x = src[a, own]
-        squares = []
         for j in range(B):
             after = src[a, own + j + 1]
             around = (before + after) + (src[a - 1, own + j] + src[a + 1, own + j])
-            value = update(x, around, own_speed[...])
-            staged[n, j] = value
-            squares.append(value * value)
+            staged[n, j] = update(x, around, own_speed[...])
             before, x = x, after
-        pltpu.make_async_copy(staged.at[n], ev.at[i], sems.at[n]).start()
-        high, low = halves(jnp.concatenate(squares, 0))
+        pltpu.make_async_copy(staged.at[n], ev.at[a - H], sems.at[n]).start()
+        return 0
+
+    lax.fori_loop(0, count, plane, 0)
+    for n in range(count):
+        values = staged[n].reshape(B * F, K)
+        high, low = halves(values * values)
         mixed = jnp.dot(
             mix[...],
             jnp.concatenate([high, low, high], 0),
@@ -124,10 +125,7 @@
         saturation = total / (1.0 + total)
         excess = 0.5 * saturation
         stress = (1.5 + saturation) * dilation + 2.0 * (1.0 + excess) * strain
-        coef[i] = jnp.where(is_excess, excess, stress)
-        return 0
-
-    lax.fori_loop(0, count, plane, 0)
+        coef[place(n) - H] = jnp.where(is_excess, excess, stress)
 
     def settle(n, _):
         pltpu.make_async_copy(staged.at[n], ev.at[place(n) - H], sems.at[n]).wait()
@@ -205,7 +203,7 @@
 
     def ends(depth):
         jump = B + H - 2 * depth - 1
-        return lambda n: depth + n + jnp.where(n >= H, jump + 1 - H, 0)
+        return lambda n: depth + n + (jump + 1 - H) * (n >= H)
 
     window_step(first, second, speed, 1, 2 * H, ends(1))
     window_step(second, first, speed, 2, 2 * H, ends(2))
@@ -348,7 +346,7 @@
 
 def solve_outer_kernel(near, far, o_near, o_far, *refs):
     state = refs[13:26]
-    out, rows, flat = refs[26:]
+    out, rows = refs[26:]
     solver = Solver(state)
     even, odd = parity()
     place = lax.axis_index("space")
@@ -383,7 +381,8 @@
     source = lax.broadcasted_iota(jnp.int32, (K // 3, K), 1) // 3
     pick = jnp.where(target == source, 1.0, 0.0).astype(jnp.bfloat16)
     pick = jnp.concatenate([pick, pick], 1)
-    rows[9 * B :] = jnp.zeros((128 - 9 * B, K), jnp.float32)
+    for i in range(B):
+        rows[i, 9 * B :] = jnp.zeros((128 - 9 * B, K), jnp.float32)
 
     def finish(i):
         a = i + GO
@@ -392,25 +391,22 @@
             mine = jnp.where(bottom, total[:B], total[J - B :])
             for q in range(3):
                 g = 3 * c + q
-                rows[B * g : B * g + B] = jnp.where(third == q, mine, 0.0)
-        high, low = halves(rows[...])
-        flat[pl.ds(i, K // 3, stride=B), :] = lax.dot_general(
+                rows[i, B * g : B * g + B] = jnp.where(third == q, mine, 0.0)
+
+    loop(0, B, finish)
+    for i in range(B):
+        high, low = halves(rows[i])
+        out[pl.ds(i, K // 3, stride=B), :] = lax.dot_general(
             pick,
             jnp.concatenate([high, low], 1),
             (((1,), (1,)), ((), ())),
             preferred_element_type=jnp.float32,
         )
 
-    loop(0, B, finish)
-    for n in range(out.shape[0]):
-        out[n] = flat[B * n : B * (n + 1), :]
-
-
-def unpack_kernel(got, out, flat):
-    for n in range(got.shape[0]):
-        flat[B * n : B * (n + 1), :] = got[n]
-    for t in range(flat.shape[0] // 128):
-        turned = flat[128 * t : 128 * (t + 1), :].T
+
+def unpack_kernel(got, out):
+    for t in range(got.shape[0] // 128):
+        turned = got[128 * t : 128 * (t + 1), :].T
         for c in range(3):
             for q in range(3):
                 g = 3 * c + q
@@ -482,15 +478,16 @@
     state = call(solve_inner_kernel, shapes, [coef, o_coef], grant=4)
     packed = call(
         solve_outer_kernel,
-        shapes + [(K // 3, B, 128)],
+        shapes + [(K // 3 * B, 128)],
         [near, far, swap(near), swap(far), *state],
-        [(128, K), (K // 3 * B, 128)],
+        [(B, 128, K)],
         grant=8,
         aliases={4 + n: n for n in range(13)},
     )[-1]
+    packed = packed.reshape(count, 1, B * 128)
     arrived = lax.all_to_all(packed, "space", 0, 0, tiled=True)
     (displacement,) = call(
-        unpack_kernel, [(3, K // count, B, count * B)], [arrived], [(count * B, 128)]
+        unpack_kernel, [(3, K // count, B, count * B)], [arrived.reshape(count * B, 128)]
     )
     return jnp.transpose(evolved, (2, 0, 1, 3)), displacement
 

time: 111 us -> 102 us (0.919)
  blocking collectives: 53.8 us -> 48.4 us
  Pallas kernels: 26.6 us -> 22.6 us
    all_to_all x1, blocking collectives: 53.8 us -> 48.4 us  [program(): arrived = lax.all_to_all(packed, 'space', 0, 0, tiled=True)]
    pallas_call x6, Pallas kernels: 26.6 us -> 22.6 us  [call(): pl.pallas_call(kernel, out_shape=[s if hasattr(s, 'dtype') else jax.Shape...]
where the time goes in v5:
time: 102 us
  blocking collectives  48.4 us (47%)
  Pallas kernels  22.6 us (22%)
  waiting for transfers between devices  14.1 us (14%)
  starting transfers between devices  13.7 us (13%)
  local copies, waits for them, and re-layouts  1.5 us (1%)
    all_to_all x1, blocking collectives, program(): arrived = lax.all_to_all(packed, 'space', 0, 0, tiled=True)  48.4 us
    pallas_call x6, Pallas kernels, call(): pl.pallas_call(kernel, out_shape=[s if hasattr(s, 'dtype') else jax.Shape...  22.6 us
    ppermute x2, waiting for transfers between devices, exchange(): near = lax.ppermute(to_near, 'space', pairs(0))  14.1 us
    ppermute x2, starting transfers between devices, exchange(): near = lax.ppermute(to_near, 'space', pairs(0))  7.13 us
    ppermute x6, starting transfers between devices, swap(): return lax.ppermute(array, 'slab', [(0, 1), (1, 0)])  5.21 us
  transfers between devices with their start and end apart: 10, of which 2 were waited for; matrix products, arithmetic and copies ran while one was open for 0% of the time, Pallas kernels for 10%

profile of v5, /device:TPU:1, one launch (start us, length us, event | category | flops | bytes accessed | tf_op | source)
XLA Modules:
  0.0 101.8 jit_solution(12938170750315118450)
XLA Ops:
  0.6 0.0 copy-start.2
  0.6 0.8 fusion.rates
  1.4 1.5 %copy-done = f32[8,12,12,384]{3,0,2,1:T(8,128)S(1)} copy-done((f32[8,12,12,384]{3,0,2,1:T(8,128)S(1)}, f32[8,12,12,384]{3,0,2,1:T(8,128)}, u32[]{:S(2)}) %copy-start) | copy-done | bytes 1769496
  2.9 0.2 shard_map.59
  3.0 2.5 %collective-permute-start = (f32[37,8,384]{2,1,0:T(8,128)S(1)}, f32[37,8,384]{2,1,0:T(8,128)S(1)}, u32[]{:S(2)}, u32[]{:S(2)}) collective-permute-start(f32[37,8,384]{2,1,0:T(8,128)S(1)} %get-tuple-element.29), channel_id=1, source_target_pairs={{0,2},{4,6},{8,10},{12,14},{16,18},{20,22},{24,26},{28,30},{32,34}... | collective-permute-start | bytes 1363976 | tf_op jit(solution)/shard_map/ppermute | solution.py:439
  5.5 0.7 collective-permute-start.1
  6.2 1.2 %collective-permute-start.4 = (f32[37,8,384]{2,1,0:T(8,128)S(1)}, f32[37,8,384]{2,1,0:T(8,128)S(1)}, u32[]{:S(2)}, u32[]{:S(2)}) collective-permute-start(f32[37,8,384]{2,1,0:T(8,128)S(1)} %get-tuple-element.32), channel_id=1, source_target_pairs={{0,1},{1,0},{2,3},{3,2},{4,5},{5,4},{6,7},{7,6},{8,9},{9,8},{10,11... | collective-permute-start | bytes 1363976 | tf_op jit(solution)/shard_map/ppermute | solution.py:443
  7.4 7.3 %collective-permute-done.near = f32[37,8,384]{2,1,0:T(8,128)S(1)} collective-permute-done((f32[37,8,384]{2,1,0:T(8,128)S(1)}, f32[37,8,384]{2,1,0:T(8,128)S(1)}, u32[]{:S(2)}, u32[]{:S(2)}) %collective-permute-start) | collective-permute-done | bytes 454688 | tf_op jit(solution)/shard_map/ppermute | solution.py:439
  14.7 2.4 %collective-permute-start.2 = (f32[10,8,384]{2,1,0:T(8,128)S(1)}, f32[10,8,384]{2,1,0:T(8,128)S(1)}, u32[]{:S(2)}, u32[]{:S(2)}) collective-permute-start(f32[10,8,384]{2,1,0:T(8,128)S(1)} %slice.8), channel_id=1, source_target_pairs={{0,1},{1,0},{2,3},{3,2},{4,5},{5,4},{6,7},{7,6},{8,9},{9,8},{10,11... | collective-permute-start | bytes 368648 | tf_op jit(solution)/shard_map/ppermute | solution.py:443
  17.0 0.0 collective-permute-done.1.far
  17.0 0.1 collective-permute-start.3
  17.2 0.0 collective-permute-done.4.across
  17.2 0.0 copy-done.2
  17.2 0.0 copy-done.1
  17.2 5.5 %shard_map.60 = (f32[18,17,8,384]{3,2,1,0:T(8,128)S(1)}, f32[18,17,8,384]{3,2,1,0:T(8,128)S(1)}, f32[12,12,8,384]{3,2,1,0:T(8,128)}, f32[12,48,384]{2,1,0:T(8,128)S(1)}, bf16[144,288]{1,0:T(8,128)(2,1)S(1)}) custom-call(f32[12,12,8,384]{3,2,1,0:T(8,128)S(1)} %bitcast.12, f32[8,384]{1,0:T(8,128)S(1)} %get-tuple-element.31.mine, ...), custom_call_target="tpu_custom_call" | custom-call | tf_op jit(solution)/shard_map/pallas_call | solution.py:417
  22.7 0.0 collective-permute-done.2.c_near
  22.7 0.0 collective-permute-done.3.c_far
  22.7 3.9 %shard_map.61 = (f32[18,17,8,384]{3,2,1,0:T(8,128)S(1)}, f32[18,17,8,384]{3,2,1,0:T(8,128)S(1)}, f32[12,12,8,384]{3,2,1,0:T(8,128)}, f32[12,48,384]{2,1,0:T(8,12...) custom-call(f32[37,8,384]{2,1,0:T(8,128)S(1)} %collective-permute-do, ...), custom_call_target="tpu_custom_call", output_to_operand_aliasing={{0}: (7, {}), {1}: (8, {}), {2}: (9, {}), {3}: (10, {})} | custom-call | tf_op jit(solution)/shard_map/pallas_call | solution.py:417
  26.6 0.6 collective-permute-start.9
  27.1 4.6 %collective-permute-start.5 = (f32[208,384]{1,0:T(8,128)S(1)}, f32[208,384]{1,0:T(8,128)S(1)}, u32[]{:S(2)}, u32[]{:S(2)}) collective-permute-start(f32[208,384]{1,0:T(8,128)S(1)} %get-tuple-element.39), channel_id=1, source_target_pairs={{0,2},{4,6},{8,10},{12,14},{16,18},{20,22},{24,26},{28,30},{32,34}... | collective-permute-start | bytes 958472 | tf_op jit(solution)/shard_map/ppermute | solution.py:439
  31.8 0.7 collective-permute-start.6
  32.4 6.8 %collective-permute-done.5.near = f32[208,384]{1,0:T(8,128)S(1)} collective-permute-done((f32[208,384]{1,0:T(8,128)S(1)}, f32[208,384]{1,0:T(8,128)S(1)}, u32[]{:S(2)}, u32[]{:S(2)}) %collective-permute-start.5) | collective-permute-done | bytes 319520 | tf_op jit(solution)/shard_map/ppermute | solution.py:439
  39.3 1.0 collective-permute-start.7
  40.3 0.0 collective-permute-done.6.far
  40.3 0.0 collective-permute-start.8
  40.3 0.0 collective-permute-done.9.o_coef
  40.3 4.2 %shard_map.62 = (f32[22,16,384]{2,1,0:T(8,128)S(1)}, f32[22,24,384]{2,1,0:T(8,128)S(1)}, f32[22,16,384]{2,1,0:T(8,128)S(1)}, f32[22,16,384]{2,1,0:T(8,128)S(1)},...) custom-call(f32[12,48,384]{2,1,0:T(8,128)S(1)} %get-tuple-element.41, ...), custom_call_target="tpu_custom_call" | custom-call | tf_op jit(solution)/shard_map/pallas_call | solution.py:417
  44.5 0.0 collective-permute-done.7.o_near
  44.5 0.0 collective-permute-done.8.o_far
  44.5 7.7 %shard_map.63 = (f32[22,16,384]{2,1,0:T(8,128)S(1)}, f32[22,24,384]{2,1,0:T(8,128)S(1)}, f32[22,16,384]{2,1,0:T(8,128)S(1)}, f32[22,16,384]{2,1,0:T(8,128)S(1)},...) custom-call(f32[208,384]{1,0:T(8,128)S(1)} %collective-permute-done., ...), custom_call_target="tpu_custom_call", output_to_operand_aliasing={{0}: (4, {}), {1}: (5, {}), {2}: (6, {}), {3}: (7, {}), {4}... | custom-call | tf_op jit(solution)/shard_map/pallas_call | solution.py:417
  52.2 48.4 %all_to_all.5 = f32[128,1,1536]{2,1,0:T(1,128)S(1)} all-to-all(f32[128,1,1536]{2,1,0:T(1,128)S(1)} %bitcast.14), channel_id=1, replica_groups=mesh['space'=128,'slab'=2] {'space'}, dimensions={0} | all-to-all | bytes 1572864 | tf_op jit(solution)/shard_map/all_to_all | solution.py:488
  100.6 1.2 %shard_map.64 = f32[3,3,12,1536]{3,2,1,0:T(8,128)} custom-call(f32[1536,128]{1,0:T(8,128)S(1)} %bitcast.13), custom_call_target="tpu_custom_call" | custom-call | tf_op jit(solution)/shard_map/pallas_call | solution.py:417
  (4 shorter events, 0.0 us)
Async XLA Ops:
  0.6 16.5 %copy-start.2 = (f32[8,3]{0,1:T(4,128)S(1)}, f32[8,3]{0,1:T(4,128)}, u32[]{:S(2)}) copy-start(f32[8,3]{0,1:T(4,128)} %param.7) | copy-start | bytes 292
  1.4 1.5 %copy-start = (f32[8,12,12,384]{3,0,2,1:T(8,128)S(1)}, f32[8,12,12,384]{3,0,2,1:T(8,128)}, u32[]{:S(2)}) copy-start(f32[8,12,12,384]{3,0,2,1:T(8,128)} %param.4) | copy-start | bytes 5308420
  2.9 14.3 %copy-start.1 = (f32[8,12,12,384]{3,0,2,1:T(8,128)S(1)}, f32[8,12,12,384]{3,0,2,1:T(8,128)}, u32[]{:S(2)}) copy-start(f32[8,12,12,384]{3,0,2,1:T(8,128)} %param.4) | copy-start | bytes 5308420
  3.0 11.6 %collective-permute-start = (f32[37,8,384]{2,1,0:T(8,128)S(1)}, f32[37,8,384]{2,1,0:T(8,128)S(1)}, u32[]{:S(2)}, u32[]{:S(2)}) collective-permute-start(f32[37,8,384]{2,1,0:T(8,128)S(1)} %get-tuple-element.29), channel_id=1, source_target_pairs={{0,2},{4,6},{8,10},{12,14},{16,18},{20,22},{24,26},{28,30},{32,34}... | collective-permute-start | bytes 1363976 | tf_op jit(solution)/shard_map/ppermute | solution.py:439
  5.5 11.5 %collective-permute-start.1 = (f32[37,8,384]{2,1,0:T(8,128)S(1)}, f32[37,8,384]{2,1,0:T(8,128)S(1)}, u32[]{:S(2)}, u32[]{:S(2)}) collective-permute-start(f32[37,8,384]{2,1,0:T(8,128)S(1)} %get-tuple-element.30), channel_id=1, source_target_pairs={{2,4},{6,8},{10,12},{14,16},{18,20},{22,24},{26,28},{30,32},{34,36... | collective-permute-start | bytes 1363976 | tf_op jit(solution)/shard_map/ppermute | solution.py:438
  6.2 10.9 %collective-permute-start.4 = (f32[37,8,384]{2,1,0:T(8,128)S(1)}, f32[37,8,384]{2,1,0:T(8,128)S(1)}, u32[]{:S(2)}, u32[]{:S(2)}) collective-permute-start(f32[37,8,384]{2,1,0:T(8,128)S(1)} %get-tuple-element.32), channel_id=1, source_target_pairs={{0,1},{1,0},{2,3},{3,2},{4,5},{5,4},{6,7},{7,6},{8,9},{9,8},{10,11... | collective-permute-start | bytes 1363976 | tf_op jit(solution)/shard_map/ppermute | solution.py:443
  14.7 8.0 %collective-permute-start.2 = (f32[10,8,384]{2,1,0:T(8,128)S(1)}, f32[10,8,384]{2,1,0:T(8,128)S(1)}, u32[]{:S(2)}, u32[]{:S(2)}) collective-permute-start(f32[10,8,384]{2,1,0:T(8,128)S(1)} %slice.8), channel_id=1, source_target_pairs={{0,1},{1,0},{2,3},{3,2},{4,5},{5,4},{6,7},{7,6},{8,9},{9,8},{10,11... | collective-permute-start | bytes 368648 | tf_op jit(solution)/shard_map/ppermute | solution.py:443
  17.0 5.6 %collective-permute-start.3 = (f32[10,8,384]{2,1,0:T(8,128)S(1)}, f32[10,8,384]{2,1,0:T(8,128)S(1)}, u32[]{:S(2)}, u32[]{:S(2)}) collective-permute-start(f32[10,8,384]{2,1,0:T(8,128)S(1)} %slice.9), channel_id=1, source_target_pairs={{0,1},{1,0},{2,3},{3,2},{4,5},{5,4},{6,7},{7,6},{8,9},{9,8},{10,11... | collective-permute-start | bytes 368648 | tf_op jit(solution)/shard_map/ppermute | solution.py:443
  26.6 13.7 %collective-permute-start.9 = (f32[12,48,384]{2,1,0:T(8,128)S(1)}, f32[12,48,384]{2,1,0:T(8,128)S(1)}, u32[]{:S(2)}, u32[]{:S(2)}) collective-permute-start(f32[12,48,384]{2,1,0:T(8,128)S(1)} %get-tuple-element.41.coef), channel_id=1, source_target_pairs={{0,1},{1,0},{2,3},{3,2},{4,5},{5,4},{6,7},{7,6},{8,9},{9,8},{10,11... | collective-permute-start | bytes 2654216 | tf_op jit(solution)/shard_map/ppermute | solution.py:443
  27.1 12.1 %collective-permute-start.5 = (f32[208,384]{1,0:T(8,128)S(1)}, f32[208,384]{1,0:T(8,128)S(1)}, u32[]{:S(2)}, u32[]{:S(2)}) collective-permute-start(f32[208,384]{1,0:T(8,128)S(1)} %get-tuple-element.39), channel_id=1, source_target_pairs={{0,2},{4,6},{8,10},{12,14},{16,18},{20,22},{24,26},{28,30},{32,34}... | collective-permute-start | bytes 958472 | tf_op jit(solution)/shard_map/ppermute | solution.py:439
  31.8 8.5 %collective-permute-start.6 = (f32[208,384]{1,0:T(8,128)S(1)}, f32[208,384]{1,0:T(8,128)S(1)}, u32[]{:S(2)}, u32[]{:S(2)}) collective-permute-start(f32[208,384]{1,0:T(8,128)S(1)} %get-tuple-element.40), channel_id=1, source_target_pairs={{2,4},{6,8},{10,12},{14,16},{18,20},{22,24},{26,28},{30,32},{34,36... | collective-permute-start | bytes 958472 | tf_op jit(solution)/shard_map/ppermute | solution.py:438
  39.3 5.2 %collective-permute-start.7 = (f32[208,384]{1,0:T(8,128)S(1)}, f32[208,384]{1,0:T(8,128)S(1)}, u32[]{:S(2)}, u32[]{:S(2)}) collective-permute-start(f32[208,384]{1,0:T(8,128)S(1)} %collective-permute-done.5.near), channel_id=1, source_target_pairs={{0,1},{1,0},{2,3},{3,2},{4,5},{5,4},{6,7},{7,6},{8,9},{9,8},{10,11... | collective-permute-start | bytes 958472 | tf_op jit(solution)/shard_map/ppermute | solution.py:443
  40.3 4.2 %collective-permute-start.8 = (f32[208,384]{1,0:T(8,128)S(1)}, f32[208,384]{1,0:T(8,128)S(1)}, u32[]{:S(2)}, u32[]{:S(2)}) collective-permute-start(f32[208,384]{1,0:T(8,128)S(1)} %collective-permute-done.6.far), channel_id=1, source_target_pairs={{0,1},{1,0},{2,3},{3,2},{4,5},{5,4},{6,7},{7,6},{8,9},{9,8},{10,11... | collective-permute-start | bytes 958472 | tf_op jit(solution)/shard_map/ppermute | solution.py:443

commit v6 on v5

--- a/solution.py
+++ b/solution.py
@@ -135,7 +135,7 @@
 
 
 def relax_inner_kernel(
-    ph, mine, across, variants, first, second, ev, coef, mix, speed, staged, sems
+    ph, mine, across, variants, first, second, ev, coef, mix, e_near, e_far, speed, staged, sems
 ):
     slab = lax.axis_index("slab")
     own = 1 + H * slab
@@ -179,6 +179,10 @@
     window_step(first, second, speed, 1, B - 2, lambda n: H + 1 + n)
     window_step(second, first, speed, 2, B - 4, lambda n: H + 2 + n)
     last_step(first, speed.at[1, 0], mix, ev, coef, B - 6, lambda n: H + 3 + n, staged, sems)
+    even, odd = parity()
+    for message, top in ((e_near, even), (e_far, odd)):
+        message[: 4 * B] = coef[H + (B - 2 * H - 1) * top]
+        message[4 * B :] = coef[H + 1 + (B - 2 * H - 3) * top, :16]
 
 
 def relax_outer_kernel(
@@ -209,9 +213,8 @@
     window_step(second, first, speed, 2, 2 * H, ends(2))
     last_step(first, speed.at[1, 0], mix, ev, coef, 2 * H, ends(3), staged, sems)
     for message, top in ((m_near, even), (m_far, odd)):
-        for t in range(ITERS):
-            message[4 * B * t : 4 * B * (t + 1)] = coef[(B - ITERS) * top + t]
-        message[4 * B * ITERS :] = coef[ITERS + (B - 2 * ITERS - 1) * top, :16]
+        for t in range(H):
+            message[4 * B * t : 4 * B * (t + 1)] = coef[(B - H) * top + t]
 
 
 J = B + ITERS
@@ -344,19 +347,24 @@
         solver.iterate(t, GO + 2 + t, GO + B - 2 - t)
 
 
-def solve_outer_kernel(near, far, o_near, o_far, *refs):
+def solve_outer_kernel(near, far, o_near, o_far, e_near, e_far, oe_near, oe_far, *refs):
     state = refs[13:26]
     out, rows = refs[26:]
     solver = Solver(state)
     even, odd = parity()
     place = lax.axis_index("space")
     bottom = lax.axis_index("slab") == 0
-    tail = slice(4 * B * ITERS, 4 * B * ITERS + 16)
-    for halo, others, top in ((near, o_near, even), (far, o_far, odd)):
-        for t in range(ITERS):
+    sides = (
+        (near, o_near, e_near, oe_near, even),
+        (far, o_far, e_far, oe_far, odd),
+    )
+    for halo, others, early, others_early, top in sides:
+        for t in range(H):
             part = slice(4 * B * t, 4 * B * (t + 1))
-            solver.put(1 + t + (GO + B - 1) * top, halo[part], others[part])
-        solver.s0[(N - 1) * top] = solver.window(joined(halo[tail], others[tail])[0])
+            solver.put(2 + t + (GO + B - 2) * top, halo[part], others[part])
+        whole, tail = slice(0, 4 * B), slice(4 * B, 4 * B + 16)
+        solver.put(1 + (N - 3) * top, early[whole], others_early[whole])
+        solver.s0[(N - 1) * top] = solver.window(joined(early[tail], others_early[tail])[0])
 
     loop(1, GO + 1, solver.force)
     loop(GO + B - 1, N - 1, solver.force)
@@ -451,16 +459,20 @@
     near, far = exchange(to_near, to_far)
     block = (B + 2 * H, W + 2, F, K)
     coefs = (B, 4 * B, K)
-    first, second, evolved, coef, mix = call(
+    message = (4 * B + 16, K)
+    products = jax.ShapeDtypeStruct((12 * B, 3 * B * F), jnp.bfloat16)
+    first, second, evolved, coef, mix, e_near, e_far = call(
         relax_inner_kernel,
-        [block, block, (B, B, F, K), coefs, jax.ShapeDtypeStruct((12 * B, 3 * B * F), jnp.bfloat16)],
+        [block, block, (B, B, F, K), coefs, products, message, message],
         [ph, speed, across, variants.T],
         [(3, 2, F, K), (B - 6, B, F, K)],
         grant=4,
         extra=[pltpu.SemaphoreType.DMA((B - 6,))],
         hbm_out=(2,),
     )
-    message = (4 * B * ITERS + 16, K)
+    e_near, e_far = exchange(e_near, e_far)
+    oe_near, oe_far = swap(e_near), swap(e_far)
+    message = (4 * B * H, K)
     first, second, evolved, coef, to_near, to_far = call(
         relax_outer_kernel,
         [block, block, (B, B, F, K), coefs, message, message],
@@ -479,10 +491,10 @@
     packed = call(
         solve_outer_kernel,
         shapes + [(K // 3 * B, 128)],
-        [near, far, swap(near), swap(far), *state],
+        [near, far, swap(near), swap(far), e_near, e_far, oe_near, oe_far, *state],
         [(B, 128, K)],
         grant=8,
-        aliases={4 + n: n for n in range(13)},
+        aliases={8 + n: n for n in range(13)},
     )[-1]
     packed = packed.reshape(count, 1, B * 128)
     arrived = lax.all_to_all(packed, "space", 0, 0, tiled=True)

time: 102 us -> 111 us (1.088)
  starting transfers between devices: 13.7 us -> 20.4 us
  blocking collectives: 48.4 us -> 50.5 us
    ppermute x2 -> x3, starting transfers between devices: 7.13 us -> 12.6 us  [exchange(): near = lax.ppermute(to_near, 'space', pairs(0))]
    all_to_all x1, blocking collectives: 48.4 us -> 50.5 us  [program(): arrived = lax.all_to_all(packed, 'space', 0, 0, tiled=True)]
    ppermute x6 -> x8, starting transfers between devices: 5.21 us -> 5.8 us  [swap(): return lax.ppermute(array, 'slab', [(0, 1), (1, 0)])]
    ppermute x2 -> x3, waiting for transfers between devices: 14.1 us -> 14.5 us  [exchange(): near = lax.ppermute(to_near, 'space', pairs(0))]
  transfers between devices with their start and end apart: 10 -> 14, of which waited for: 2 -> 3; matrix products, arithmetic and copies ran while one was open for 0% -> 0% of each run, Pallas kernels for 10% -> 9%
where the time goes in v6:
time: 111 us
  blocking collectives  50.5 us (45%)
  Pallas kernels  22.6 us (20%)
  starting transfers between devices  20.4 us (18%)
  waiting for transfers between devices  14.5 us (13%)
  local copies, waits for them, and re-layouts  1.5 us (1%)
    all_to_all x1, blocking collectives, program(): arrived = lax.all_to_all(packed, 'space', 0, 0, tiled=True)  50.5 us
    pallas_call x6, Pallas kernels, call(): pl.pallas_call(kernel, out_shape=[s if hasattr(s, 'dtype') else jax.Shape...  22.6 us
    ppermute x3, waiting for transfers between devices, exchange(): near = lax.ppermute(to_near, 'space', pairs(0))  14.5 us
    ppermute x3, starting transfers between devices, exchange(): near = lax.ppermute(to_near, 'space', pairs(0))  12.6 us
    ppermute x8, starting transfers between devices, swap(): return lax.ppermute(array, 'slab', [(0, 1), (1, 0)])  5.8 us
  transfers between devices with their start and end apart: 14, of which 3 were waited for; matrix products, arithmetic and copies ran while one was open for 0% of the time, Pallas kernels for 9%

profile of v6, /device:TPU:1, one launch (start us, length us, event | category | flops | bytes accessed | tf_op | source)
XLA Modules:
  0.0 111.0 jit_solution(4519629306176330051)
XLA Ops:
  0.6 0.8 fusion.rates
  1.4 1.5 %copy-done = f32[8,12,12,384]{3,0,2,1:T(8,128)S(1)} copy-done((f32[8,12,12,384]{3,0,2,1:T(8,128)S(1)}, f32[8,12,12,384]{3,0,2,1:T(8,128)}, u32[]{:S(2)}) %copy-start) | copy-done | bytes 1769496
  2.9 0.2 shard_map.59
  3.0 2.5 %collective-permute-start = (f32[37,8,384]{2,1,0:T(8,128)S(1)}, f32[37,8,384]{2,1,0:T(8,128)S(1)}, u32[]{:S(2)}, u32[]{:S(2)}) collective-permute-start(f32[37,8,384]{2,1,0:T(8,128)S(1)} %get-tuple-element.31), channel_id=1, source_target_pairs={{0,2},{4,6},{8,10},{12,14},{16,18},{20,22},{24,26},{28,30},{32,34}... | collective-permute-start | bytes 1363976 | tf_op jit(solution)/shard_map/ppermute | solution.py:447
  5.5 0.7 collective-permute-start.1
  6.2 1.2 %collective-permute-start.4 = (f32[37,8,384]{2,1,0:T(8,128)S(1)}, f32[37,8,384]{2,1,0:T(8,128)S(1)}, u32[]{:S(2)}, u32[]{:S(2)}) collective-permute-start(f32[37,8,384]{2,1,0:T(8,128)S(1)} %get-tuple-element.34), channel_id=1, source_target_pairs={{0,1},{1,0},{2,3},{3,2},{4,5},{5,4},{6,7},{7,6},{8,9},{9,8},{10,11... | collective-permute-start | bytes 1363976 | tf_op jit(solution)/shard_map/ppermute | solution.py:451
  7.4 7.3 %collective-permute-done.near = f32[37,8,384]{2,1,0:T(8,128)S(1)} collective-permute-done((f32[37,8,384]{2,1,0:T(8,128)S(1)}, f32[37,8,384]{2,1,0:T(8,128)S(1)}, u32[]{:S(2)}, u32[]{:S(2)}) %collective-permute-start) | collective-permute-done | bytes 454688 | tf_op jit(solution)/shard_map/ppermute | solution.py:447
  14.7 2.4 %collective-permute-start.2 = (f32[10,8,384]{2,1,0:T(8,128)S(1)}, f32[10,8,384]{2,1,0:T(8,128)S(1)}, u32[]{:S(2)}, u32[]{:S(2)}) collective-permute-start(f32[10,8,384]{2,1,0:T(8,128)S(1)} %slice.8), channel_id=1, source_target_pairs={{0,1},{1,0},{2,3},{3,2},{4,5},{5,4},{6,7},{7,6},{8,9},{9,8},{10,11... | collective-permute-start | bytes 368648 | tf_op jit(solution)/shard_map/ppermute | solution.py:451
  17.0 0.0 collective-permute-done.1.far
  17.0 0.1 collective-permute-start.3
  17.2 5.5 %shard_map.60 = (f32[18,17,8,384]{3,2,1,0:T(8,128)S(1)}, f32[18,17,8,384]{3,2,1,0:T(8,128)S(1)}, f32[12,12,8,384]{3,2,1,0:T(8,128)}, f32[12,48,384]{2,1,0:T(8,12...) custom-call(f32[12,12,8,384]{3,2,1,0:T(8,128)S(1)} %bitcast.12, ...), custom_call_target="tpu_custom_call" | custom-call | tf_op jit(solution)/shard_map/pallas_call | solution.py:425
  22.7 0.0 collective-permute-done.2.c_near
  22.7 3.8 %shard_map.61 = (f32[18,17,8,384]{3,2,1,0:T(8,128)S(1)}, f32[18,17,8,384]{3,2,1,0:T(8,128)S(1)}, f32[12,12,8,384]{3,2,1,0:T(8,128)}, f32[12,48,384]{2,1,0:T(8,12...) custom-call(f32[37,8,384]{2,1,0:T(8,128)S(1)} %collective-permute-do, ...), custom_call_target="tpu_custom_call", output_to_operand_aliasing={{0}: (7, {}), {1}: (8, {}), {2}: (9, {}), {3}: (10, {})} | custom-call | tf_op jit(solution)/shard_map/pallas_call | solution.py:425
  26.6 0.6 collective-permute-start.13
  27.1 4.6 %collective-permute-start.5 = (f32[144,384]{1,0:T(8,128)S(1)}, f32[144,384]{1,0:T(8,128)S(1)}, u32[]{:S(2)}, u32[]{:S(2)}) collective-permute-start(f32[144,384]{1,0:T(8,128)S(1)} %get-tuple-element.41), channel_id=1, source_target_pairs={{0,2},{4,6},{8,10},{12,14},{16,18},{20,22},{24,26},{28,30},{32,34}... | collective-permute-start | bytes 663560 | tf_op jit(solution)/shard_map/ppermute | solution.py:447
  31.8 0.7 collective-permute-start.6
  32.5 4.7 %collective-permute-done.5.near = f32[144,384]{1,0:T(8,128)S(1)} collective-permute-done((f32[144,384]{1,0:T(8,128)S(1)}, f32[144,384]{1,0:T(8,128)S(1)}, u32[]{:S(2)}, u32[]{:S(2)}) %collective-permute-start.5) | collective-permute-done | bytes 221216 | tf_op jit(solution)/shard_map/ppermute | solution.py:447
  37.2 1.0 collective-permute-start.7
  38.2 0.0 collective-permute-done.6.far
  38.2 0.0 collective-permute-start.8
  38.2 5.5 %collective-permute-start.9 = (f32[64,384]{1,0:T(8,128)S(1)}, f32[64,384]{1,0:T(8,128)S(1)}, u32[]{:S(2)}, u32[]{:S(2)}) collective-permute-start(f32[64,384]{1,0:T(8,128)S(1)} %get-tuple-element.43), channel_id=1, source_target_pairs={{0,2},{4,6},{8,10},{12,14},{16,18},{20,22},{24,26},{28,30},{32,34}... | collective-permute-start | bytes 294920 | tf_op jit(solution)/shard_map/ppermute | solution.py:447
  43.6 0.7 collective-permute-start.10
  44.3 2.5 %collective-permute-done.9.e_near = f32[64,384]{1,0:T(8,128)S(1)} collective-permute-done((f32[64,384]{1,0:T(8,128)S(1)}, f32[64,384]{1,0:T(8,128)S(1)}, u32[]{:S(2)}, u32[]{:S(2)}) %collective-permute-start.9) | collective-permute-done | bytes 98336 | tf_op jit(solution)/shard_map/ppermute | solution.py:447
  46.8 0.6 collective-permute-start.11
  47.4 0.0 collective-permute-done.10.e_far
  47.4 0.0 collective-permute-start.12
  47.4 4.2 %shard_map.62 = (f32[22,16,384]{2,1,0:T(8,128)S(1)}, f32[22,24,384]{2,1,0:T(8,128)S(1)}, f32[22,16,384]{2,1,0:T(8,128)S(1)}, f32[22,16,384]{2,1,0:T(8,128)S(1)},...) custom-call(f32[12,48,384]{2,1,0:T(8,128)S(1)} %get-tuple-element.45, ...), custom_call_target="tpu_custom_call" | custom-call | tf_op jit(solution)/shard_map/pallas_call | solution.py:425
  51.6 0.0 collective-permute-done.11.oe_near
  51.6 0.0 collective-permute-done.7.o_near
  51.6 7.7 %shard_map.63 = (f32[22,16,384]{2,1,0:T(8,128)S(1)}, f32[22,24,384]{2,1,0:T(8,128)S(1)}, f32[22,16,384]{2,1,0:T(8,128)S(1)}, f32[22,16,384]{2,1,0:T(8,128)S(1)},...) custom-call(f32[144,384]{1,0:T(8,128)S(1)} %collective-permute-done., ...), custom_call_target="tpu_custom_call", output_to_operand_aliasing={{0}: (8, {}), {1}: (9, {}), {2}: (10, {}), {3}: (11, {}), {... | custom-call | tf_op jit(solution)/shard_map/pallas_call | solution.py:425
  59.3 50.5 %all_to_all.5 = f32[128,1,1536]{2,1,0:T(1,128)S(1)} all-to-all(f32[128,1,1536]{2,1,0:T(1,128)S(1)} %bitcast.14), channel_id=1, replica_groups=mesh['space'=128,'slab'=2] {'space'}, dimensions={0} | all-to-all | bytes 1572864 | tf_op jit(solution)/shard_map/all_to_all | solution.py:500
  109.8 1.2 %shard_map.64 = f32[3,3,12,1536]{3,2,1,0:T(8,128)} custom-call(f32[1536,128]{1,0:T(8,128)S(1)} %bitcast.13), custom_call_target="tpu_custom_call" | custom-call | tf_op jit(solution)/shard_map/pallas_call | solution.py:425
  (12 shorter events, 0.0 us)
Async XLA Ops:
  0.6 16.5 %copy-start.2 = (f32[8,3]{0,1:T(4,128)S(1)}, f32[8,3]{0,1:T(4,128)}, u32[]{:S(2)}) copy-start(f32[8,3]{0,1:T(4,128)} %param.7) | copy-start | bytes 292
  1.4 1.5 %copy-start = (f32[8,12,12,384]{3,0,2,1:T(8,128)S(1)}, f32[8,12,12,384]{3,0,2,1:T(8,128)}, u32[]{:S(2)}) copy-start(f32[8,12,12,384]{3,0,2,1:T(8,128)} %param.4) | copy-start | bytes 5308420
  2.9 14.3 %copy-start.1 = (f32[8,12,12,384]{3,0,2,1:T(8,128)S(1)}, f32[8,12,12,384]{3,0,2,1:T(8,128)}, u32[]{:S(2)}) copy-start(f32[8,12,12,384]{3,0,2,1:T(8,128)} %param.4) | copy-start | bytes 5308420
  3.0 11.6 %collective-permute-start = (f32[37,8,384]{2,1,0:T(8,128)S(1)}, f32[37,8,384]{2,1,0:T(8,128)S(1)}, u32[]{:S(2)}, u32[]{:S(2)}) collective-permute-start(f32[37,8,384]{2,1,0:T(8,128)S(1)} %get-tuple-element.31), channel_id=1, source_target_pairs={{0,2},{4,6},{8,10},{12,14},{16,18},{20,22},{24,26},{28,30},{32,34}... | collective-permute-start | bytes 1363976 | tf_op jit(solution)/shard_map/ppermute | solution.py:447
  5.5 11.5 %collective-permute-start.1 = (f32[37,8,384]{2,1,0:T(8,128)S(1)}, f32[37,8,384]{2,1,0:T(8,128)S(1)}, u32[]{:S(2)}, u32[]{:S(2)}) collective-permute-start(f32[37,8,384]{2,1,0:T(8,128)S(1)} %get-tuple-element.32), channel_id=1, source_target_pairs={{2,4},{6,8},{10,12},{14,16},{18,20},{22,24},{26,28},{30,32},{34,36... | collective-permute-start | bytes 1363976 | tf_op jit(solution)/shard_map/ppermute | solution.py:446
  6.2 10.9 %collective-permute-start.4 = (f32[37,8,384]{2,1,0:T(8,128)S(1)}, f32[37,8,384]{2,1,0:T(8,128)S(1)}, u32[]{:S(2)}, u32[]{:S(2)}) collective-permute-start(f32[37,8,384]{2,1,0:T(8,128)S(1)} %get-tuple-element.34), channel_id=1, source_target_pairs={{0,1},{1,0},{2,3},{3,2},{4,5},{5,4},{6,7},{7,6},{8,9},{9,8},{10,11... | collective-permute-start | bytes 1363976 | tf_op jit(solution)/shard_map/ppermute | solution.py:451
  14.7 8.0 %collective-permute-start.2 = (f32[10,8,384]{2,1,0:T(8,128)S(1)}, f32[10,8,384]{2,1,0:T(8,128)S(1)}, u32[]{:S(2)}, u32[]{:S(2)}) collective-permute-start(f32[10,8,384]{2,1,0:T(8,128)S(1)} %slice.8), channel_id=1, source_target_pairs={{0,1},{1,0},{2,3},{3,2},{4,5},{5,4},{6,7},{7,6},{8,9},{9,8},{10,11... | collective-permute-start | bytes 368648 | tf_op jit(solution)/shard_map/ppermute | solution.py:451
  17.0 5.7 %collective-permute-start.3 = (f32[10,8,384]{2,1,0:T(8,128)S(1)}, f32[10,8,384]{2,1,0:T(8,128)S(1)}, u32[]{:S(2)}, u32[]{:S(2)}) collective-permute-start(f32[10,8,384]{2,1,0:T(8,128)S(1)} %slice.9), channel_id=1, source_target_pairs={{0,1},{1,0},{2,3},{3,2},{4,5},{5,4},{6,7},{7,6},{8,9},{9,8},{10,11... | collective-permute-start | bytes 368648 | tf_op jit(solution)/shard_map/ppermute | solution.py:451
  26.6 20.8 %collective-permute-start.13 = (f32[12,48,384]{2,1,0:T(8,128)S(1)}, f32[12,48,384]{2,1,0:T(8,128)S(1)}, u32[]{:S(2)}, u32[]{:S(2)}) collective-permute-start(f32[12,48,384]{2,1,0:T(8,128)S(1)} %get-tuple-element.45.coef), channel_id=1, source_target_pairs={{0,1},{1,0},{2,3},{3,2},{4,5},{5,4},{6,7},{7,6},{8,9},{9,8},{10,11... | collective-permute-start | bytes 2654216 | tf_op jit(solution)/shard_map/ppermute | solution.py:451
  27.1 10.0 %collective-permute-start.5 = (f32[144,384]{1,0:T(8,128)S(1)}, f32[144,384]{1,0:T(8,128)S(1)}, u32[]{:S(2)}, u32[]{:S(2)}) collective-permute-start(f32[144,384]{1,0:T(8,128)S(1)} %get-tuple-element.41), channel_id=1, source_target_pairs={{0,2},{4,6},{8,10},{12,14},{16,18},{20,22},{24,26},{28,30},{32,34}... | collective-permute-start | bytes 663560 | tf_op jit(solution)/shard_map/ppermute | solution.py:447
  31.8 6.4 %collective-permute-start.6 = (f32[144,384]{1,0:T(8,128)S(1)}, f32[144,384]{1,0:T(8,128)S(1)}, u32[]{:S(2)}, u32[]{:S(2)}) collective-permute-start(f32[144,384]{1,0:T(8,128)S(1)} %get-tuple-element.42), channel_id=1, source_target_pairs={{2,4},{6,8},{10,12},{14,16},{18,20},{22,24},{26,28},{30,32},{34,36... | collective-permute-start | bytes 663560 | tf_op jit(solution)/shard_map/ppermute | solution.py:446
  37.2 14.4 %collective-permute-start.7 = (f32[144,384]{1,0:T(8,128)S(1)}, f32[144,384]{1,0:T(8,128)S(1)}, u32[]{:S(2)}, u32[]{:S(2)}) collective-permute-start(f32[144,384]{1,0:T(8,128)S(1)} %collective-permute-done.5.near), channel_id=1, source_target_pairs={{0,1},{1,0},{2,3},{3,2},{4,5},{5,4},{6,7},{7,6},{8,9},{9,8},{10,11... | collective-permute-start | bytes 663560 | tf_op jit(solution)/shard_map/ppermute | solution.py:451
  38.2 13.5 %collective-permute-start.8 = (f32[144,384]{1,0:T(8,128)S(1)}, f32[144,384]{1,0:T(8,128)S(1)}, u32[]{:S(2)}, u32[]{:S(2)}) collective-permute-start(f32[144,384]{1,0:T(8,128)S(1)} %collective-permute-done.6.far), channel_id=1, source_target_pairs={{0,1},{1,0},{2,3},{3,2},{4,5},{5,4},{6,7},{7,6},{8,9},{9,8},{10,11... | collective-permute-start | bytes 663560 | tf_op jit(solution)/shard_map/ppermute | solution.py:451
  38.2 8.6 %collective-permute-start.9 = (f32[64,384]{1,0:T(8,128)S(1)}, f32[64,384]{1,0:T(8,128)S(1)}, u32[]{:S(2)}, u32[]{:S(2)}) collective-permute-start(f32[64,384]{1,0:T(8,128)S(1)} %get-tuple-element.43), channel_id=1, source_target_pairs={{0,2},{4,6},{8,10},{12,14},{16,18},{20,22},{24,26},{28,30},{32,34}... | collective-permute-start | bytes 294920 | tf_op jit(solution)/shard_map/ppermute | solution.py:447
  43.6 3.8 %collective-permute-start.10 = (f32[64,384]{1,0:T(8,128)S(1)}, f32[64,384]{1,0:T(8,128)S(1)}, u32[]{:S(2)}, u32[]{:S(2)}) collective-permute-start(f32[64,384]{1,0:T(8,128)S(1)} %get-tuple-element.44), channel_id=1, source_target_pairs={{2,4},{6,8},{10,12},{14,16},{18,20},{22,24},{26,28},{30,32},{34,36... | collective-permute-start | bytes 294920 | tf_op jit(solution)/shard_map/ppermute | solution.py:446
  46.8 4.8 %collective-permute-start.11 = (f32[64,384]{1,0:T(8,128)S(1)}, f32[64,384]{1,0:T(8,128)S(1)}, u32[]{:S(2)}, u32[]{:S(2)}) collective-permute-start(f32[64,384]{1,0:T(8,128)S(1)} %collective-permute-done.9.e_near), channel_id=1, source_target_pairs={{0,1},{1,0},{2,3},{3,2},{4,5},{5,4},{6,7},{7,6},{8,9},{9,8},{10,11... | collective-permute-start | bytes 294920 | tf_op jit(solution)/shard_map/ppermute | solution.py:451
  47.4 4.2 %collective-permute-start.12 = (f32[64,384]{1,0:T(8,128)S(1)}, f32[64,384]{1,0:T(8,128)S(1)}, u32[]{:S(2)}, u32[]{:S(2)}) collective-permute-start(f32[64,384]{1,0:T(8,128)S(1)} %collective-permute-done.10.e_far), channel_id=1, source_target_pairs={{0,1},{1,0},{2,3},{3,2},{4,5},{5,4},{6,7},{7,6},{8,9},{9,8},{10,11... | collective-permute-start | bytes 294920 | tf_op jit(solution)/shard_map/ppermute | solution.py:451

commit v7 on v6

--- a/solution.py
+++ b/solution.py
@@ -186,7 +186,7 @@
 
 
 def relax_outer_kernel(
-    near, far, c_near, c_far, mine, across, mix, first_in, second_in, ev_in, coef_in,
+    near, far, corners, mine, across, mix, first_in, second_in, ev_in, coef_in,
     first, second, ev, coef, m_near, m_far, speed, staged, sems,
 ):
     even, odd = parity()
@@ -195,13 +195,13 @@
     other = 1 + B * (1 - slab)
     speed[1, 0] = mine[...]
     speed[1, 1] = across[H * B]
-    for halo, corner, top in ((near, c_near, even), (far, c_far, odd)):
+    for halo, at, top in ((near, 0, even), (far, REST, odd)):
         speed[2 * top, 0] = halo[REST - 1]
-        speed[2 * top, 1] = corner[REST - 1]
+        speed[2 * top, 1] = corners[at + REST - 1]
         for a in range(H):
             for t in range(H):
                 first[(H + B) * top + a, own + (B - H) * (1 - slab) + t] = halo[H * a + t]
-                first[(H + B) * top + a, other + t] = corner[H * a + t]
+                first[(H + B) * top + a, other + t] = corners[at + H * a + t]
             for m in range(B - H):
                 first[(H + B) * top + a, own + H * slab + m] = halo[REST + (B - H) * a + m]
 
@@ -384,32 +384,38 @@
         solver.iterate(t, 2 + t, GO + 2 + t)
         solver.iterate(t, GO + B - 2 - t, N - 2 - t)
 
-    third = lax.broadcasted_iota(jnp.int32, (B, K), 1) % 3
-    target = lax.broadcasted_iota(jnp.int32, (K // 3, K), 0)
-    source = lax.broadcasted_iota(jnp.int32, (K // 3, K), 1) // 3
-    pick = jnp.where(target == source, 1.0, 0.0).astype(jnp.bfloat16)
-    pick = jnp.concatenate([pick, pick], 1)
-    for i in range(B):
-        rows[i, 9 * B :] = jnp.zeros((128 - 9 * B, K), jnp.float32)
-
-    def finish(i):
-        a = i + GO
-        for c, (v, new) in enumerate(solver.advance(ITERS - 1, a)):
-            total = solver.sol[c, i] + v + new
-            mine = jnp.where(bottom, total[:B], total[J - B :])
-            for q in range(3):
-                g = 3 * c + q
-                rows[i, B * g : B * g + B] = jnp.where(third == q, mine, 0.0)
-
-    loop(0, B, finish)
-    for i in range(B):
-        high, low = halves(rows[i])
-        out[pl.ds(i, K // 3, stride=B), :] = lax.dot_general(
-            pick,
-            jnp.concatenate([high, low], 1),
-            (((1,), (1,)), ((), ())),
-            preferred_element_type=jnp.float32,
-        )
+    target = 3 * lax.broadcasted_iota(jnp.int32, (K // 3, K), 0)
+    source = lax.broadcasted_iota(jnp.int32, (K // 3, K), 1)
+    picks = [jnp.where(source == target + q, 1.0, 0.0).astype(jnp.bfloat16) for q in range(3)]
+    picks = [jnp.concatenate([pick, pick], 1) for pick in picks]
+    for g in range(B // 3):
+        rows[g, 9 * B :] = jnp.zeros((128 - 9 * B, K), jnp.float32)
+
+    def finish(g):
+        for p in range(3):
+            i = 3 * g + p
+            for c, (v, new) in enumerate(solver.advance(ITERS - 1, i + GO)):
+                total = solver.sol[c, i] + v + new
+                mine = jnp.where(bottom, total[:B], total[J - B :])
+                at = B * (3 * p + c)
+                rows[g, at : at + B] = mine
+
+    loop(0, B // 3, finish)
+    lane = lax.broadcasted_iota(jnp.int32, (K // 3, 128), 1)
+    for g in range(B // 3):
+        both = jnp.concatenate(halves(rows[g]), 1)
+        parts = [
+            lax.dot_general(
+                pick, both, (((1,), (1,)), ((), ())), preferred_element_type=jnp.float32
+            )
+            for pick in picks
+        ]
+        for p in range(3):
+            moved = [
+                part if q == p else roll(part, 3 * B * (q - p), 1) for q, part in enumerate(parts)
+            ]
+            value = jnp.where(lane < 6 * B, jnp.where(lane < 3 * B, moved[0], moved[1]), moved[2])
+            out[pl.ds(3 * g + p, K // 3, stride=B), :] = value
 
 
 def unpack_kernel(got, out):
@@ -417,7 +423,7 @@
         turned = got[128 * t : 128 * (t + 1), :].T
         for c in range(3):
             for q in range(3):
-                g = 3 * c + q
+                g = 3 * q + c
                 out[c, q, :, 128 * t : 128 * (t + 1)] = turned[B * g : B * g + B]
 
 
@@ -473,15 +479,16 @@
     e_near, e_far = exchange(e_near, e_far)
     oe_near, oe_far = swap(e_near), swap(e_far)
     message = (4 * B * H, K)
+    corners = swap(jnp.concatenate([near[:REST], far[:REST]]))
     first, second, evolved, coef, to_near, to_far = call(
         relax_outer_kernel,
         [block, block, (B, B, F, K), coefs, message, message],
-        [near, far, swap(near[:REST]), swap(far[:REST]), speed, across, mix, first, second, evolved, coef],
+        [near, far, corners, speed, across, mix, first, second, evolved, coef],
         [(3, 2, F, K), (2 * H, B, F, K)],
         grant=4,
-        aliases={7: 0, 8: 1, 9: 2, 10: 3},
+        aliases={6: 0, 7: 1, 8: 2, 9: 3},
         extra=[pltpu.SemaphoreType.DMA((2 * H,))],
-        hbm_in=(9,),
+        hbm_in=(8,),
         hbm_out=(2,),
     )
     o_coef = swap(coef)
@@ -492,7 +499,7 @@
         solve_outer_kernel,
         shapes + [(K // 3 * B, 128)],
         [near, far, swap(near), swap(far), e_near, e_far, oe_near, oe_far, *state],
-        [(B, 128, K)],
+        [(B // 3, 128, K)],
         grant=8,
         aliases={8 + n: n for n in range(13)},
     )[-1]

time: 111 us -> 111 us (level)
    ppermute x8 -> x7, starting transfers between devices: 5.8 us -> 5.24 us  [swap(): return lax.ppermute(array, 'slab', [(0, 1), (1, 0)])]
  transfers between devices with their start and end apart: 14 -> 13, of which waited for: 3 -> 3; matrix products, arithmetic and copies ran while one was open for 0% -> 0% of each run, Pallas kernels for 9% -> 9%
where the time goes in v7:
time: 111 us; the launch traced here: 110 us
  blocking collectives  50.5 us (45%)
  Pallas kernels  22 us (20%)
  starting transfers between devices  20.4 us (18%)
  waiting for transfers between devices  14.5 us (13%)
  local copies, waits for them, and re-layouts  1.5 us (1%)
    all_to_all x1, blocking collectives, program(): arrived = lax.all_to_all(packed, 'space', 0, 0, tiled=True)  50.5 us
    pallas_call x6, Pallas kernels, call(): pl.pallas_call(kernel, out_shape=[s if hasattr(s, 'dtype') else jax.Shape...  22 us
    ppermute x3, waiting for transfers between devices, exchange(): near = lax.ppermute(to_near, 'space', pairs(0))  14.5 us
    ppermute x3, starting transfers between devices, exchange(): near = lax.ppermute(to_near, 'space', pairs(0))  13.2 us
    ppermute x7, starting transfers between devices, swap(): return lax.ppermute(array, 'slab', [(0, 1), (1, 0)])  5.24 us
  transfers between devices with their start and end apart: 13, of which 3 were waited for; matrix products, arithmetic and copies ran while one was open for 0% of the time, Pallas kernels for 9%

profile of v7, /device:TPU:1, one launch (start us, length us, event | category | flops | bytes accessed | tf_op | source)
XLA Modules:
  0.0 110.5 jit_solution(18411949137266488875)
XLA Ops:
  0.6 0.8 fusion.rates
  1.4 1.5 %copy-done = f32[8,12,12,384]{3,0,2,1:T(8,128)S(1)} copy-done((f32[8,12,12,384]{3,0,2,1:T(8,128)S(1)}, f32[8,12,12,384]{3,0,2,1:T(8,128)}, u32[]{:S(2)}) %copy-start) | copy-done | bytes 1769496
  2.9 0.2 shard_map.59
  3.0 2.5 %collective-permute-start = (f32[37,8,384]{2,1,0:T(8,128)S(1)}, f32[37,8,384]{2,1,0:T(8,128)S(1)}, u32[]{:S(2)}, u32[]{:S(2)}) collective-permute-start(f32[37,8,384]{2,1,0:T(8,128)S(1)} %get-tuple-element.31), channel_id=1, source_target_pairs={{0,2},{4,6},{8,10},{12,14},{16,18},{20,22},{24,26},{28,30},{32,34}... | collective-permute-start | bytes 1363976 | tf_op jit(solution)/shard_map/ppermute | solution.py:453
  5.5 0.7 collective-permute-start.1
  6.2 1.2 %collective-permute-start.3 = (f32[37,8,384]{2,1,0:T(8,128)S(1)}, f32[37,8,384]{2,1,0:T(8,128)S(1)}, u32[]{:S(2)}, u32[]{:S(2)}) collective-permute-start(f32[37,8,384]{2,1,0:T(8,128)S(1)} %get-tuple-element.34), channel_id=1, source_target_pairs={{0,1},{1,0},{2,3},{3,2},{4,5},{5,4},{6,7},{7,6},{8,9},{9,8},{10,11... | collective-permute-start | bytes 1363976 | tf_op jit(solution)/shard_map/ppermute | solution.py:457
  7.4 7.3 %collective-permute-done.near = f32[37,8,384]{2,1,0:T(8,128)S(1)} collective-permute-done((f32[37,8,384]{2,1,0:T(8,128)S(1)}, f32[37,8,384]{2,1,0:T(8,128)S(1)}, u32[]{:S(2)}, u32[]{:S(2)}) %collective-permute-start) | collective-permute-done | bytes 454688 | tf_op jit(solution)/shard_map/ppermute | solution.py:453
  14.7 0.0 collective-permute-done.1.far
  14.7 2.4 %collective-permute-start.2 = (f32[20,8,384]{2,1,0:T(8,128)S(1)}, f32[20,8,384]{2,1,0:T(8,128)S(1)}, u32[]{:S(2)}, u32[]{:S(2)}) collective-permute-start(f32[20,8,384]{2,1,0:T(8,128)S(1)} %pad_maximum_fusion), channel_id=1, source_target_pairs={{0,1},{1,0},{2,3},{3,2},{4,5},{5,4},{6,7},{7,6},{8,9},{9,8},{10,11... | collective-permute-start | bytes 737288 | tf_op jit(solution)/shard_map/ppermute | solution.py:457
  17.1 0.0 collective-permute-done.3.across
  17.1 5.5 %shard_map.60 = (f32[18,17,8,384]{3,2,1,0:T(8,128)S(1)}, f32[18,17,8,384]{3,2,1,0:T(8,128)S(1)}, f32[12,12,8,384]{3,2,1,0:T(8,128)}, f32[12,48,384]{2,1,0:T(8,12...) custom-call(f32[12,12,8,384]{3,2,1,0:T(8,128)S(1)} %bitcast.12, ...), custom_call_target="tpu_custom_call" | custom-call | tf_op jit(solution)/shard_map/pallas_call | solution.py:431
  22.6 0.0 collective-permute-done.2.corners
  22.6 3.8 %shard_map.61 = (f32[18,17,8,384]{3,2,1,0:T(8,128)S(1)}, f32[18,17,8,384]{3,2,1,0:T(8,128)S(1)}, f32[12,12,8,384]{3,2,1,0:T(8,128)}, f32[12,48,384]{2,1,0:T(8,12...) custom-call(f32[37,8,384]{2,1,0:T(8,128)S(1)} %collective-permute-do, ...), custom_call_target="tpu_custom_call", output_to_operand_aliasing={{0}: (6, {}), {1}: (7, {}), {2}: (8, {}), {3}: (9, {})} | custom-call | tf_op jit(solution)/shard_map/pallas_call | solution.py:431
  26.5 0.1 collective-permute-start.12
  26.6 5.2 %collective-permute-start.4 = (f32[144,384]{1,0:T(8,128)S(1)}, f32[144,384]{1,0:T(8,128)S(1)}, u32[]{:S(2)}, u32[]{:S(2)}) collective-permute-start(f32[144,384]{1,0:T(8,128)S(1)} %get-tuple-element.41), channel_id=1, source_target_pairs={{0,2},{4,6},{8,10},{12,14},{16,18},{20,22},{24,26},{28,30},{32,34}... | collective-permute-start | bytes 663560 | tf_op jit(solution)/shard_map/ppermute | solution.py:453
  31.8 0.7 collective-permute-start.5
  32.5 4.7 %collective-permute-done.4.near = f32[144,384]{1,0:T(8,128)S(1)} collective-permute-done((f32[144,384]{1,0:T(8,128)S(1)}, f32[144,384]{1,0:T(8,128)S(1)}, u32[]{:S(2)}, u32[]{:S(2)}) %collective-permute-start.4) | collective-permute-done | bytes 221216 | tf_op jit(solution)/shard_map/ppermute | solution.py:453
  37.2 1.0 collective-permute-start.6
  38.2 0.0 collective-permute-start.7
  38.2 5.5 %collective-permute-start.8 = (f32[64,384]{1,0:T(8,128)S(1)}, f32[64,384]{1,0:T(8,128)S(1)}, u32[]{:S(2)}, u32[]{:S(2)}) collective-permute-start(f32[64,384]{1,0:T(8,128)S(1)} %get-tuple-element.43), channel_id=1, source_target_pairs={{0,2},{4,6},{8,10},{12,14},{16,18},{20,22},{24,26},{28,30},{32,34}... | collective-permute-start | bytes 294920 | tf_op jit(solution)/shard_map/ppermute | solution.py:453
  43.7 0.7 collective-permute-start.9
  44.3 2.5 %collective-permute-done.8.e_near = f32[64,384]{1,0:T(8,128)S(1)} collective-permute-done((f32[64,384]{1,0:T(8,128)S(1)}, f32[64,384]{1,0:T(8,128)S(1)}, u32[]{:S(2)}, u32[]{:S(2)}) %collective-permute-start.8) | collective-permute-done | bytes 98336 | tf_op jit(solution)/shard_map/ppermute | solution.py:453
  46.8 0.6 collective-permute-start.10
  47.4 0.0 collective-permute-start.11
  47.4 0.0 collective-permute-done.12.o_coef
  47.4 4.2 %shard_map.62 = (f32[22,16,384]{2,1,0:T(8,128)S(1)}, f32[22,24,384]{2,1,0:T(8,128)S(1)}, f32[22,16,384]{2,1,0:T(8,128)S(1)}, f32[22,16,384]{2,1,0:T(8,128)S(1)},...) custom-call(f32[12,48,384]{2,1,0:T(8,128)S(1)} %get-tuple-element.45, ...), custom_call_target="tpu_custom_call" | custom-call | tf_op jit(solution)/shard_map/pallas_call | solution.py:431
  51.6 0.0 collective-permute-done.10.oe_near
  51.6 0.0 collective-permute-done.11.oe_far
  51.6 0.0 collective-permute-done.7.o_far
  51.7 7.2 %shard_map.63 = (f32[22,16,384]{2,1,0:T(8,128)S(1)}, f32[22,24,384]{2,1,0:T(8,128)S(1)}, f32[22,16,384]{2,1,0:T(8,128)S(1)}, f32[22,16,384]{2,1,0:T(8,128)S(1)},...) custom-call(f32[144,384]{1,0:T(8,128)S(1)} %collective-permute-done., ...), custom_call_target="tpu_custom_call", output_to_operand_aliasing={{0}: (8, {}), {1}: (9, {}), {2}: (10, {}), {3}: (11, {}), {... | custom-call | tf_op jit(solution)/shard_map/pallas_call | solution.py:431
  58.8 50.5 %all_to_all.5 = f32[128,1,1536]{2,1,0:T(1,128)S(1)} all-to-all(f32[128,1,1536]{2,1,0:T(1,128)S(1)} %bitcast.14), channel_id=1, replica_groups=mesh['space'=128,'slab'=2] {'space'}, dimensions={0} | all-to-all | bytes 1572864 | tf_op jit(solution)/shard_map/all_to_all | solution.py:507
  109.3 1.2 %shard_map.64 = f32[3,3,12,1536]{3,2,1,0:T(8,128)} custom-call(f32[1536,128]{1,0:T(8,128)S(1)} %bitcast.13), custom_call_target="tpu_custom_call" | custom-call | tf_op jit(solution)/shard_map/pallas_call | solution.py:431
  (11 shorter events, 0.1 us)
Async XLA Ops:
  0.6 16.5 %copy-start.2 = (f32[8,3]{0,1:T(4,128)S(1)}, f32[8,3]{0,1:T(4,128)}, u32[]{:S(2)}) copy-start(f32[8,3]{0,1:T(4,128)} %param.7) | copy-start | bytes 292
  1.4 1.5 %copy-start = (f32[8,12,12,384]{3,0,2,1:T(8,128)S(1)}, f32[8,12,12,384]{3,0,2,1:T(8,128)}, u32[]{:S(2)}) copy-start(f32[8,12,12,384]{3,0,2,1:T(8,128)} %param.4) | copy-start | bytes 5308420
  2.9 14.2 %copy-start.1 = (f32[8,12,12,384]{3,0,2,1:T(8,128)S(1)}, f32[8,12,12,384]{3,0,2,1:T(8,128)}, u32[]{:S(2)}) copy-start(f32[8,12,12,384]{3,0,2,1:T(8,128)} %param.4) | copy-start | bytes 5308420
  3.0 11.6 %collective-permute-start = (f32[37,8,384]{2,1,0:T(8,128)S(1)}, f32[37,8,384]{2,1,0:T(8,128)S(1)}, u32[]{:S(2)}, u32[]{:S(2)}) collective-permute-start(f32[37,8,384]{2,1,0:T(8,128)S(1)} %get-tuple-element.31), channel_id=1, source_target_pairs={{0,2},{4,6},{8,10},{12,14},{16,18},{20,22},{24,26},{28,30},{32,34}... | collective-permute-start | bytes 1363976 | tf_op jit(solution)/shard_map/ppermute | solution.py:453
  5.5 9.1 %collective-permute-start.1 = (f32[37,8,384]{2,1,0:T(8,128)S(1)}, f32[37,8,384]{2,1,0:T(8,128)S(1)}, u32[]{:S(2)}, u32[]{:S(2)}) collective-permute-start(f32[37,8,384]{2,1,0:T(8,128)S(1)} %get-tuple-element.32), channel_id=1, source_target_pairs={{2,4},{6,8},{10,12},{14,16},{18,20},{22,24},{26,28},{30,32},{34,36... | collective-permute-start | bytes 1363976 | tf_op jit(solution)/shard_map/ppermute | solution.py:452
  6.2 10.9 %collective-permute-start.3 = (f32[37,8,384]{2,1,0:T(8,128)S(1)}, f32[37,8,384]{2,1,0:T(8,128)S(1)}, u32[]{:S(2)}, u32[]{:S(2)}) collective-permute-start(f32[37,8,384]{2,1,0:T(8,128)S(1)} %get-tuple-element.34), channel_id=1, source_target_pairs={{0,1},{1,0},{2,3},{3,2},{4,5},{5,4},{6,7},{7,6},{8,9},{9,8},{10,11... | collective-permute-start | bytes 1363976 | tf_op jit(solution)/shard_map/ppermute | solution.py:457
  14.7 7.9 %collective-permute-start.2 = (f32[20,8,384]{2,1,0:T(8,128)S(1)}, f32[20,8,384]{2,1,0:T(8,128)S(1)}, u32[]{:S(2)}, u32[]{:S(2)}) collective-permute-start(f32[20,8,384]{2,1,0:T(8,128)S(1)} %pad_maximum_fusion), channel_id=1, source_target_pairs={{0,1},{1,0},{2,3},{3,2},{4,5},{5,4},{6,7},{7,6},{8,9},{9,8},{10,11... | collective-permute-start | bytes 737288 | tf_op jit(solution)/shard_map/ppermute | solution.py:457
  26.5 20.9 %collective-permute-start.12 = (f32[12,48,384]{2,1,0:T(8,128)S(1)}, f32[12,48,384]{2,1,0:T(8,128)S(1)}, u32[]{:S(2)}, u32[]{:S(2)}) collective-permute-start(f32[12,48,384]{2,1,0:T(8,128)S(1)} %get-tuple-element.45.coef), channel_id=1, source_target_pairs={{0,1},{1,0},{2,3},{3,2},{4,5},{5,4},{6,7},{7,6},{8,9},{9,8},{10,11... | collective-permute-start | bytes 2654216 | tf_op jit(solution)/shard_map/ppermute | solution.py:457
  26.6 10.6 %collective-permute-start.4 = (f32[144,384]{1,0:T(8,128)S(1)}, f32[144,384]{1,0:T(8,128)S(1)}, u32[]{:S(2)}, u32[]{:S(2)}) collective-permute-start(f32[144,384]{1,0:T(8,128)S(1)} %get-tuple-element.41), channel_id=1, source_target_pairs={{0,2},{4,6},{8,10},{12,14},{16,18},{20,22},{24,26},{28,30},{32,34}... | collective-permute-start | bytes 663560 | tf_op jit(solution)/shard_map/ppermute | solution.py:453
  31.8 6.4 %collective-permute-start.5 = (f32[144,384]{1,0:T(8,128)S(1)}, f32[144,384]{1,0:T(8,128)S(1)}, u32[]{:S(2)}, u32[]{:S(2)}) collective-permute-start(f32[144,384]{1,0:T(8,128)S(1)} %get-tuple-element.42), channel_id=1, source_target_pairs={{2,4},{6,8},{10,12},{14,16},{18,20},{22,24},{26,28},{30,32},{34,36... | collective-permute-start | bytes 663560 | tf_op jit(solution)/shard_map/ppermute | solution.py:452
  37.2 14.4 %collective-permute-start.6 = (f32[144,384]{1,0:T(8,128)S(1)}, f32[144,384]{1,0:T(8,128)S(1)}, u32[]{:S(2)}, u32[]{:S(2)}) collective-permute-start(f32[144,384]{1,0:T(8,128)S(1)} %collective-permute-done.4.near), channel_id=1, source_target_pairs={{0,1},{1,0},{2,3},{3,2},{4,5},{5,4},{6,7},{7,6},{8,9},{9,8},{10,11... | collective-permute-start | bytes 663560 | tf_op jit(solution)/shard_map/ppermute | solution.py:457
  38.2 13.5 %collective-permute-start.7 = (f32[144,384]{1,0:T(8,128)S(1)}, f32[144,384]{1,0:T(8,128)S(1)}, u32[]{:S(2)}, u32[]{:S(2)}) collective-permute-start(f32[144,384]{1,0:T(8,128)S(1)} %collective-permute-done.5.far), channel_id=1, source_target_pairs={{0,1},{1,0},{2,3},{3,2},{4,5},{5,4},{6,7},{7,6},{8,9},{9,8},{10,11... | collective-permute-start | bytes 663560 | tf_op jit(solution)/shard_map/ppermute | solution.py:457
  38.2 8.6 %collective-permute-start.8 = (f32[64,384]{1,0:T(8,128)S(1)}, f32[64,384]{1,0:T(8,128)S(1)}, u32[]{:S(2)}, u32[]{:S(2)}) collective-permute-start(f32[64,384]{1,0:T(8,128)S(1)} %get-tuple-element.43), channel_id=1, source_target_pairs={{0,2},{4,6},{8,10},{12,14},{16,18},{20,22},{24,26},{28,30},{32,34}... | collective-permute-start | bytes 294920 | tf_op jit(solution)/shard_map/ppermute | solution.py:453
  43.7 3.8 %collective-permute-start.9 = (f32[64,384]{1,0:T(8,128)S(1)}, f32[64,384]{1,0:T(8,128)S(1)}, u32[]{:S(2)}, u32[]{:S(2)}) collective-permute-start(f32[64,384]{1,0:T(8,128)S(1)} %get-tuple-element.44), channel_id=1, source_target_pairs={{2,4},{6,8},{10,12},{14,16},{18,20},{22,24},{26,28},{30,32},{34,36... | collective-permute-start | bytes 294920 | tf_op jit(solution)/shard_map/ppermute | solution.py:452
  46.8 4.8 %collective-permute-start.10 = (f32[64,384]{1,0:T(8,128)S(1)}, f32[64,384]{1,0:T(8,128)S(1)}, u32[]{:S(2)}, u32[]{:S(2)}) collective-permute-start(f32[64,384]{1,0:T(8,128)S(1)} %collective-permute-done.8.e_near), channel_id=1, source_target_pairs={{0,1},{1,0},{2,3},{3,2},{4,5},{5,4},{6,7},{7,6},{8,9},{9,8},{10,11... | collective-permute-start | bytes 294920 | tf_op jit(solution)/shard_map/ppermute | solution.py:457
  47.4 4.2 %collective-permute-start.11 = (f32[64,384]{1,0:T(8,128)S(1)}, f32[64,384]{1,0:T(8,128)S(1)}, u32[]{:S(2)}, u32[]{:S(2)}) collective-permute-start(f32[64,384]{1,0:T(8,128)S(1)} %collective-permute-done.9.e_far), channel_id=1, source_target_pairs={{0,1},{1,0},{2,3},{3,2},{4,5},{5,4},{6,7},{7,6},{8,9},{9,8},{10,11... | collective-permute-start | bytes 294920 | tf_op jit(solution)/shard_map/ppermute | solution.py:457

commit v8 on v7

--- a/solution.py
+++ b/solution.py
@@ -318,7 +318,7 @@
             out.append((v, new - past * dst[c, a] if t else new))
         return out
 
-    def iterate(self, t, start, stop):
+    def iterate(self, t, start, stop, static=False):
         dst = self.buffers(t)[1]
 
         def plane(a, inner):
@@ -328,13 +328,16 @@
                     self.sol[c, a - GO] = v if t == 0 else self.sol[c, a - GO] + v
 
         low, high = min(max(start, GO), stop), max(min(stop, GO + B), start)
-        loop(start, low, lambda a: plane(a, False))
-        loop(low, high, lambda a: plane(a, True))
-        loop(high, stop, lambda a: plane(a, False))
-
-
-def loop(start, stop, body):
-    if start < stop:
+        loop(start, low, lambda a: plane(a, False), static)
+        loop(low, high, lambda a: plane(a, True), static)
+        loop(high, stop, lambda a: plane(a, False), static)
+
+
+def loop(start, stop, body, static=False):
+    if static:
+        for a in range(start, stop):
+            body(a)
+    elif start < stop:
         lax.fori_loop(start, stop, lambda a, _: (body(a), 0)[1], 0)
 
 
@@ -366,11 +369,11 @@
         solver.put(1 + (N - 3) * top, early[whole], others_early[whole])
         solver.s0[(N - 1) * top] = solver.window(joined(early[tail], others_early[tail])[0])
 
-    loop(1, GO + 1, solver.force)
-    loop(GO + B - 1, N - 1, solver.force)
+    loop(1, GO + 1, solver.force, True)
+    loop(GO + B - 1, N - 1, solver.force, True)
     solver.wi[1] = 1.0 + 0.5 * (solver.ex[1] + solver.ex[2])
-    loop(2, GO + 1, solver.weigh)
-    loop(GO + B - 1, N - 2, solver.weigh)
+    loop(2, GO + 1, solver.weigh, True)
+    loop(GO + B - 1, N - 2, solver.weigh, True)
 
     @pl.when(place == 0)
     def _():
@@ -381,8 +384,8 @@
         solver.wi[GO + B - 1] = jnp.zeros((J, K), jnp.float32)
 
     for t in range(ITERS - 1):
-        solver.iterate(t, 2 + t, GO + 2 + t)
-        solver.iterate(t, GO + B - 2 - t, N - 2 - t)
+        solver.iterate(t, 2 + t, GO + 2 + t, True)
+        solver.iterate(t, GO + B - 2 - t, N - 2 - t, True)
 
     target = 3 * lax.broadcasted_iota(jnp.int32, (K // 3, K), 0)
     source = lax.broadcasted_iota(jnp.int32, (K // 3, K), 1)
@@ -400,7 +403,7 @@
                 at = B * (3 * p + c)
                 rows[g, at : at + B] = mine
 
-    loop(0, B // 3, finish)
+    loop(0, B // 3, finish, True)
     lane = lax.broadcasted_iota(jnp.int32, (K // 3, 128), 1)
     for g in range(B // 3):
         both = jnp.concatenate(halves(rows[g]), 1)

time: 111 us -> 108 us (0.973)
  Pallas kernels: 22 us -> 19.2 us
    pallas_call x6, Pallas kernels: 22 us -> 19.2 us  [call(): pl.pallas_call(kernel, out_shape=[s if hasattr(s, 'dtype') else jax.Shape...]
where the time goes in v8:
time: 108 us
  blocking collectives  50.5 us (47%)
  starting transfers between devices  20.4 us (19%)
  Pallas kernels  19.2 us (18%)
  waiting for transfers between devices  14.5 us (13%)
  local copies, waits for them, and re-layouts  1.5 us (1%)
    all_to_all x1, blocking collectives, program(): arrived = lax.all_to_all(packed, 'space', 0, 0, tiled=True)  50.5 us
    pallas_call x6, Pallas kernels, call(): pl.pallas_call(kernel, out_shape=[s if hasattr(s, 'dtype') else jax.Shape...  19.2 us
    ppermute x3, waiting for transfers between devices, exchange(): near = lax.ppermute(to_near, 'space', pairs(0))  14.5 us
    ppermute x3, starting transfers between devices, exchange(): near = lax.ppermute(to_near, 'space', pairs(0))  13.1 us
    ppermute x7, starting transfers between devices, swap(): return lax.ppermute(array, 'slab', [(0, 1), (1, 0)])  5.24 us
  transfers between devices with their start and end apart: 13, of which 3 were waited for; matrix products, arithmetic and copies ran while one was open for 0% of the time, Pallas kernels for 9%

profile of v8, /device:TPU:1, one launch (start us, length us, event | category | flops | bytes accessed | tf_op | source)
XLA Modules:
  0.0 107.6 jit_solution(5266189773130048759)
XLA Ops:
  0.6 0.8 fusion.rates
  1.4 1.5 %copy-done = f32[8,12,12,384]{3,0,2,1:T(8,128)S(1)} copy-done((f32[8,12,12,384]{3,0,2,1:T(8,128)S(1)}, f32[8,12,12,384]{3,0,2,1:T(8,128)}, u32[]{:S(2)}) %copy-start) | copy-done | bytes 1769496
  2.9 0.2 shard_map.59
  3.0 2.5 %collective-permute-start = (f32[37,8,384]{2,1,0:T(8,128)S(1)}, f32[37,8,384]{2,1,0:T(8,128)S(1)}, u32[]{:S(2)}, u32[]{:S(2)}) collective-permute-start(f32[37,8,384]{2,1,0:T(8,128)S(1)} %get-tuple-element.31), channel_id=1, source_target_pairs={{0,2},{4,6},{8,10},{12,14},{16,18},{20,22},{24,26},{28,30},{32,34}... | collective-permute-start | bytes 1363976 | tf_op jit(solution)/shard_map/ppermute | solution.py:456
  5.5 0.7 collective-permute-start.1
  6.2 1.2 %collective-permute-start.3 = (f32[37,8,384]{2,1,0:T(8,128)S(1)}, f32[37,8,384]{2,1,0:T(8,128)S(1)}, u32[]{:S(2)}, u32[]{:S(2)}) collective-permute-start(f32[37,8,384]{2,1,0:T(8,128)S(1)} %get-tuple-element.34), channel_id=1, source_target_pairs={{0,1},{1,0},{2,3},{3,2},{4,5},{5,4},{6,7},{7,6},{8,9},{9,8},{10,11... | collective-permute-start | bytes 1363976 | tf_op jit(solution)/shard_map/ppermute | solution.py:460
  7.4 7.3 %collective-permute-done.near = f32[37,8,384]{2,1,0:T(8,128)S(1)} collective-permute-done((f32[37,8,384]{2,1,0:T(8,128)S(1)}, f32[37,8,384]{2,1,0:T(8,128)S(1)}, u32[]{:S(2)}, u32[]{:S(2)}) %collective-permute-start) | collective-permute-done | bytes 454688 | tf_op jit(solution)/shard_map/ppermute | solution.py:456
  14.7 0.0 collective-permute-done.1.far
  14.7 2.4 %collective-permute-start.2 = (f32[20,8,384]{2,1,0:T(8,128)S(1)}, f32[20,8,384]{2,1,0:T(8,128)S(1)}, u32[]{:S(2)}, u32[]{:S(2)}) collective-permute-start(f32[20,8,384]{2,1,0:T(8,128)S(1)} %pad_maximum_fusion), channel_id=1, source_target_pairs={{0,1},{1,0},{2,3},{3,2},{4,5},{5,4},{6,7},{7,6},{8,9},{9,8},{10,11... | collective-permute-start | bytes 737288 | tf_op jit(solution)/shard_map/ppermute | solution.py:460
  17.1 0.0 collective-permute-done.3.across
  17.1 5.5 %shard_map.60 = (f32[18,17,8,384]{3,2,1,0:T(8,128)S(1)}, f32[18,17,8,384]{3,2,1,0:T(8,128)S(1)}, f32[12,12,8,384]{3,2,1,0:T(8,128)}, f32[12,48,384]{2,1,0:T(8,12...) custom-call(f32[12,12,8,384]{3,2,1,0:T(8,128)S(1)} %bitcast.12, ...), custom_call_target="tpu_custom_call" | custom-call | tf_op jit(solution)/shard_map/pallas_call | solution.py:434
  22.6 0.0 collective-permute-done.2.corners
  22.6 3.8 %shard_map.61 = (f32[18,17,8,384]{3,2,1,0:T(8,128)S(1)}, f32[18,17,8,384]{3,2,1,0:T(8,128)S(1)}, f32[12,12,8,384]{3,2,1,0:T(8,128)}, f32[12,48,384]{2,1,0:T(8,12...) custom-call(f32[37,8,384]{2,1,0:T(8,128)S(1)} %collective-permute-do, ...), custom_call_target="tpu_custom_call", output_to_operand_aliasing={{0}: (6, {}), {1}: (7, {}), {2}: (8, {}), {3}: (9, {})} | custom-call | tf_op jit(solution)/shard_map/pallas_call | solution.py:434
  26.5 0.1 collective-permute-start.12
  26.6 5.2 %collective-permute-start.4 = (f32[144,384]{1,0:T(8,128)S(1)}, f32[144,384]{1,0:T(8,128)S(1)}, u32[]{:S(2)}, u32[]{:S(2)}) collective-permute-start(f32[144,384]{1,0:T(8,128)S(1)} %get-tuple-element.41), channel_id=1, source_target_pairs={{0,2},{4,6},{8,10},{12,14},{16,18},{20,22},{24,26},{28,30},{32,34}... | collective-permute-start | bytes 663560 | tf_op jit(solution)/shard_map/ppermute | solution.py:456
  31.8 0.7 collective-permute-start.5
  32.5 4.7 %collective-permute-done.4.near = f32[144,384]{1,0:T(8,128)S(1)} collective-permute-done((f32[144,384]{1,0:T(8,128)S(1)}, f32[144,384]{1,0:T(8,128)S(1)}, u32[]{:S(2)}, u32[]{:S(2)}) %collective-permute-start.4) | collective-permute-done | bytes 221216 | tf_op jit(solution)/shard_map/ppermute | solution.py:456
  37.2 1.0 collective-permute-start.6
  38.2 0.0 collective-permute-done.5.far
  38.2 0.0 collective-permute-start.7
  38.2 5.5 %collective-permute-start.8 = (f32[64,384]{1,0:T(8,128)S(1)}, f32[64,384]{1,0:T(8,128)S(1)}, u32[]{:S(2)}, u32[]{:S(2)}) collective-permute-start(f32[64,384]{1,0:T(8,128)S(1)} %get-tuple-element.43), channel_id=1, source_target_pairs={{0,2},{4,6},{8,10},{12,14},{16,18},{20,22},{24,26},{28,30},{32,34}... | collective-permute-start | bytes 294920 | tf_op jit(solution)/shard_map/ppermute | solution.py:456
  43.7 0.7 collective-permute-start.9
  44.3 2.5 %collective-permute-done.8.e_near = f32[64,384]{1,0:T(8,128)S(1)} collective-permute-done((f32[64,384]{1,0:T(8,128)S(1)}, f32[64,384]{1,0:T(8,128)S(1)}, u32[]{:S(2)}, u32[]{:S(2)}) %collective-permute-start.8) | collective-permute-done | bytes 98336 | tf_op jit(solution)/shard_map/ppermute | solution.py:456
  46.8 0.6 collective-permute-start.10
  47.4 0.0 collective-permute-start.11
  47.4 0.0 collective-permute-done.12.o_coef
  47.4 4.2 %shard_map.62 = (f32[22,16,384]{2,1,0:T(8,128)S(1)}, f32[22,24,384]{2,1,0:T(8,128)S(1)}, f32[22,16,384]{2,1,0:T(8,128)S(1)}, f32[22,16,384]{2,1,0:T(8,128)S(1)},...) custom-call(f32[12,48,384]{2,1,0:T(8,128)S(1)} %get-tuple-element.45, ...), custom_call_target="tpu_custom_call" | custom-call | tf_op jit(solution)/shard_map/pallas_call | solution.py:434
  51.6 0.0 collective-permute-done.10.oe_near
  51.6 0.0 collective-permute-done.11.oe_far
  51.6 4.3 %shard_map.63 = (f32[22,16,384]{2,1,0:T(8,128)S(1)}, f32[22,24,384]{2,1,0:T(8,128)S(1)}, f32[22,16,384]{2,1,0:T(8,128)S(1)}, f32[22,16,384]{2,1,0:T(8,128)S(1)},...) custom-call(f32[144,384]{1,0:T(8,128)S(1)} %collective-permute-done., ...), custom_call_target="tpu_custom_call", output_to_operand_aliasing={{0}: (8, {}), {1}: (9, {}), {2}: (10, {}), {3}: (11, {}), {... | custom-call | tf_op jit(solution)/shard_map/pallas_call | solution.py:434
  56.0 50.5 %all_to_all.5 = f32[128,1,1536]{2,1,0:T(1,128)S(1)} all-to-all(f32[128,1,1536]{2,1,0:T(1,128)S(1)} %bitcast.14), channel_id=1, replica_groups=mesh['space'=128,'slab'=2] {'space'}, dimensions={0} | all-to-all | bytes 1572864 | tf_op jit(solution)/shard_map/all_to_all | solution.py:510
  106.4 1.2 %shard_map.64 = f32[3,3,12,1536]{3,2,1,0:T(8,128)} custom-call(f32[1536,128]{1,0:T(8,128)S(1)} %bitcast.13), custom_call_target="tpu_custom_call" | custom-call | tf_op jit(solution)/shard_map/pallas_call | solution.py:434
  (11 shorter events, 0.1 us)
Async XLA Ops:
  0.6 16.5 %copy-start.2 = (f32[8,3]{0,1:T(4,128)S(1)}, f32[8,3]{0,1:T(4,128)}, u32[]{:S(2)}) copy-start(f32[8,3]{0,1:T(4,128)} %param.7) | copy-start | bytes 292
  1.4 1.5 %copy-start = (f32[8,12,12,384]{3,0,2,1:T(8,128)S(1)}, f32[8,12,12,384]{3,0,2,1:T(8,128)}, u32[]{:S(2)}) copy-start(f32[8,12,12,384]{3,0,2,1:T(8,128)} %param.4) | copy-start | bytes 5308420
  2.9 14.2 %copy-start.1 = (f32[8,12,12,384]{3,0,2,1:T(8,128)S(1)}, f32[8,12,12,384]{3,0,2,1:T(8,128)}, u32[]{:S(2)}) copy-start(f32[8,12,12,384]{3,0,2,1:T(8,128)} %param.4) | copy-start | bytes 5308420
  3.0 11.6 %collective-permute-start = (f32[37,8,384]{2,1,0:T(8,128)S(1)}, f32[37,8,384]{2,1,0:T(8,128)S(1)}, u32[]{:S(2)}, u32[]{:S(2)}) collective-permute-start(f32[37,8,384]{2,1,0:T(8,128)S(1)} %get-tuple-element.31), channel_id=1, source_target_pairs={{0,2},{4,6},{8,10},{12,14},{16,18},{20,22},{24,26},{28,30},{32,34}... | collective-permute-start | bytes 1363976 | tf_op jit(solution)/shard_map/ppermute | solution.py:456
  5.5 9.1 %collective-permute-start.1 = (f32[37,8,384]{2,1,0:T(8,128)S(1)}, f32[37,8,384]{2,1,0:T(8,128)S(1)}, u32[]{:S(2)}, u32[]{:S(2)}) collective-permute-start(f32[37,8,384]{2,1,0:T(8,128)S(1)} %get-tuple-element.32), channel_id=1, source_target_pairs={{2,4},{6,8},{10,12},{14,16},{18,20},{22,24},{26,28},{30,32},{34,36... | collective-permute-start | bytes 1363976 | tf_op jit(solution)/shard_map/ppermute | solution.py:455
  6.2 10.9 %collective-permute-start.3 = (f32[37,8,384]{2,1,0:T(8,128)S(1)}, f32[37,8,384]{2,1,0:T(8,128)S(1)}, u32[]{:S(2)}, u32[]{:S(2)}) collective-permute-start(f32[37,8,384]{2,1,0:T(8,128)S(1)} %get-tuple-element.34), channel_id=1, source_target_pairs={{0,1},{1,0},{2,3},{3,2},{4,5},{5,4},{6,7},{7,6},{8,9},{9,8},{10,11... | collective-permute-start | bytes 1363976 | tf_op jit(solution)/shard_map/ppermute | solution.py:460
  14.7 7.9 %collective-permute-start.2 = (f32[20,8,384]{2,1,0:T(8,128)S(1)}, f32[20,8,384]{2,1,0:T(8,128)S(1)}, u32[]{:S(2)}, u32[]{:S(2)}) collective-permute-start(f32[20,8,384]{2,1,0:T(8,128)S(1)} %pad_maximum_fusion), channel_id=1, source_target_pairs={{0,1},{1,0},{2,3},{3,2},{4,5},{5,4},{6,7},{7,6},{8,9},{9,8},{10,11... | collective-permute-start | bytes 737288 | tf_op jit(solution)/shard_map/ppermute | solution.py:460
  26.5 20.9 %collective-permute-start.12 = (f32[12,48,384]{2,1,0:T(8,128)S(1)}, f32[12,48,384]{2,1,0:T(8,128)S(1)}, u32[]{:S(2)}, u32[]{:S(2)}) collective-permute-start(f32[12,48,384]{2,1,0:T(8,128)S(1)} %get-tuple-element.45.coef), channel_id=1, source_target_pairs={{0,1},{1,0},{2,3},{3,2},{4,5},{5,4},{6,7},{7,6},{8,9},{9,8},{10,11... | collective-permute-start | bytes 2654216 | tf_op jit(solution)/shard_map/ppermute | solution.py:460
  26.6 10.6 %collective-permute-start.4 = (f32[144,384]{1,0:T(8,128)S(1)}, f32[144,384]{1,0:T(8,128)S(1)}, u32[]{:S(2)}, u32[]{:S(2)}) collective-permute-start(f32[144,384]{1,0:T(8,128)S(1)} %get-tuple-element.41), channel_id=1, source_target_pairs={{0,2},{4,6},{8,10},{12,14},{16,18},{20,22},{24,26},{28,30},{32,34}... | collective-permute-start | bytes 663560 | tf_op jit(solution)/shard_map/ppermute | solution.py:456
  31.8 6.4 %collective-permute-start.5 = (f32[144,384]{1,0:T(8,128)S(1)}, f32[144,384]{1,0:T(8,128)S(1)}, u32[]{:S(2)}, u32[]{:S(2)}) collective-permute-start(f32[144,384]{1,0:T(8,128)S(1)} %get-tuple-element.42), channel_id=1, source_target_pairs={{2,4},{6,8},{10,12},{14,16},{18,20},{22,24},{26,28},{30,32},{34,36... | collective-permute-start | bytes 663560 | tf_op jit(solution)/shard_map/ppermute | solution.py:455
  37.2 14.4 %collective-permute-start.6 = (f32[144,384]{1,0:T(8,128)S(1)}, f32[144,384]{1,0:T(8,128)S(1)}, u32[]{:S(2)}, u32[]{:S(2)}) collective-permute-start(f32[144,384]{1,0:T(8,128)S(1)} %collective-permute-done.4.near), channel_id=1, source_target_pairs={{0,1},{1,0},{2,3},{3,2},{4,5},{5,4},{6,7},{7,6},{8,9},{9,8},{10,11... | collective-permute-start | bytes 663560 | tf_op jit(solution)/shard_map/ppermute | solution.py:460
  38.2 13.5 %collective-permute-start.7 = (f32[144,384]{1,0:T(8,128)S(1)}, f32[144,384]{1,0:T(8,128)S(1)}, u32[]{:S(2)}, u32[]{:S(2)}) collective-permute-start(f32[144,384]{1,0:T(8,128)S(1)} %collective-permute-done.5.far), channel_id=1, source_target_pairs={{0,1},{1,0},{2,3},{3,2},{4,5},{5,4},{6,7},{7,6},{8,9},{9,8},{10,11... | collective-permute-start | bytes 663560 | tf_op jit(solution)/shard_map/ppermute | solution.py:460
  38.2 8.6 %collective-permute-start.8 = (f32[64,384]{1,0:T(8,128)S(1)}, f32[64,384]{1,0:T(8,128)S(1)}, u32[]{:S(2)}, u32[]{:S(2)}) collective-permute-start(f32[64,384]{1,0:T(8,128)S(1)} %get-tuple-element.43), channel_id=1, source_target_pairs={{0,2},{4,6},{8,10},{12,14},{16,18},{20,22},{24,26},{28,30},{32,34}... | collective-permute-start | bytes 294920 | tf_op jit(solution)/shard_map/ppermute | solution.py:456
  43.7 3.8 %collective-permute-start.9 = (f32[64,384]{1,0:T(8,128)S(1)}, f32[64,384]{1,0:T(8,128)S(1)}, u32[]{:S(2)}, u32[]{:S(2)}) collective-permute-start(f32[64,384]{1,0:T(8,128)S(1)} %get-tuple-element.44), channel_id=1, source_target_pairs={{2,4},{6,8},{10,12},{14,16},{18,20},{22,24},{26,28},{30,32},{34,36... | collective-permute-start | bytes 294920 | tf_op jit(solution)/shard_map/ppermute | solution.py:455
  46.8 4.8 %collective-permute-start.10 = (f32[64,384]{1,0:T(8,128)S(1)}, f32[64,384]{1,0:T(8,128)S(1)}, u32[]{:S(2)}, u32[]{:S(2)}) collective-permute-start(f32[64,384]{1,0:T(8,128)S(1)} %collective-permute-done.8.e_near), channel_id=1, source_target_pairs={{0,1},{1,0},{2,3},{3,2},{4,5},{5,4},{6,7},{7,6},{8,9},{9,8},{10,11... | collective-permute-start | bytes 294920 | tf_op jit(solution)/shard_map/ppermute | solution.py:460
  47.4 4.2 %collective-permute-start.11 = (f32[64,384]{1,0:T(8,128)S(1)}, f32[64,384]{1,0:T(8,128)S(1)}, u32[]{:S(2)}, u32[]{:S(2)}) collective-permute-start(f32[64,384]{1,0:T(8,128)S(1)} %collective-permute-done.9.e_far), channel_id=1, source_target_pairs={{0,1},{1,0},{2,3},{3,2},{4,5},{5,4},{6,7},{7,6},{8,9},{9,8},{10,11... | collective-permute-start | bytes 294920 | tf_op jit(solution)/shard_map/ppermute | solution.py:460

commit v9 on v8

--- a/solution.py
+++ b/solution.py
@@ -68,12 +68,12 @@
     return x - s * (x * (5.0 + 3.0 * total - 2.0 * square) - summed)
 
 
-def window_step(src, dst, speed, depth, count, place):
+def window_step(src, dst, speed, depth, count, place, static=False):
     slab = lax.axis_index("slab")
 
-    def plane(n, _):
+    def plane(n):
         a = place(n)
-        group = (a >= H).astype(jnp.int32) + (a >= H + B).astype(jnp.int32)
+        group = (a >= H) * 1 + (a >= H + B) * 1
         edge = depth * slab
         before = src[a, edge]
         x = src[a, edge + 1]
@@ -83,9 +83,8 @@
             around = (before + after) + (src[a - 1, edge + w + 1] + src[a + 1, edge + w + 1])
             dst[a, edge + w + 1] = update(x, around, speed[group, whose])
             before, x = x, after
-        return 0
-
-    lax.fori_loop(0, count, plane, 0)
+
+    loop(0, count, plane, static)
 
 
 def halves(x):
@@ -93,12 +92,12 @@
     return high, (x - high.astype(jnp.float32)).astype(jnp.bfloat16)
 
 
-def last_step(src, own_speed, mix, ev, coef, count, place, staged, sems):
+def last_step(src, own_speed, mix, ev, coef, count, place, staged, sems, static=False):
     own = 1 + H * lax.axis_index("slab")
     row = lax.broadcasted_iota(jnp.int32, (4 * B, K), 0)
     is_excess = (row >= B) & (row < 2 * B)
 
-    def plane(n, _):
+    def plane(n):
         a = place(n)
         before = src[a, own - 1]
         x = src[a, own]
@@ -108,9 +107,8 @@
             staged[n, j] = update(x, around, own_speed[...])
             before, x = x, after
         pltpu.make_async_copy(staged.at[n], ev.at[a - H], sems.at[n]).start()
-        return 0
-
-    lax.fori_loop(0, count, plane, 0)
+
+    loop(0, count, plane, static)
     for n in range(count):
         values = staged[n].reshape(B * F, K)
         high, low = halves(values * values)
@@ -209,9 +207,9 @@
         jump = B + H - 2 * depth - 1
         return lambda n: depth + n + (jump + 1 - H) * (n >= H)
 
-    window_step(first, second, speed, 1, 2 * H, ends(1))
-    window_step(second, first, speed, 2, 2 * H, ends(2))
-    last_step(first, speed.at[1, 0], mix, ev, coef, 2 * H, ends(3), staged, sems)
+    window_step(first, second, speed, 1, 2 * H, ends(1), True)
+    window_step(second, first, speed, 2, 2 * H, ends(2), True)
+    last_step(first, speed.at[1, 0], mix, ev, coef, 2 * H, ends(3), staged, sems, True)
     for message, top in ((m_near, even), (m_far, odd)):
         for t in range(H):
             message[4 * B * t : 4 * B * (t + 1)] = coef[(B - H) * top + t]

time: 108 us -> 108 us (level)
  no operation moved by 1% of the time
where the time goes in v9:
time: 108 us; the launch traced here: 107 us
  blocking collectives  50.5 us (47%)
  starting transfers between devices  20.4 us (19%)
  Pallas kernels  18.9 us (17%)
  waiting for transfers between devices  14.5 us (13%)
  local copies, waits for them, and re-layouts  1.5 us (1%)
    all_to_all x1, blocking collectives, program(): arrived = lax.all_to_all(packed, 'space', 0, 0, tiled=True)  50.5 us
    pallas_call x6, Pallas kernels, call(): pl.pallas_call(kernel, out_shape=[s if hasattr(s, 'dtype') else jax.Shape...  18.9 us
    ppermute x3, waiting for transfers between devices, exchange(): near = lax.ppermute(to_near, 'space', pairs(0))  14.5 us
    ppermute x3, starting transfers between devices, exchange(): near = lax.ppermute(to_near, 'space', pairs(0))  13.2 us
    ppermute x7, starting transfers between devices, swap(): return lax.ppermute(array, 'slab', [(0, 1), (1, 0)])  5.22 us
  transfers between devices with their start and end apart: 13, of which 3 were waited for; matrix products, arithmetic and copies ran while one was open for 0% of the time, Pallas kernels for 9%

profile of v9, /device:TPU:1, one launch (start us, length us, event | category | flops | bytes accessed | tf_op | source)
XLA Modules:
  0.0 107.3 jit_solution(2168559972208488826)
XLA Ops:
  0.6 0.8 fusion.rates
  1.4 1.5 %copy-done = f32[8,12,12,384]{3,0,2,1:T(8,128)S(1)} copy-done((f32[8,12,12,384]{3,0,2,1:T(8,128)S(1)}, f32[8,12,12,384]{3,0,2,1:T(8,128)}, u32[]{:S(2)}) %copy-start) | copy-done | bytes 1769496
  2.9 0.2 shard_map.59
  3.0 2.5 %collective-permute-start = (f32[37,8,384]{2,1,0:T(8,128)S(1)}, f32[37,8,384]{2,1,0:T(8,128)S(1)}, u32[]{:S(2)}, u32[]{:S(2)}) collective-permute-start(f32[37,8,384]{2,1,0:T(8,128)S(1)} %get-tuple-element.31), channel_id=1, source_target_pairs={{0,2},{4,6},{8,10},{12,14},{16,18},{20,22},{24,26},{28,30},{32,34}... | collective-permute-start | bytes 1363976 | tf_op jit(solution)/shard_map/ppermute | solution.py:454
  5.5 0.7 collective-permute-start.1
  6.2 1.2 %collective-permute-start.3 = (f32[37,8,384]{2,1,0:T(8,128)S(1)}, f32[37,8,384]{2,1,0:T(8,128)S(1)}, u32[]{:S(2)}, u32[]{:S(2)}) collective-permute-start(f32[37,8,384]{2,1,0:T(8,128)S(1)} %get-tuple-element.34), channel_id=1, source_target_pairs={{0,1},{1,0},{2,3},{3,2},{4,5},{5,4},{6,7},{7,6},{8,9},{9,8},{10,11... | collective-permute-start | bytes 1363976 | tf_op jit(solution)/shard_map/ppermute | solution.py:458
  7.4 7.3 %collective-permute-done.near = f32[37,8,384]{2,1,0:T(8,128)S(1)} collective-permute-done((f32[37,8,384]{2,1,0:T(8,128)S(1)}, f32[37,8,384]{2,1,0:T(8,128)S(1)}, u32[]{:S(2)}, u32[]{:S(2)}) %collective-permute-start) | collective-permute-done | bytes 454688 | tf_op jit(solution)/shard_map/ppermute | solution.py:454
  14.7 0.0 collective-permute-done.1.far
  14.7 2.4 %collective-permute-start.2 = (f32[20,8,384]{2,1,0:T(8,128)S(1)}, f32[20,8,384]{2,1,0:T(8,128)S(1)}, u32[]{:S(2)}, u32[]{:S(2)}) collective-permute-start(f32[20,8,384]{2,1,0:T(8,128)S(1)} %pad_maximum_fusion), channel_id=1, source_target_pairs={{0,1},{1,0},{2,3},{3,2},{4,5},{5,4},{6,7},{7,6},{8,9},{9,8},{10,11... | collective-permute-start | bytes 737288 | tf_op jit(solution)/shard_map/ppermute | solution.py:458
  17.1 0.0 collective-permute-done.3.across
  17.1 5.5 %shard_map.60 = (f32[18,17,8,384]{3,2,1,0:T(8,128)S(1)}, f32[18,17,8,384]{3,2,1,0:T(8,128)S(1)}, f32[12,12,8,384]{3,2,1,0:T(8,128)}, f32[12,48,384]{2,1,0:T(8,12...) custom-call(f32[12,12,8,384]{3,2,1,0:T(8,128)S(1)} %bitcast.12, ...), custom_call_target="tpu_custom_call" | custom-call | tf_op jit(solution)/shard_map/pallas_call | solution.py:432
  22.6 0.0 collective-permute-done.2.corners
  22.6 3.6 %shard_map.61 = (f32[18,17,8,384]{3,2,1,0:T(8,128)S(1)}, f32[18,17,8,384]{3,2,1,0:T(8,128)S(1)}, f32[12,12,8,384]{3,2,1,0:T(8,128)}, f32[12,48,384]{2,1,0:T(8,12...) custom-call(f32[37,8,384]{2,1,0:T(8,128)S(1)} %collective-permute-do, ...), custom_call_target="tpu_custom_call", output_to_operand_aliasing={{0}: (6, {}), {1}: (7, {}), {2}: (8, {}), {3}: (9, {})} | custom-call | tf_op jit(solution)/shard_map/pallas_call | solution.py:432
  26.2 0.1 collective-permute-start.12
  26.3 5.2 %collective-permute-start.4 = (f32[144,384]{1,0:T(8,128)S(1)}, f32[144,384]{1,0:T(8,128)S(1)}, u32[]{:S(2)}, u32[]{:S(2)}) collective-permute-start(f32[144,384]{1,0:T(8,128)S(1)} %get-tuple-element.41), channel_id=1, source_target_pairs={{0,2},{4,6},{8,10},{12,14},{16,18},{20,22},{24,26},{28,30},{32,34}... | collective-permute-start | bytes 663560 | tf_op jit(solution)/shard_map/ppermute | solution.py:454
  31.5 0.7 collective-permute-start.5
  32.2 4.7 %collective-permute-done.4.near = f32[144,384]{1,0:T(8,128)S(1)} collective-permute-done((f32[144,384]{1,0:T(8,128)S(1)}, f32[144,384]{1,0:T(8,128)S(1)}, u32[]{:S(2)}, u32[]{:S(2)}) %collective-permute-start.4) | collective-permute-done | bytes 221216 | tf_op jit(solution)/shard_map/ppermute | solution.py:454
  36.9 1.0 collective-permute-start.6
  37.9 0.0 collective-permute-start.7
  37.9 5.5 %collective-permute-start.8 = (f32[64,384]{1,0:T(8,128)S(1)}, f32[64,384]{1,0:T(8,128)S(1)}, u32[]{:S(2)}, u32[]{:S(2)}) collective-permute-start(f32[64,384]{1,0:T(8,128)S(1)} %get-tuple-element.43), channel_id=1, source_target_pairs={{0,2},{4,6},{8,10},{12,14},{16,18},{20,22},{24,26},{28,30},{32,34}... | collective-permute-start | bytes 294920 | tf_op jit(solution)/shard_map/ppermute | solution.py:454
  43.4 0.7 collective-permute-start.9
  44.0 2.5 %collective-permute-done.8.e_near = f32[64,384]{1,0:T(8,128)S(1)} collective-permute-done((f32[64,384]{1,0:T(8,128)S(1)}, f32[64,384]{1,0:T(8,128)S(1)}, u32[]{:S(2)}, u32[]{:S(2)}) %collective-permute-start.8) | collective-permute-done | bytes 98336 | tf_op jit(solution)/shard_map/ppermute | solution.py:454
  46.5 0.6 collective-permute-start.10
  47.1 0.0 collective-permute-done.9.e_far
  47.1 0.0 collective-permute-start.11
  47.1 4.2 %shard_map.62 = (f32[22,16,384]{2,1,0:T(8,128)S(1)}, f32[22,24,384]{2,1,0:T(8,128)S(1)}, f32[22,16,384]{2,1,0:T(8,128)S(1)}, f32[22,16,384]{2,1,0:T(8,128)S(1)},...) custom-call(f32[12,48,384]{2,1,0:T(8,128)S(1)} %get-tuple-element.45, ...), custom_call_target="tpu_custom_call" | custom-call | tf_op jit(solution)/shard_map/pallas_call | solution.py:432
  51.3 0.0 collective-permute-done.10.oe_near
  51.4 0.0 collective-permute-done.6.o_near
  51.4 0.0 collective-permute-done.7.o_far
  51.4 4.3 %shard_map.63 = (f32[22,16,384]{2,1,0:T(8,128)S(1)}, f32[22,24,384]{2,1,0:T(8,128)S(1)}, f32[22,16,384]{2,1,0:T(8,128)S(1)}, f32[22,16,384]{2,1,0:T(8,128)S(1)},...) custom-call(f32[144,384]{1,0:T(8,128)S(1)} %collective-permute-done., ...), custom_call_target="tpu_custom_call", output_to_operand_aliasing={{0}: (8, {}), {1}: (9, {}), {2}: (10, {}), {3}: (11, {}), {... | custom-call | tf_op jit(solution)/shard_map/pallas_call | solution.py:432
  55.7 50.5 %all_to_all.5 = f32[128,1,1536]{2,1,0:T(1,128)S(1)} all-to-all(f32[128,1,1536]{2,1,0:T(1,128)S(1)} %bitcast.14), channel_id=1, replica_groups=mesh['space'=128,'slab'=2] {'space'}, dimensions={0} | all-to-all | bytes 1572864 | tf_op jit(solution)/shard_map/all_to_all | solution.py:508
  106.2 1.2 %shard_map.64 = f32[3,3,12,1536]{3,2,1,0:T(8,128)} custom-call(f32[1536,128]{1,0:T(8,128)S(1)} %bitcast.13), custom_call_target="tpu_custom_call" | custom-call | tf_op jit(solution)/shard_map/pallas_call | solution.py:432
  (11 shorter events, 0.1 us)
Async XLA Ops:
  0.6 16.5 %copy-start.2 = (f32[8,3]{0,1:T(4,128)S(1)}, f32[8,3]{0,1:T(4,128)}, u32[]{:S(2)}) copy-start(f32[8,3]{0,1:T(4,128)} %param.7) | copy-start | bytes 292
  1.4 1.5 %copy-start = (f32[8,12,12,384]{3,0,2,1:T(8,128)S(1)}, f32[8,12,12,384]{3,0,2,1:T(8,128)}, u32[]{:S(2)}) copy-start(f32[8,12,12,384]{3,0,2,1:T(8,128)} %param.4) | copy-start | bytes 5308420
  2.9 14.2 %copy-start.1 = (f32[8,12,12,384]{3,0,2,1:T(8,128)S(1)}, f32[8,12,12,384]{3,0,2,1:T(8,128)}, u32[]{:S(2)}) copy-start(f32[8,12,12,384]{3,0,2,1:T(8,128)} %param.4) | copy-start | bytes 5308420
  3.0 11.6 %collective-permute-start = (f32[37,8,384]{2,1,0:T(8,128)S(1)}, f32[37,8,384]{2,1,0:T(8,128)S(1)}, u32[]{:S(2)}, u32[]{:S(2)}) collective-permute-start(f32[37,8,384]{2,1,0:T(8,128)S(1)} %get-tuple-element.31), channel_id=1, source_target_pairs={{0,2},{4,6},{8,10},{12,14},{16,18},{20,22},{24,26},{28,30},{32,34}... | collective-permute-start | bytes 1363976 | tf_op jit(solution)/shard_map/ppermute | solution.py:454
  5.5 9.1 %collective-permute-start.1 = (f32[37,8,384]{2,1,0:T(8,128)S(1)}, f32[37,8,384]{2,1,0:T(8,128)S(1)}, u32[]{:S(2)}, u32[]{:S(2)}) collective-permute-start(f32[37,8,384]{2,1,0:T(8,128)S(1)} %get-tuple-element.32), channel_id=1, source_target_pairs={{2,4},{6,8},{10,12},{14,16},{18,20},{22,24},{26,28},{30,32},{34,36... | collective-permute-start | bytes 1363976 | tf_op jit(solution)/shard_map/ppermute | solution.py:453
  6.2 10.9 %collective-permute-start.3 = (f32[37,8,384]{2,1,0:T(8,128)S(1)}, f32[37,8,384]{2,1,0:T(8,128)S(1)}, u32[]{:S(2)}, u32[]{:S(2)}) collective-permute-start(f32[37,8,384]{2,1,0:T(8,128)S(1)} %get-tuple-element.34), channel_id=1, source_target_pairs={{0,1},{1,0},{2,3},{3,2},{4,5},{5,4},{6,7},{7,6},{8,9},{9,8},{10,11... | collective-permute-start | bytes 1363976 | tf_op jit(solution)/shard_map/ppermute | solution.py:458
  14.7 7.9 %collective-permute-start.2 = (f32[20,8,384]{2,1,0:T(8,128)S(1)}, f32[20,8,384]{2,1,0:T(8,128)S(1)}, u32[]{:S(2)}, u32[]{:S(2)}) collective-permute-start(f32[20,8,384]{2,1,0:T(8,128)S(1)} %pad_maximum_fusion), channel_id=1, source_target_pairs={{0,1},{1,0},{2,3},{3,2},{4,5},{5,4},{6,7},{7,6},{8,9},{9,8},{10,11... | collective-permute-start | bytes 737288 | tf_op jit(solution)/shard_map/ppermute | solution.py:458
  26.2 20.9 %collective-permute-start.12 = (f32[12,48,384]{2,1,0:T(8,128)S(1)}, f32[12,48,384]{2,1,0:T(8,128)S(1)}, u32[]{:S(2)}, u32[]{:S(2)}) collective-permute-start(f32[12,48,384]{2,1,0:T(8,128)S(1)} %get-tuple-element.45.coef), channel_id=1, source_target_pairs={{0,1},{1,0},{2,3},{3,2},{4,5},{5,4},{6,7},{7,6},{8,9},{9,8},{10,11... | collective-permute-start | bytes 2654216 | tf_op jit(solution)/shard_map/ppermute | solution.py:458
  26.3 10.6 %collective-permute-start.4 = (f32[144,384]{1,0:T(8,128)S(1)}, f32[144,384]{1,0:T(8,128)S(1)}, u32[]{:S(2)}, u32[]{:S(2)}) collective-permute-start(f32[144,384]{1,0:T(8,128)S(1)} %get-tuple-element.41), channel_id=1, source_target_pairs={{0,2},{4,6},{8,10},{12,14},{16,18},{20,22},{24,26},{28,30},{32,34}... | collective-permute-start | bytes 663560 | tf_op jit(solution)/shard_map/ppermute | solution.py:454
  31.5 6.4 %collective-permute-start.5 = (f32[144,384]{1,0:T(8,128)S(1)}, f32[144,384]{1,0:T(8,128)S(1)}, u32[]{:S(2)}, u32[]{:S(2)}) collective-permute-start(f32[144,384]{1,0:T(8,128)S(1)} %get-tuple-element.42), channel_id=1, source_target_pairs={{2,4},{6,8},{10,12},{14,16},{18,20},{22,24},{26,28},{30,32},{34,36... | collective-permute-start | bytes 663560 | tf_op jit(solution)/shard_map/ppermute | solution.py:453
  36.9 14.4 %collective-permute-start.6 = (f32[144,384]{1,0:T(8,128)S(1)}, f32[144,384]{1,0:T(8,128)S(1)}, u32[]{:S(2)}, u32[]{:S(2)}) collective-permute-start(f32[144,384]{1,0:T(8,128)S(1)} %collective-permute-done.4.near), channel_id=1, source_target_pairs={{0,1},{1,0},{2,3},{3,2},{4,5},{5,4},{6,7},{7,6},{8,9},{9,8},{10,11... | collective-permute-start | bytes 663560 | tf_op jit(solution)/shard_map/ppermute | solution.py:458
  37.9 13.5 %collective-permute-start.7 = (f32[144,384]{1,0:T(8,128)S(1)}, f32[144,384]{1,0:T(8,128)S(1)}, u32[]{:S(2)}, u32[]{:S(2)}) collective-permute-start(f32[144,384]{1,0:T(8,128)S(1)} %collective-permute-done.5.far), channel_id=1, source_target_pairs={{0,1},{1,0},{2,3},{3,2},{4,5},{5,4},{6,7},{7,6},{8,9},{9,8},{10,11... | collective-permute-start | bytes 663560 | tf_op jit(solution)/shard_map/ppermute | solution.py:458
  37.9 8.6 %collective-permute-start.8 = (f32[64,384]{1,0:T(8,128)S(1)}, f32[64,384]{1,0:T(8,128)S(1)}, u32[]{:S(2)}, u32[]{:S(2)}) collective-permute-start(f32[64,384]{1,0:T(8,128)S(1)} %get-tuple-element.43), channel_id=1, source_target_pairs={{0,2},{4,6},{8,10},{12,14},{16,18},{20,22},{24,26},{28,30},{32,34}... | collective-permute-start | bytes 294920 | tf_op jit(solution)/shard_map/ppermute | solution.py:454
  43.4 3.8 %collective-permute-start.9 = (f32[64,384]{1,0:T(8,128)S(1)}, f32[64,384]{1,0:T(8,128)S(1)}, u32[]{:S(2)}, u32[]{:S(2)}) collective-permute-start(f32[64,384]{1,0:T(8,128)S(1)} %get-tuple-element.44), channel_id=1, source_target_pairs={{2,4},{6,8},{10,12},{14,16},{18,20},{22,24},{26,28},{30,32},{34,36... | collective-permute-start | bytes 294920 | tf_op jit(solution)/shard_map/ppermute | solution.py:453
  46.5 4.8 %collective-permute-start.10 = (f32[64,384]{1,0:T(8,128)S(1)}, f32[64,384]{1,0:T(8,128)S(1)}, u32[]{:S(2)}, u32[]{:S(2)}) collective-permute-start(f32[64,384]{1,0:T(8,128)S(1)} %collective-permute-done.8.e_near), channel_id=1, source_target_pairs={{0,1},{1,0},{2,3},{3,2},{4,5},{5,4},{6,7},{7,6},{8,9},{9,8},{10,11... | collective-permute-start | bytes 294920 | tf_op jit(solution)/shard_map/ppermute | solution.py:458
  47.1 4.2 %collective-permute-start.11 = (f32[64,384]{1,0:T(8,128)S(1)}, f32[64,384]{1,0:T(8,128)S(1)}, u32[]{:S(2)}, u32[]{:S(2)}) collective-permute-start(f32[64,384]{1,0:T(8,128)S(1)} %collective-permute-done.9.e_far), channel_id=1, source_target_pairs={{0,1},{1,0},{2,3},{3,2},{4,5},{5,4},{6,7},{7,6},{8,9},{9,8},{10,11... | collective-permute-start | bytes 294920 | tf_op jit(solution)/shard_map/ppermute | solution.py:458

commit v10 on v9

--- a/solution.py
+++ b/solution.py
@@ -342,10 +342,10 @@
 def solve_inner_kernel(coef, o_coef, *state):
     solver = Solver(state)
     loop(0, B, lambda i: solver.put(i + GO, coef[i], o_coef[i]))
-    loop(GO + 1, GO + B - 1, solver.force)
-    loop(GO + 1, GO + B - 1, solver.weigh)
+    loop(GO + 1, GO + B - 1, solver.force, True)
+    loop(GO + 1, GO + B - 1, solver.weigh, True)
     for t in range(ITERS - 1):
-        solver.iterate(t, GO + 2 + t, GO + B - 2 - t)
+        solver.iterate(t, GO + 2 + t, GO + B - 2 - t, True)
 
 
 def solve_outer_kernel(near, far, o_near, o_far, e_near, e_far, oe_near, oe_far, *refs):

time: 108 us -> 105 us (0.972)
  Pallas kernels: 18.9 us -> 16.4 us
    pallas_call x6, Pallas kernels: 18.9 us -> 16.4 us  [call(): pl.pallas_call(kernel, out_shape=[s if hasattr(s, 'dtype') else jax.Shape...]
  transfers between devices with their start and end apart: 13 -> 13, of which waited for: 3 -> 3; matrix products, arithmetic and copies ran while one was open for 0% -> 0% of each run, Pallas kernels for 9% -> 7%
where the time goes in v10:
time: 105 us
  blocking collectives  50.5 us (48%)
  starting transfers between devices  20.4 us (19%)
  Pallas kernels  16.4 us (16%)
  waiting for transfers between devices  14.5 us (14%)
  local copies, waits for them, and re-layouts  1.5 us (1%)
    all_to_all x1, blocking collectives, program(): arrived = lax.all_to_all(packed, 'space', 0, 0, tiled=True)  50.5 us
    pallas_call x6, Pallas kernels, call(): pl.pallas_call(kernel, out_shape=[s if hasattr(s, 'dtype') else jax.Shape...  16.4 us
    ppermute x3, waiting for transfers between devices, exchange(): near = lax.ppermute(to_near, 'space', pairs(0))  14.5 us
    ppermute x3, starting transfers between devices, exchange(): near = lax.ppermute(to_near, 'space', pairs(0))  13.2 us
    ppermute x7, starting transfers between devices, swap(): return lax.ppermute(array, 'slab', [(0, 1), (1, 0)])  5.22 us
  transfers between devices with their start and end apart: 13, of which 3 were waited for; matrix products, arithmetic and copies ran while one was open for 0% of the time, Pallas kernels for 7%

profile of v10, /device:TPU:1, one launch (start us, length us, event | category | flops | bytes accessed | tf_op | source)
XLA Modules:
  0.0 104.9 jit_solution(13639416009347294980)
XLA Ops:
  0.6 0.8 fusion.rates
  1.4 1.5 %copy-done = f32[8,12,12,384]{3,0,2,1:T(8,128)S(1)} copy-done((f32[8,12,12,384]{3,0,2,1:T(8,128)S(1)}, f32[8,12,12,384]{3,0,2,1:T(8,128)}, u32[]{:S(2)}) %copy-start) | copy-done | bytes 1769496
  2.9 0.2 shard_map.59
  3.0 2.5 %collective-permute-start = (f32[37,8,384]{2,1,0:T(8,128)S(1)}, f32[37,8,384]{2,1,0:T(8,128)S(1)}, u32[]{:S(2)}, u32[]{:S(2)}) collective-permute-start(f32[37,8,384]{2,1,0:T(8,128)S(1)} %get-tuple-element.31), channel_id=1, source_target_pairs={{0,2},{4,6},{8,10},{12,14},{16,18},{20,22},{24,26},{28,30},{32,34}... | collective-permute-start | bytes 1363976 | tf_op jit(solution)/shard_map/ppermute | solution.py:454
  5.5 0.7 collective-permute-start.1
  6.2 1.2 %collective-permute-start.3 = (f32[37,8,384]{2,1,0:T(8,128)S(1)}, f32[37,8,384]{2,1,0:T(8,128)S(1)}, u32[]{:S(2)}, u32[]{:S(2)}) collective-permute-start(f32[37,8,384]{2,1,0:T(8,128)S(1)} %get-tuple-element.34), channel_id=1, source_target_pairs={{0,1},{1,0},{2,3},{3,2},{4,5},{5,4},{6,7},{7,6},{8,9},{9,8},{10,11... | collective-permute-start | bytes 1363976 | tf_op jit(solution)/shard_map/ppermute | solution.py:458
  7.4 7.3 %collective-permute-done.near = f32[37,8,384]{2,1,0:T(8,128)S(1)} collective-permute-done((f32[37,8,384]{2,1,0:T(8,128)S(1)}, f32[37,8,384]{2,1,0:T(8,128)S(1)}, u32[]{:S(2)}, u32[]{:S(2)}) %collective-permute-start) | collective-permute-done | bytes 454688 | tf_op jit(solution)/shard_map/ppermute | solution.py:454
  14.7 0.0 collective-permute-done.1.far
  14.7 2.4 %collective-permute-start.2 = (f32[20,8,384]{2,1,0:T(8,128)S(1)}, f32[20,8,384]{2,1,0:T(8,128)S(1)}, u32[]{:S(2)}, u32[]{:S(2)}) collective-permute-start(f32[20,8,384]{2,1,0:T(8,128)S(1)} %pad_maximum_fusion), channel_id=1, source_target_pairs={{0,1},{1,0},{2,3},{3,2},{4,5},{5,4},{6,7},{7,6},{8,9},{9,8},{10,11... | collective-permute-start | bytes 737288 | tf_op jit(solution)/shard_map/ppermute | solution.py:458
  17.1 0.0 collective-permute-done.3.across
  17.1 5.5 %shard_map.60 = (f32[18,17,8,384]{3,2,1,0:T(8,128)S(1)}, f32[18,17,8,384]{3,2,1,0:T(8,128)S(1)}, f32[12,12,8,384]{3,2,1,0:T(8,128)}, f32[12,48,384]{2,1,0:T(8,12...) custom-call(f32[12,12,8,384]{3,2,1,0:T(8,128)S(1)} %bitcast.12, ...), custom_call_target="tpu_custom_call" | custom-call | tf_op jit(solution)/shard_map/pallas_call | solution.py:432
  22.6 0.0 collective-permute-done.2.corners
  22.6 3.6 %shard_map.61 = (f32[18,17,8,384]{3,2,1,0:T(8,128)S(1)}, f32[18,17,8,384]{3,2,1,0:T(8,128)S(1)}, f32[12,12,8,384]{3,2,1,0:T(8,128)}, f32[12,48,384]{2,1,0:T(8,12...) custom-call(f32[37,8,384]{2,1,0:T(8,128)S(1)} %collective-permute-do, ...), custom_call_target="tpu_custom_call", output_to_operand_aliasing={{0}: (6, {}), {1}: (7, {}), {2}: (8, {}), {3}: (9, {})} | custom-call | tf_op jit(solution)/shard_map/pallas_call | solution.py:432
  26.2 0.1 collective-permute-start.12
  26.3 5.2 %collective-permute-start.4 = (f32[144,384]{1,0:T(8,128)S(1)}, f32[144,384]{1,0:T(8,128)S(1)}, u32[]{:S(2)}, u32[]{:S(2)}) collective-permute-start(f32[144,384]{1,0:T(8,128)S(1)} %get-tuple-element.41), channel_id=1, source_target_pairs={{0,2},{4,6},{8,10},{12,14},{16,18},{20,22},{24,26},{28,30},{32,34}... | collective-permute-start | bytes 663560 | tf_op jit(solution)/shard_map/ppermute | solution.py:454
  31.5 0.7 collective-permute-start.5
  32.2 4.7 %collective-permute-done.4.near = f32[144,384]{1,0:T(8,128)S(1)} collective-permute-done((f32[144,384]{1,0:T(8,128)S(1)}, f32[144,384]{1,0:T(8,128)S(1)}, u32[]{:S(2)}, u32[]{:S(2)}) %collective-permute-start.4) | collective-permute-done | bytes 221216 | tf_op jit(solution)/shard_map/ppermute | solution.py:454
  36.9 1.0 collective-permute-start.6
  37.9 0.0 collective-permute-start.7
  37.9 5.5 %collective-permute-start.8 = (f32[64,384]{1,0:T(8,128)S(1)}, f32[64,384]{1,0:T(8,128)S(1)}, u32[]{:S(2)}, u32[]{:S(2)}) collective-permute-start(f32[64,384]{1,0:T(8,128)S(1)} %get-tuple-element.43), channel_id=1, source_target_pairs={{0,2},{4,6},{8,10},{12,14},{16,18},{20,22},{24,26},{28,30},{32,34}... | collective-permute-start | bytes 294920 | tf_op jit(solution)/shard_map/ppermute | solution.py:454
  43.4 0.7 collective-permute-start.9
  44.0 2.5 %collective-permute-done.8.e_near = f32[64,384]{1,0:T(8,128)S(1)} collective-permute-done((f32[64,384]{1,0:T(8,128)S(1)}, f32[64,384]{1,0:T(8,128)S(1)}, u32[]{:S(2)}, u32[]{:S(2)}) %collective-permute-start.8) | collective-permute-done | bytes 98336 | tf_op jit(solution)/shard_map/ppermute | solution.py:454
  46.5 0.6 collective-permute-start.10
  47.1 0.0 collective-permute-done.9.e_far
  47.1 0.0 collective-permute-start.11
  47.1 0.0 collective-permute-done.12.o_coef
  47.1 1.9 %shard_map.62 = (f32[22,16,384]{2,1,0:T(8,128)S(1)}, f32[22,24,384]{2,1,0:T(8,128)S(1)}, f32[22,16,384]{2,1,0:T(8,128)S(1)}, f32[22,16,384]{2,1,0:T(8,128)S(1)},...) custom-call(f32[12,48,384]{2,1,0:T(8,128)S(1)} %get-tuple-element.45, ...), custom_call_target="tpu_custom_call" | custom-call | tf_op jit(solution)/shard_map/pallas_call | solution.py:432
  49.1 0.0 collective-permute-done.10.oe_near
  49.1 0.0 collective-permute-done.11.oe_far
  49.1 4.1 %shard_map.63 = (f32[22,16,384]{2,1,0:T(8,128)S(1)}, f32[22,24,384]{2,1,0:T(8,128)S(1)}, f32[22,16,384]{2,1,0:T(8,128)S(1)}, f32[22,16,384]{2,1,0:T(8,128)S(1)},...) custom-call(f32[144,384]{1,0:T(8,128)S(1)} %collective-permute-done., ...), custom_call_target="tpu_custom_call", output_to_operand_aliasing={{0}: (8, {}), {1}: (9, {}), {2}: (10, {}), {3}: (11, {}), {... | custom-call | tf_op jit(solution)/shard_map/pallas_call | solution.py:432
  53.2 50.5 %all_to_all.5 = f32[128,1,1536]{2,1,0:T(1,128)S(1)} all-to-all(f32[128,1,1536]{2,1,0:T(1,128)S(1)} %bitcast.14), channel_id=1, replica_groups=mesh['space'=128,'slab'=2] {'space'}, dimensions={0} | all-to-all | bytes 1572864 | tf_op jit(solution)/shard_map/all_to_all | solution.py:508
  103.7 1.2 %shard_map.64 = f32[3,3,12,1536]{3,2,1,0:T(8,128)} custom-call(f32[1536,128]{1,0:T(8,128)S(1)} %bitcast.13), custom_call_target="tpu_custom_call" | custom-call | tf_op jit(solution)/shard_map/pallas_call | solution.py:432
  (11 shorter events, 0.1 us)
Async XLA Ops:
  0.6 16.5 %copy-start.2 = (f32[8,3]{0,1:T(4,128)S(1)}, f32[8,3]{0,1:T(4,128)}, u32[]{:S(2)}) copy-start(f32[8,3]{0,1:T(4,128)} %param.7) | copy-start | bytes 292
  1.4 1.5 %copy-start = (f32[8,12,12,384]{3,0,2,1:T(8,128)S(1)}, f32[8,12,12,384]{3,0,2,1:T(8,128)}, u32[]{:S(2)}) copy-start(f32[8,12,12,384]{3,0,2,1:T(8,128)} %param.4) | copy-start | bytes 5308420
  2.9 14.2 %copy-start.1 = (f32[8,12,12,384]{3,0,2,1:T(8,128)S(1)}, f32[8,12,12,384]{3,0,2,1:T(8,128)}, u32[]{:S(2)}) copy-start(f32[8,12,12,384]{3,0,2,1:T(8,128)} %param.4) | copy-start | bytes 5308420
  3.0 11.6 %collective-permute-start = (f32[37,8,384]{2,1,0:T(8,128)S(1)}, f32[37,8,384]{2,1,0:T(8,128)S(1)}, u32[]{:S(2)}, u32[]{:S(2)}) collective-permute-start(f32[37,8,384]{2,1,0:T(8,128)S(1)} %get-tuple-element.31), channel_id=1, source_target_pairs={{0,2},{4,6},{8,10},{12,14},{16,18},{20,22},{24,26},{28,30},{32,34}... | collective-permute-start | bytes 1363976 | tf_op jit(solution)/shard_map/ppermute | solution.py:454
  5.5 9.1 %collective-permute-start.1 = (f32[37,8,384]{2,1,0:T(8,128)S(1)}, f32[37,8,384]{2,1,0:T(8,128)S(1)}, u32[]{:S(2)}, u32[]{:S(2)}) collective-permute-start(f32[37,8,384]{2,1,0:T(8,128)S(1)} %get-tuple-element.32), channel_id=1, source_target_pairs={{2,4},{6,8},{10,12},{14,16},{18,20},{22,24},{26,28},{30,32},{34,36... | collective-permute-start | bytes 1363976 | tf_op jit(solution)/shard_map/ppermute | solution.py:453
  6.2 10.9 %collective-permute-start.3 = (f32[37,8,384]{2,1,0:T(8,128)S(1)}, f32[37,8,384]{2,1,0:T(8,128)S(1)}, u32[]{:S(2)}, u32[]{:S(2)}) collective-permute-start(f32[37,8,384]{2,1,0:T(8,128)S(1)} %get-tuple-element.34), channel_id=1, source_target_pairs={{0,1},{1,0},{2,3},{3,2},{4,5},{5,4},{6,7},{7,6},{8,9},{9,8},{10,11... | collective-permute-start | bytes 1363976 | tf_op jit(solution)/shard_map/ppermute | solution.py:458
  14.7 7.9 %collective-permute-start.2 = (f32[20,8,384]{2,1,0:T(8,128)S(1)}, f32[20,8,384]{2,1,0:T(8,128)S(1)}, u32[]{:S(2)}, u32[]{:S(2)}) collective-permute-start(f32[20,8,384]{2,1,0:T(8,128)S(1)} %pad_maximum_fusion), channel_id=1, source_target_pairs={{0,1},{1,0},{2,3},{3,2},{4,5},{5,4},{6,7},{7,6},{8,9},{9,8},{10,11... | collective-permute-start | bytes 737288 | tf_op jit(solution)/shard_map/ppermute | solution.py:458
  26.2 20.9 %collective-permute-start.12 = (f32[12,48,384]{2,1,0:T(8,128)S(1)}, f32[12,48,384]{2,1,0:T(8,128)S(1)}, u32[]{:S(2)}, u32[]{:S(2)}) collective-permute-start(f32[12,48,384]{2,1,0:T(8,128)S(1)} %get-tuple-element.45.coef), channel_id=1, source_target_pairs={{0,1},{1,0},{2,3},{3,2},{4,5},{5,4},{6,7},{7,6},{8,9},{9,8},{10,11... | collective-permute-start | bytes 2654216 | tf_op jit(solution)/shard_map/ppermute | solution.py:458
  26.3 10.6 %collective-permute-start.4 = (f32[144,384]{1,0:T(8,128)S(1)}, f32[144,384]{1,0:T(8,128)S(1)}, u32[]{:S(2)}, u32[]{:S(2)}) collective-permute-start(f32[144,384]{1,0:T(8,128)S(1)} %get-tuple-element.41), channel_id=1, source_target_pairs={{0,2},{4,6},{8,10},{12,14},{16,18},{20,22},{24,26},{28,30},{32,34}... | collective-permute-start | bytes 663560 | tf_op jit(solution)/shard_map/ppermute | solution.py:454
  31.5 6.4 %collective-permute-start.5 = (f32[144,384]{1,0:T(8,128)S(1)}, f32[144,384]{1,0:T(8,128)S(1)}, u32[]{:S(2)}, u32[]{:S(2)}) collective-permute-start(f32[144,384]{1,0:T(8,128)S(1)} %get-tuple-element.42), channel_id=1, source_target_pairs={{2,4},{6,8},{10,12},{14,16},{18,20},{22,24},{26,28},{30,32},{34,36... | collective-permute-start | bytes 663560 | tf_op jit(solution)/shard_map/ppermute | solution.py:453
  36.9 12.2 %collective-permute-start.6 = (f32[144,384]{1,0:T(8,128)S(1)}, f32[144,384]{1,0:T(8,128)S(1)}, u32[]{:S(2)}, u32[]{:S(2)}) collective-permute-start(f32[144,384]{1,0:T(8,128)S(1)} %collective-permute-done.4.near), channel_id=1, source_target_pairs={{0,1},{1,0},{2,3},{3,2},{4,5},{5,4},{6,7},{7,6},{8,9},{9,8},{10,11... | collective-permute-start | bytes 663560 | tf_op jit(solution)/shard_map/ppermute | solution.py:458
  37.9 11.2 %collective-permute-start.7 = (f32[144,384]{1,0:T(8,128)S(1)}, f32[144,384]{1,0:T(8,128)S(1)}, u32[]{:S(2)}, u32[]{:S(2)}) collective-permute-start(f32[144,384]{1,0:T(8,128)S(1)} %collective-permute-done.5.far), channel_id=1, source_target_pairs={{0,1},{1,0},{2,3},{3,2},{4,5},{5,4},{6,7},{7,6},{8,9},{9,8},{10,11... | collective-permute-start | bytes 663560 | tf_op jit(solution)/shard_map/ppermute | solution.py:458
  37.9 8.6 %collective-permute-start.8 = (f32[64,384]{1,0:T(8,128)S(1)}, f32[64,384]{1,0:T(8,128)S(1)}, u32[]{:S(2)}, u32[]{:S(2)}) collective-permute-start(f32[64,384]{1,0:T(8,128)S(1)} %get-tuple-element.43), channel_id=1, source_target_pairs={{0,2},{4,6},{8,10},{12,14},{16,18},{20,22},{24,26},{28,30},{32,34}... | collective-permute-start | bytes 294920 | tf_op jit(solution)/shard_map/ppermute | solution.py:454
  43.4 3.8 %collective-permute-start.9 = (f32[64,384]{1,0:T(8,128)S(1)}, f32[64,384]{1,0:T(8,128)S(1)}, u32[]{:S(2)}, u32[]{:S(2)}) collective-permute-start(f32[64,384]{1,0:T(8,128)S(1)} %get-tuple-element.44), channel_id=1, source_target_pairs={{2,4},{6,8},{10,12},{14,16},{18,20},{22,24},{26,28},{30,32},{34,36... | collective-permute-start | bytes 294920 | tf_op jit(solution)/shard_map/ppermute | solution.py:453
  46.5 2.5 %collective-permute-start.10 = (f32[64,384]{1,0:T(8,128)S(1)}, f32[64,384]{1,0:T(8,128)S(1)}, u32[]{:S(2)}, u32[]{:S(2)}) collective-permute-start(f32[64,384]{1,0:T(8,128)S(1)} %collective-permute-done.8.e_near), channel_id=1, source_target_pairs={{0,1},{1,0},{2,3},{3,2},{4,5},{5,4},{6,7},{7,6},{8,9},{9,8},{10,11... | collective-permute-start | bytes 294920 | tf_op jit(solution)/shard_map/ppermute | solution.py:458
  47.1 1.9 %collective-permute-start.11 = (f32[64,384]{1,0:T(8,128)S(1)}, f32[64,384]{1,0:T(8,128)S(1)}, u32[]{:S(2)}, u32[]{:S(2)}) collective-permute-start(f32[64,384]{1,0:T(8,128)S(1)} %collective-permute-done.9.e_far), channel_id=1, source_target_pairs={{0,1},{1,0},{2,3},{3,2},{4,5},{5,4},{6,7},{7,6},{8,9},{9,8},{10,11... | collective-permute-start | bytes 294920 | tf_op jit(solution)/shard_map/ppermute | solution.py:458

commit v11 on v10

--- a/solution.py
+++ b/solution.py
@@ -174,9 +174,9 @@
         return 0
 
     lax.fori_loop(0, B, fill, 0)
-    window_step(first, second, speed, 1, B - 2, lambda n: H + 1 + n)
-    window_step(second, first, speed, 2, B - 4, lambda n: H + 2 + n)
-    last_step(first, speed.at[1, 0], mix, ev, coef, B - 6, lambda n: H + 3 + n, staged, sems)
+    window_step(first, second, speed, 1, B - 2, lambda n: H + 1 + n, True)
+    window_step(second, first, speed, 2, B - 4, lambda n: H + 2 + n, True)
+    last_step(first, speed.at[1, 0], mix, ev, coef, B - 6, lambda n: H + 3 + n, staged, sems, True)
     even, odd = parity()
     for message, top in ((e_near, even), (e_far, odd)):
         message[: 4 * B] = coef[H + (B - 2 * H - 1) * top]

time: 105 us -> 105 us (level)
  no operation moved by 1% of the time
where the time goes in v11:
time: 105 us; the launch traced here: 104 us
  blocking collectives  50.5 us (48%)
  starting transfers between devices  20.4 us (19%)
  Pallas kernels  15.9 us (15%)
  waiting for transfers between devices  14.5 us (14%)
  local copies, waits for them, and re-layouts  1.5 us (1%)
    all_to_all x1, blocking collectives, program(): arrived = lax.all_to_all(packed, 'space', 0, 0, tiled=True)  50.5 us
    pallas_call x6, Pallas kernels, call(): pl.pallas_call(kernel, out_shape=[s if hasattr(s, 'dtype') else jax.Shape...  15.9 us
    ppermute x3, waiting for transfers between devices, exchange(): near = lax.ppermute(to_near, 'space', pairs(0))  14.5 us
    ppermute x3, starting transfers between devices, exchange(): near = lax.ppermute(to_near, 'space', pairs(0))  13.2 us
    ppermute x7, starting transfers between devices, swap(): return lax.ppermute(array, 'slab', [(0, 1), (1, 0)])  5.21 us
  transfers between devices with their start and end apart: 13, of which 3 were waited for; matrix products, arithmetic and copies ran while one was open for 0% of the time, Pallas kernels for 7%

profile of v11, /device:TPU:1, one launch (start us, length us, event | category | flops | bytes accessed | tf_op | source)
XLA Modules:
  0.0 104.4 jit_solution(14286325721578528769)
XLA Ops:
  0.6 0.8 fusion.rates
  1.4 1.5 %copy-done = f32[8,12,12,384]{3,0,2,1:T(8,128)S(1)} copy-done((f32[8,12,12,384]{3,0,2,1:T(8,128)S(1)}, f32[8,12,12,384]{3,0,2,1:T(8,128)}, u32[]{:S(2)}) %copy-start) | copy-done | bytes 1769496
  2.9 0.2 shard_map.59
  3.0 2.5 %collective-permute-start = (f32[37,8,384]{2,1,0:T(8,128)S(1)}, f32[37,8,384]{2,1,0:T(8,128)S(1)}, u32[]{:S(2)}, u32[]{:S(2)}) collective-permute-start(f32[37,8,384]{2,1,0:T(8,128)S(1)} %get-tuple-element.31), channel_id=1, source_target_pairs={{0,2},{4,6},{8,10},{12,14},{16,18},{20,22},{24,26},{28,30},{32,34}... | collective-permute-start | bytes 1363976 | tf_op jit(solution)/shard_map/ppermute | solution.py:454
  5.5 0.7 collective-permute-start.1
  6.2 1.2 %collective-permute-start.3 = (f32[37,8,384]{2,1,0:T(8,128)S(1)}, f32[37,8,384]{2,1,0:T(8,128)S(1)}, u32[]{:S(2)}, u32[]{:S(2)}) collective-permute-start(f32[37,8,384]{2,1,0:T(8,128)S(1)} %get-tuple-element.34), channel_id=1, source_target_pairs={{0,1},{1,0},{2,3},{3,2},{4,5},{5,4},{6,7},{7,6},{8,9},{9,8},{10,11... | collective-permute-start | bytes 1363976 | tf_op jit(solution)/shard_map/ppermute | solution.py:458
  7.4 7.3 %collective-permute-done.near = f32[37,8,384]{2,1,0:T(8,128)S(1)} collective-permute-done((f32[37,8,384]{2,1,0:T(8,128)S(1)}, f32[37,8,384]{2,1,0:T(8,128)S(1)}, u32[]{:S(2)}, u32[]{:S(2)}) %collective-permute-start) | collective-permute-done | bytes 454688 | tf_op jit(solution)/shard_map/ppermute | solution.py:454
  14.7 0.0 collective-permute-done.1.far
  14.7 2.4 %collective-permute-start.2 = (f32[20,8,384]{2,1,0:T(8,128)S(1)}, f32[20,8,384]{2,1,0:T(8,128)S(1)}, u32[]{:S(2)}, u32[]{:S(2)}) collective-permute-start(f32[20,8,384]{2,1,0:T(8,128)S(1)} %pad_maximum_fusion), channel_id=1, source_target_pairs={{0,1},{1,0},{2,3},{3,2},{4,5},{5,4},{6,7},{7,6},{8,9},{9,8},{10,11... | collective-permute-start | bytes 737288 | tf_op jit(solution)/shard_map/ppermute | solution.py:458
  17.1 0.0 collective-permute-done.3.across
  17.1 5.0 %shard_map.60 = (f32[18,17,8,384]{3,2,1,0:T(8,128)S(1)}, f32[18,17,8,384]{3,2,1,0:T(8,128)S(1)}, f32[12,12,8,384]{3,2,1,0:T(8,128)}, f32[12,48,384]{2,1,0:T(8,12...) custom-call(f32[12,12,8,384]{3,2,1,0:T(8,128)S(1)} %bitcast.12, ...), custom_call_target="tpu_custom_call" | custom-call | tf_op jit(solution)/shard_map/pallas_call | solution.py:432
  22.1 0.0 collective-permute-done.2.corners
  22.1 3.6 %shard_map.61 = (f32[18,17,8,384]{3,2,1,0:T(8,128)S(1)}, f32[18,17,8,384]{3,2,1,0:T(8,128)S(1)}, f32[12,12,8,384]{3,2,1,0:T(8,128)}, f32[12,48,384]{2,1,0:T(8,12...) custom-call(f32[37,8,384]{2,1,0:T(8,128)S(1)} %collective-permute-do, ...), custom_call_target="tpu_custom_call", output_to_operand_aliasing={{0}: (6, {}), {1}: (7, {}), {2}: (8, {}), {3}: (9, {})} | custom-call | tf_op jit(solution)/shard_map/pallas_call | solution.py:432
  25.7 0.1 collective-permute-start.12
  25.8 5.2 %collective-permute-start.4 = (f32[144,384]{1,0:T(8,128)S(1)}, f32[144,384]{1,0:T(8,128)S(1)}, u32[]{:S(2)}, u32[]{:S(2)}) collective-permute-start(f32[144,384]{1,0:T(8,128)S(1)} %get-tuple-element.41), channel_id=1, source_target_pairs={{0,2},{4,6},{8,10},{12,14},{16,18},{20,22},{24,26},{28,30},{32,34}... | collective-permute-start | bytes 663560 | tf_op jit(solution)/shard_map/ppermute | solution.py:454
  31.0 0.7 collective-permute-start.5
  31.7 4.7 %collective-permute-done.4.near = f32[144,384]{1,0:T(8,128)S(1)} collective-permute-done((f32[144,384]{1,0:T(8,128)S(1)}, f32[144,384]{1,0:T(8,128)S(1)}, u32[]{:S(2)}, u32[]{:S(2)}) %collective-permute-start.4) | collective-permute-done | bytes 221216 | tf_op jit(solution)/shard_map/ppermute | solution.py:454
  36.4 1.0 collective-permute-start.6
  37.4 0.0 collective-permute-done.5.far
  37.4 0.0 collective-permute-start.7
  37.4 5.5 %collective-permute-start.8 = (f32[64,384]{1,0:T(8,128)S(1)}, f32[64,384]{1,0:T(8,128)S(1)}, u32[]{:S(2)}, u32[]{:S(2)}) collective-permute-start(f32[64,384]{1,0:T(8,128)S(1)} %get-tuple-element.43), channel_id=1, source_target_pairs={{0,2},{4,6},{8,10},{12,14},{16,18},{20,22},{24,26},{28,30},{32,34}... | collective-permute-start | bytes 294920 | tf_op jit(solution)/shard_map/ppermute | solution.py:454
  42.9 0.7 collective-permute-start.9
  43.5 2.5 %collective-permute-done.8.e_near = f32[64,384]{1,0:T(8,128)S(1)} collective-permute-done((f32[64,384]{1,0:T(8,128)S(1)}, f32[64,384]{1,0:T(8,128)S(1)}, u32[]{:S(2)}, u32[]{:S(2)}) %collective-permute-start.8) | collective-permute-done | bytes 98336 | tf_op jit(solution)/shard_map/ppermute | solution.py:454
  46.0 0.6 collective-permute-start.10
  46.6 0.0 collective-permute-done.9.e_far
  46.6 0.0 collective-permute-start.11
  46.6 0.0 collective-permute-done.12.o_coef
  46.6 1.9 %shard_map.62 = (f32[22,16,384]{2,1,0:T(8,128)S(1)}, f32[22,24,384]{2,1,0:T(8,128)S(1)}, f32[22,16,384]{2,1,0:T(8,128)S(1)}, f32[22,16,384]{2,1,0:T(8,128)S(1)},...) custom-call(f32[12,48,384]{2,1,0:T(8,128)S(1)} %get-tuple-element.45, ...), custom_call_target="tpu_custom_call" | custom-call | tf_op jit(solution)/shard_map/pallas_call | solution.py:432
  48.5 0.0 collective-permute-done.10.oe_near
  48.6 4.1 %shard_map.63 = (f32[22,16,384]{2,1,0:T(8,128)S(1)}, f32[22,24,384]{2,1,0:T(8,128)S(1)}, f32[22,16,384]{2,1,0:T(8,128)S(1)}, f32[22,16,384]{2,1,0:T(8,128)S(1)},...) custom-call(f32[144,384]{1,0:T(8,128)S(1)} %collective-permute-done., ...), custom_call_target="tpu_custom_call", output_to_operand_aliasing={{0}: (8, {}), {1}: (9, {}), {2}: (10, {}), {3}: (11, {}), {... | custom-call | tf_op jit(solution)/shard_map/pallas_call | solution.py:432
  52.7 50.5 %all_to_all.5 = f32[128,1,1536]{2,1,0:T(1,128)S(1)} all-to-all(f32[128,1,1536]{2,1,0:T(1,128)S(1)} %bitcast.14), channel_id=1, replica_groups=mesh['space'=128,'slab'=2] {'space'}, dimensions={0} | all-to-all | bytes 1572864 | tf_op jit(solution)/shard_map/all_to_all | solution.py:508
  103.2 1.2 %shard_map.64 = f32[3,3,12,1536]{3,2,1,0:T(8,128)} custom-call(f32[1536,128]{1,0:T(8,128)S(1)} %bitcast.13), custom_call_target="tpu_custom_call" | custom-call | tf_op jit(solution)/shard_map/pallas_call | solution.py:432
  (11 shorter events, 0.1 us)
Async XLA Ops:
  0.6 16.5 %copy-start.2 = (f32[8,3]{0,1:T(4,128)S(1)}, f32[8,3]{0,1:T(4,128)}, u32[]{:S(2)}) copy-start(f32[8,3]{0,1:T(4,128)} %param.7) | copy-start | bytes 292
  1.4 1.5 %copy-start = (f32[8,12,12,384]{3,0,2,1:T(8,128)S(1)}, f32[8,12,12,384]{3,0,2,1:T(8,128)}, u32[]{:S(2)}) copy-start(f32[8,12,12,384]{3,0,2,1:T(8,128)} %param.4) | copy-start | bytes 5308420
  2.9 14.2 %copy-start.1 = (f32[8,12,12,384]{3,0,2,1:T(8,128)S(1)}, f32[8,12,12,384]{3,0,2,1:T(8,128)}, u32[]{:S(2)}) copy-start(f32[8,12,12,384]{3,0,2,1:T(8,128)} %param.4) | copy-start | bytes 5308420
  3.0 11.6 %collective-permute-start = (f32[37,8,384]{2,1,0:T(8,128)S(1)}, f32[37,8,384]{2,1,0:T(8,128)S(1)}, u32[]{:S(2)}, u32[]{:S(2)}) collective-permute-start(f32[37,8,384]{2,1,0:T(8,128)S(1)} %get-tuple-element.31), channel_id=1, source_target_pairs={{0,2},{4,6},{8,10},{12,14},{16,18},{20,22},{24,26},{28,30},{32,34}... | collective-permute-start | bytes 1363976 | tf_op jit(solution)/shard_map/ppermute | solution.py:454
  5.5 9.1 %collective-permute-start.1 = (f32[37,8,384]{2,1,0:T(8,128)S(1)}, f32[37,8,384]{2,1,0:T(8,128)S(1)}, u32[]{:S(2)}, u32[]{:S(2)}) collective-permute-start(f32[37,8,384]{2,1,0:T(8,128)S(1)} %get-tuple-element.32), channel_id=1, source_target_pairs={{2,4},{6,8},{10,12},{14,16},{18,20},{22,24},{26,28},{30,32},{34,36... | collective-permute-start | bytes 1363976 | tf_op jit(solution)/shard_map/ppermute | solution.py:453
  6.2 10.9 %collective-permute-start.3 = (f32[37,8,384]{2,1,0:T(8,128)S(1)}, f32[37,8,384]{2,1,0:T(8,128)S(1)}, u32[]{:S(2)}, u32[]{:S(2)}) collective-permute-start(f32[37,8,384]{2,1,0:T(8,128)S(1)} %get-tuple-element.34), channel_id=1, source_target_pairs={{0,1},{1,0},{2,3},{3,2},{4,5},{5,4},{6,7},{7,6},{8,9},{9,8},{10,11... | collective-permute-start | bytes 1363976 | tf_op jit(solution)/shard_map/ppermute | solution.py:458
  14.7 7.4 %collective-permute-start.2 = (f32[20,8,384]{2,1,0:T(8,128)S(1)}, f32[20,8,384]{2,1,0:T(8,128)S(1)}, u32[]{:S(2)}, u32[]{:S(2)}) collective-permute-start(f32[20,8,384]{2,1,0:T(8,128)S(1)} %pad_maximum_fusion), channel_id=1, source_target_pairs={{0,1},{1,0},{2,3},{3,2},{4,5},{5,4},{6,7},{7,6},{8,9},{9,8},{10,11... | collective-permute-start | bytes 737288 | tf_op jit(solution)/shard_map/ppermute | solution.py:458
  25.7 20.9 %collective-permute-start.12 = (f32[12,48,384]{2,1,0:T(8,128)S(1)}, f32[12,48,384]{2,1,0:T(8,128)S(1)}, u32[]{:S(2)}, u32[]{:S(2)}) collective-permute-start(f32[12,48,384]{2,1,0:T(8,128)S(1)} %get-tuple-element.45.coef), channel_id=1, source_target_pairs={{0,1},{1,0},{2,3},{3,2},{4,5},{5,4},{6,7},{7,6},{8,9},{9,8},{10,11... | collective-permute-start | bytes 2654216 | tf_op jit(solution)/shard_map/ppermute | solution.py:458
  25.8 10.6 %collective-permute-start.4 = (f32[144,384]{1,0:T(8,128)S(1)}, f32[144,384]{1,0:T(8,128)S(1)}, u32[]{:S(2)}, u32[]{:S(2)}) collective-permute-start(f32[144,384]{1,0:T(8,128)S(1)} %get-tuple-element.41), channel_id=1, source_target_pairs={{0,2},{4,6},{8,10},{12,14},{16,18},{20,22},{24,26},{28,30},{32,34}... | collective-permute-start | bytes 663560 | tf_op jit(solution)/shard_map/ppermute | solution.py:454
  31.0 6.4 %collective-permute-start.5 = (f32[144,384]{1,0:T(8,128)S(1)}, f32[144,384]{1,0:T(8,128)S(1)}, u32[]{:S(2)}, u32[]{:S(2)}) collective-permute-start(f32[144,384]{1,0:T(8,128)S(1)} %get-tuple-element.42), channel_id=1, source_target_pairs={{2,4},{6,8},{10,12},{14,16},{18,20},{22,24},{26,28},{30,32},{34,36... | collective-permute-start | bytes 663560 | tf_op jit(solution)/shard_map/ppermute | solution.py:453
  36.4 12.2 %collective-permute-start.6 = (f32[144,384]{1,0:T(8,128)S(1)}, f32[144,384]{1,0:T(8,128)S(1)}, u32[]{:S(2)}, u32[]{:S(2)}) collective-permute-start(f32[144,384]{1,0:T(8,128)S(1)} %collective-permute-done.4.near), channel_id=1, source_target_pairs={{0,1},{1,0},{2,3},{3,2},{4,5},{5,4},{6,7},{7,6},{8,9},{9,8},{10,11... | collective-permute-start | bytes 663560 | tf_op jit(solution)/shard_map/ppermute | solution.py:458
  37.4 11.2 %collective-permute-start.7 = (f32[144,384]{1,0:T(8,128)S(1)}, f32[144,384]{1,0:T(8,128)S(1)}, u32[]{:S(2)}, u32[]{:S(2)}) collective-permute-start(f32[144,384]{1,0:T(8,128)S(1)} %collective-permute-done.5.far), channel_id=1, source_target_pairs={{0,1},{1,0},{2,3},{3,2},{4,5},{5,4},{6,7},{7,6},{8,9},{9,8},{10,11... | collective-permute-start | bytes 663560 | tf_op jit(solution)/shard_map/ppermute | solution.py:458
  37.4 8.6 %collective-permute-start.8 = (f32[64,384]{1,0:T(8,128)S(1)}, f32[64,384]{1,0:T(8,128)S(1)}, u32[]{:S(2)}, u32[]{:S(2)}) collective-permute-start(f32[64,384]{1,0:T(8,128)S(1)} %get-tuple-element.43), channel_id=1, source_target_pairs={{0,2},{4,6},{8,10},{12,14},{16,18},{20,22},{24,26},{28,30},{32,34}... | collective-permute-start | bytes 294920 | tf_op jit(solution)/shard_map/ppermute | solution.py:454
  42.9 3.8 %collective-permute-start.9 = (f32[64,384]{1,0:T(8,128)S(1)}, f32[64,384]{1,0:T(8,128)S(1)}, u32[]{:S(2)}, u32[]{:S(2)}) collective-permute-start(f32[64,384]{1,0:T(8,128)S(1)} %get-tuple-element.44), channel_id=1, source_target_pairs={{2,4},{6,8},{10,12},{14,16},{18,20},{22,24},{26,28},{30,32},{34,36... | collective-permute-start | bytes 294920 | tf_op jit(solution)/shard_map/ppermute | solution.py:453
  46.0 2.5 %collective-permute-start.10 = (f32[64,384]{1,0:T(8,128)S(1)}, f32[64,384]{1,0:T(8,128)S(1)}, u32[]{:S(2)}, u32[]{:S(2)}) collective-permute-start(f32[64,384]{1,0:T(8,128)S(1)} %collective-permute-done.8.e_near), channel_id=1, source_target_pairs={{0,1},{1,0},{2,3},{3,2},{4,5},{5,4},{6,7},{7,6},{8,9},{9,8},{10,11... | collective-permute-start | bytes 294920 | tf_op jit(solution)/shard_map/ppermute | solution.py:458
  46.6 1.9 %collective-permute-start.11 = (f32[64,384]{1,0:T(8,128)S(1)}, f32[64,384]{1,0:T(8,128)S(1)}, u32[]{:S(2)}, u32[]{:S(2)}) collective-permute-start(f32[64,384]{1,0:T(8,128)S(1)} %collective-permute-done.9.e_far), channel_id=1, source_target_pairs={{0,1},{1,0},{2,3},{3,2},{4,5},{5,4},{6,7},{7,6},{8,9},{9,8},{10,11... | collective-permute-start | bytes 294920 | tf_op jit(solution)/shard_map/ppermute | solution.py:458
